TPU v7x, 256 devices: a whole 4x4x8 slice. The times are simulated.
256 devices in a mesh: row: 8 (over y, z_lo), col: 8 (over z_hi, core), layer: 4 (over x).
Axes of the slice: x: 4, y: 4, z: 8 (z_hi: 4, z_lo: 2; z = z_hi * 2 + z_lo), core: 2. Of those that a mesh axis runs over, the one named last changes fastest.
Arguments:
- density_tiles: bfloat16 [192, 8, 2, 128, 128], P(('row', 'col')), may hold values from -1.5 to 1.5
- tile_columns: int32 [192, 8, 2], P(('row', 'col')), may hold values from -1 to 191, as said below
Outputs:
- square_tiles: bfloat16 [192, 8, 2, 128, 128], P(('row', 'col'), None, None, 'layer')
Inputs may be any that keep to these rules, and one draw needn't show every extreme that they name: `tile_columns`: entry [i, g, s] is a tile column in group g (columns g * 24 to (g + 1) * 24 - 1) or -1; within one block row and group the listed columns are distinct and empty slots come after the listed ones; block row i lists its own column i in the first slot of its group, whose 2 slots are all listed; other groups hold 0 to 2 listed tiles.
All inputs are finite; a program needn't handle non-finite values.
Results may differ from a plain program's by a relative error of at most 0.0048.
Values may be sent and summed in bfloat16 or wider, within the bound.
No kernel may reach another device: no remote copies, remote signals or barrier semaphores. Data moves between devices by JAX's collectives and lax.ppermute only.
A program may use at most 64 MiB of HBM per device.

v0:
```python
import functools

import jax
import jax.numpy as jnp
from jax import lax
from jax.experimental import pallas as pl
from jax.experimental.pallas import tpu as pltpu
from jax.sharding import Mesh
from jax.sharding import PartitionSpec as P


ROWS_COLS = ("y", "z_lo", "z_hi", "core")
ZC = ("z_lo", "z_hi", "core")
TAIL = 16
NO_TARGET = -3


def z_place(z, n_hi, n_lo):
    z = z % (n_hi * n_lo)
    return (z % n_lo) * n_hi + z // n_lo


def z_steps(step, flip, n_hi, n_lo):
    n = n_hi * n_lo
    return [
        (z_place(z, n_hi, n_lo) * 2 + c, z_place(z + step, n_hi, n_lo) * 2 + (c ^ flip))
        for z in range(n)
        for c in range(2)
    ]


def picked(tiles, columns, wanted):
    out = []
    for number in wanted:
        total = None
        for tile, column in zip(tiles, columns):
            part = tile * jnp.where(column == number, 1.0, 0.0).astype(tile.dtype)
            total = part if total is None else total + part
        out.append(total)
    return jnp.concatenate(out, axis=1)


class Rows:
    def __init__(self, sizes, columns, own):
        self.rows, self.slots, self.n_y, self.n_lo, self.n_hi, self.tb = sizes
        self.columns = columns
        self.x, self.y, self.z, self.core = (own[n] for n in range(4))

    def all(self):
        return [(n, row) for n in range(2 * self.n_y) for row in range(self.rows)]

    def place(self, n):
        flip, step = divmod(n, self.n_y)
        return lax.rem(self.y + step, self.n_y) * 2 + (self.core ^ flip)

    def wanted(self, n, row):
        at = (2 * self.x + self.core) * self.slots
        return [self.columns[n * self.rows + row, at + t] for t in range(self.slots)]

    def inner(self, n, row, group, slot):
        n_z = self.n_lo * self.n_hi
        first = self.n_lo * self.y + group
        column = self.columns[n * self.rows + row, first * self.slots + slot]
        listed = column >= 0
        local = jnp.where(listed, column - first * (self.rows * 2 * self.n_hi), 0)
        owner = lax.div(local, self.rows)
        inner_z = lax.div(owner, 2) * self.n_lo + group
        behind = lax.rem(inner_z - self.z - n_z // 2 - 1 + 2 * n_z, n_z)
        source = (lax.rem(owner, 2) ^ self.core) * n_z + behind
        return listed, source, (local - owner * self.rows) * self.slots

    def product(self, left, right, right_columns, n, row):
        tb, slots = self.tb, self.slots
        wanted = self.wanted(n, row)
        total = None
        for group in range(self.n_lo):
            lefts, rights = [], []
            for slot in range(slots):
                here, source, at = self.inner(n, row, group, slot)
                tiles = [
                    right[source, pl.ds(pl.multiple_of((at + s) * tb, tb), tb), :]
                    for s in range(slots)
                ]
                listed = [right_columns[pl.ds(source * TAIL + at + s, 1), :] for s in range(slots)]
                numbers = [
                    jnp.where(here & (wanted[t] >= 0), wanted[t], NO_TARGET).astype(jnp.float32)
                    for t in range(slots)
                ]
                rows = pl.ds(((row * self.n_lo + group) * slots + slot) * tb, tb)
                lefts.append(left[n][rows, :])
                rights.append(picked(tiles, listed, numbers))
            part = jnp.dot(
                jnp.concatenate(lefts, axis=1),
                jnp.concatenate(rights, axis=0),
                preferred_element_type=jnp.float32,
            )
            total = part if total is None else total + part
        return total


def first_payloads(places, columns, tiles, own, other, left_tail, held, arrived, listed):
    rows, groups, slots, tb, _ = tiles.shape
    copies = [
        pltpu.make_async_copy(tiles.at[row, places[g], slot], out.at[pl.ds((row * slots + slot) * tb, tb)], arrived)
        for g, out in enumerate((own, other))
        for row in range(rows)
        for slot in range(slots)
    ]
    fetch = pltpu.make_async_copy(columns, held, listed)
    fetch.start()
    for copy in copies:
        copy.start()
    fetch.wait()
    line = lax.broadcasted_iota(jnp.int32, (TAIL, tb), 0)
    lane = lax.broadcasted_iota(jnp.int32, (TAIL, tb), 1)
    numbers = [held[row].astype(jnp.float32) for row in range(rows)]
    for g, out in enumerate((own, other)):
        tail = jnp.zeros((TAIL, tb), jnp.float32)
        chosen = lax.broadcasted_iota(jnp.int32, (slots, groups), 1) == places[g]
        for row in range(rows):
            of_group = jnp.sum(jnp.where(chosen, numbers[row], 0.0), axis=1, keepdims=True)
            for slot in range(slots):
                number = jnp.broadcast_to(of_group[slot : slot + 1], (TAIL, tb))
                tail = jnp.where(line == row * slots + slot, number, tail)
        out[pl.ds(rows * slots * tb, TAIL), :] = tail.astype(out.dtype)
    tail = jnp.zeros((TAIL, tb), jnp.float32)
    for row in range(rows):
        for g in range(groups):
            for slot in range(slots):
                number = jnp.broadcast_to(numbers[row][slot : slot + 1, g : g + 1], (TAIL, tb))
                tail = jnp.where((line == row) & (lane == g * slots + slot), number, tail)
    left_tail[...] = tail.astype(left_tail.dtype)
    for copy in copies:
        copy.wait()


def listed_columns(rows, *refs):
    left, out = refs[:-1], refs[-1]
    for n, ref in enumerate(left):
        tail = ref[pl.ds(ref.shape[0] - TAIL, TAIL), :].astype(jnp.float32).astype(jnp.int32)
        out[pl.ds(n * rows, rows), :] = tail[:rows]


def products(sizes, columns, own, *refs):
    work = Rows(sizes, columns, own)
    n_left, tb = 2 * work.n_y, work.tb
    left, right_in = refs[:n_left], refs[n_left:-4]
    out, right, right_columns, arrived = refs[-4:]
    copies = [
        pltpu.make_async_copy(ref, right.at[n], arrived.at[n]) for n, ref in enumerate(right_in)
    ]
    for copy in copies:
        copy.start()
    for n, copy in enumerate(copies):
        copy.wait()
        tail = right[n, pl.ds(work.rows * work.slots * tb, TAIL), :]
        right_columns[pl.ds(n * TAIL, TAIL), :] = tail.astype(jnp.float32)
    quarters, quarter = out.shape[1], out.shape[4]
    for n, row in work.all():
        rounded = work.product(left, right, right_columns, n, row).astype(out.dtype)
        for t in range(work.slots):
            for q in range(quarters):
                out[work.place(n), q, row, t] = rounded[
                    q * quarter : (q + 1) * quarter, t * tb : (t + 1) * tb
                ]


def final_sum(n_y, arrived, out):
    rows, groups, slots = out.shape[:3]
    for g in range(groups):
        x, core = divmod(g, 2)
        for row in range(rows):
            for t in range(slots):
                total = arrived[0, core, x, row, t].astype(jnp.float32)
                for y in range(1, n_y):
                    total += arrived[y, core, x, row, t].astype(jnp.float32)
                out[row, g, t] = total.astype(out.dtype)


def on_device(density_tiles, tile_columns):
    rows, groups, slots, tb, _ = density_tiles.shape
    n_x, n_y, n_lo, n_hi = (lax.axis_size(a) for a in ("x", "y", "z_lo", "z_hi"))
    n_z = n_lo * n_hi
    x, y, core = lax.axis_index("x"), lax.axis_index("y"), lax.axis_index("core")
    z = lax.axis_index("z_hi") * n_lo + lax.axis_index("z_lo")
    cores = [(0, 1), (1, 0)]

    smem, vmem = pl.BlockSpec(memory_space=pltpu.SMEM), pl.BlockSpec(memory_space=pltpu.VMEM)
    hbm = pl.BlockSpec(memory_space=pltpu.HBM)
    limit = pltpu.CompilerParams(vmem_limit_bytes=4 * 2**20)
    payload = (rows * slots * tb + TAIL, tb)
    own, other, left_tail = pl.pallas_call(
        first_payloads,
        out_shape=[pltpu.VMEM(shape, jnp.bfloat16) for shape in (payload, payload, (TAIL, tb))],
        in_specs=[smem, hbm, hbm],
        out_specs=[vmem] * 3,
        scratch_shapes=[
            pltpu.VMEM((rows, slots, groups), jnp.int32),
            pltpu.SemaphoreType.DMA,
            pltpu.SemaphoreType.DMA,
        ],
        compiler_params=limit,
    )(
        jnp.stack([2 * x + core, 2 * x + 1 - core]).astype(jnp.int32),
        pltpu.with_memory_space_constraint(tile_columns.transpose(0, 2, 1), pltpu.HBM),
        pltpu.with_memory_space_constraint(density_tiles, pltpu.HBM),
    )
    right = {}
    right[0, 0] = own
    chains = {(0, 1): own, (0, -1): own, (1, 1): other, (1, -1): other}

    def ring(step, keys):
        for flip, way in keys:
            perm = z_steps(way, flip if step == 1 else 0, n_hi, n_lo)
            chains[flip, way] = lax.ppermute(chains[flip, way], ZC, perm)
            right[flip, (-way * step) % n_z] = chains[flip, way]

    half = n_z // 2
    ring(1, [(0, 1), (0, -1), (1, 1), (1, -1)])

    def left_payload(to_y):
        tiles = lax.dynamic_slice_in_dim(density_tiles, 2 * to_y, 2, 1)
        return jnp.concatenate([tiles.reshape(-1, tb), left_tail], axis=0)

    left = {(0, 0): lax.optimization_barrier(left_payload(y))}
    for step in (2, 1, 3):
        perm = [(s, (s + step) % n_y) for s in range(n_y)]
        sent = left_payload((y + step) % n_y)
        left[0, -step % n_y] = lax.ppermute(sent, "y", perm)
    right[1, 0] = lax.ppermute(other, "core", cores)
    left[1, 0] = lax.ppermute(left[0, 0], "core", cores)
    for step in range(1, n_y):
        left[1, step] = lax.ppermute(left[0, step], "core", cores)

    for step in range(2, half):
        ring(step, [(0, 1), (0, -1), (1, 1), (1, -1)])
    ring(half, [(0, 1), (1, -1)])

    left_keys = [(flip, step) for flip in range(2) for step in range(n_y)]
    sizes = (rows, slots, n_y, n_lo, n_hi, tb)
    quarter = tb // n_x

    rights = [right[flip, (n + half + 1) % n_z] for flip in range(2) for n in range(n_z)]
    lefts = [pltpu.with_memory_space_constraint(left[k], pltpu.VMEM) for k in left_keys]
    rights = [pltpu.with_memory_space_constraint(r, pltpu.HBM) for r in rights]
    columns = pl.pallas_call(
        functools.partial(listed_columns, rows),
        out_shape=jax.ShapeDtypeStruct((len(lefts) * rows, tb), jnp.int32),
        in_specs=[vmem] * len(lefts),
        out_specs=vmem,
        compiler_params=limit,
    )(*lefts)
    partial = pl.pallas_call(
        functools.partial(products, sizes),
        out_shape=pltpu.VMEM((2 * n_y, n_x, rows, slots, quarter, tb), jnp.bfloat16),
        in_specs=[smem] * 2 + [vmem] * len(lefts) + [hbm] * len(rights),
        out_specs=vmem,
        scratch_shapes=[
            pltpu.VMEM((len(rights), *payload), jnp.bfloat16),
            pltpu.VMEM((len(rights) * TAIL, tb), jnp.float32),
            pltpu.SemaphoreType.DMA((len(rights),)),
        ],
        compiler_params=pltpu.CompilerParams(vmem_limit_bytes=12 * 2**20),
    )(columns, jnp.stack([x, y, z, core]).astype(jnp.int32), *lefts, *rights)

    arrived = lax.all_to_all(
        partial.reshape(2 * n_y * n_x, rows, slots, quarter, tb),
        ("y", "core", "x"),
        split_axis=0,
        concat_axis=0,
        tiled=True,
    )
    arrived = arrived.reshape(n_y, 2, n_x, rows, slots, quarter, tb)
    return pl.pallas_call(
        functools.partial(final_sum, n_y),
        out_shape=jax.ShapeDtypeStruct((rows, groups, slots, quarter, tb), jnp.bfloat16),
        in_specs=[vmem],
        out_specs=vmem,
        compiler_params=limit,
    )(pltpu.with_memory_space_constraint(arrived, pltpu.VMEM))


def solution(mesh):
    fine = Mesh(mesh.devices.reshape(4, 2, 4, 2, 4), ("y", "z_lo", "z_hi", "core", "x"))

    return jax.shard_map(
        on_device,
        mesh=fine,
        in_specs=(P(ROWS_COLS, None, None, None, None), P(ROWS_COLS, None, None)),
        out_specs=P(ROWS_COLS, None, None, "x", None),
        check_vma=False,
    )
```

profile of v0, /device:TPU:1, one launch (start us, length us, event | category | flops | bytes accessed | tf_op | source)
XLA Modules:
  0.0 98.3 jit_solution(16882820952072697592)
XLA Ops:
  0.1 1.6 %shard_map.28 = (bf16[784,128]{1,0:T(8,128)(2,1)S(1)}, bf16[784,128]{1,0:T(8,128)(2,1)S(1)}, bf16[16,128]{1,0:T(8,128)(2,1)S(1)}) custom-call(s32[2]{0:T(128)S(1)} %pad_add_fusion.places, s32[3,2,8]{2,1,0:T(2,128)} %bitcast.19, bf16[3,8,2,128,128]{4,3,2,1,0:T(8,128)(2,1)} %tiles.1), custom_call_target="tpu_custom_call" | custom-call | tf_op jit(solution)/shard_map/pallas_call | solution.py:192
  1.7 6.5 %collective-permute-start.10 = (bf16[784,128]{1,0:T(8,128)(2,1)S(1)}, bf16[784,128]{1,0:T(8,128)(2,1)S(1)}, u32[]{:S(2)}, u32[]{:S(2)}) collective-permute-start(bf16[784,128]{1,0:T(8,128)(2,1)S(1)} %get-tuple-element.9.refs_11_), channel_id=1, source_target_pairs={{0,56},{4,60},{32,0},{36,4},{8,32},{12,36},{40,8},{44,12},{16,40},... | collective-permute-start | bytes 602120 | tf_op jit(solution)/shard_map/ppermute | solution.py:215
  8.2 3.8 %collective-permute-start.18 = (bf16[784,128]{1,0:T(8,128)(2,1)S(1)}, bf16[784,128]{1,0:T(8,128)(2,1)}, u32[]{:S(2)}, u32[]{:S(2)}) collective-permute-start(bf16[784,128]{1,0:T(8,128)(2,1)S(1)} %get-tuple-element.10), channel_id=1, source_target_pairs={{0,60},{4,56},{32,4},{36,0},{8,36},{12,32},{40,12},{44,8},{16,44},... | collective-permute-start | bytes 602120 | tf_op jit(solution)/shard_map/ppermute | solution.py:215
  12.3 1.4 %collective-permute-start.2 = (bf16[1552,128]{1,0:T(8,128)(2,1)S(1)}, bf16[1552,128]{1,0:T(8,128)(2,1)S(1)}, u32[]{:S(2)}, u32[]{:S(2)}) collective-permute-start(bf16[1552,128]{1,0:T(8,128)(2,1)S(1)} %get-tuple-element.15), channel_id=1, source_target_pairs={{0,64},{64,128},{128,192},{192,0},{1,65},{65,129},{129,193},{193,1... | collective-permute-start | bytes 1191944 | tf_op jit(solution)/shard_map/ppermute | solution.py:229
  13.7 1.5 %collective-permute-start = (bf16[1552,128]{1,0:T(8,128)(2,1)S(1)}, bf16[1552,128]{1,0:T(8,128)(2,1)S(1)}, u32[]{:S(2)}, u32[]{:S(2)}) collective-permute-start(bf16[1552,128]{1,0:T(8,128)(2,1)S(1)} %get-tuple-element.16), channel_id=1, source_target_pairs={{0,192},{64,0},{128,64},{192,128},{1,193},{65,1},{129,65},{193,129... | collective-permute-start | bytes 1191944 | tf_op jit(solution)/shard_map/ppermute | solution.py:229
  15.2 1.6 %collective-permute-start.1 = (bf16[1552,128]{1,0:T(8,128)(2,1)S(1)}, bf16[1552,128]{1,0:T(8,128)(2,1)S(1)}, u32[]{:S(2)}, u32[]{:S(2)}) collective-permute-start(bf16[1552,128]{1,0:T(8,128)(2,1)S(1)} %get-tuple-element.17), channel_id=1, source_target_pairs={{0,128},{64,192},{128,0},{192,64},{1,129},{65,193},{129,1},{193,65... | collective-permute-start | bytes 1191944 | tf_op jit(solution)/shard_map/ppermute | solution.py:229
  16.9 0.8 collective-permute-start.3
  17.7 7.3 %collective-permute-done.14.refs_18_ = bf16[784,128]{1,0:T(8,128)(2,1)S(1)} collective-permute-done((bf16[784,128]{1,0:T(8,128)(2,1)S(1)}, bf16[784,128]{1,0:T(8,128)(2,1)S(1)}, u32[]{:S(2)}, u32[]{:S(2)}) %collective-permute-start.14) | collective-permute-done | bytes 200736 | tf_op jit(solution)/shard_map/ppermute | solution.py:215
  25.0 0.5 collective-permute-start.11
  25.4 1.0 %collective-permute-start.8 = (bf16[784,128]{1,0:T(8,128)(2,1)S(1)}, bf16[784,128]{1,0:T(8,128)(2,1)S(1)}, u32[]{:S(2)}, u32[]{:S(2)}) collective-permute-start(bf16[784,128]{1,0:T(8,128)(2,1)S(1)} %collective-permute-done.7.refs_10_), channel_id=1, source_target_pairs={{0,32},{4,36},{32,8},{36,12},{8,40},{12,44},{40,16},{44,20},{16,48... | collective-permute-start | bytes 602120 | tf_op jit(solution)/shard_map/ppermute | solution.py:215
  26.4 1.7 %collective-permute-start.19 = (bf16[784,128]{1,0:T(8,128)(2,1)}, bf16[784,128]{1,0:T(8,128)(2,1)S(1)}, u32[]{:S(2)}, u32[]{:S(2)}) collective-permute-start(bf16[784,128]{1,0:T(8,128)(2,1)} %collective-permute-done.18.refs_20_), channel_id=1, source_target_pairs={{0,56},{4,60},{32,0},{36,4},{8,32},{12,36},{40,8},{44,12},{16,40},... | collective-permute-start | bytes 602120 | tf_op jit(solution)/shard_map/ppermute | solution.py:215
  28.1 5.9 %collective-permute-done.1.refs_2_ = bf16[1552,128]{1,0:T(8,128)(2,1)S(1)} collective-permute-done((bf16[1552,128]{1,0:T(8,128)(2,1)S(1)}, bf16[1552,128]{1,0:T(8,128)(2,1)S(1)}, u32[]{:S(2)}, u32[]{:S(2)}) %collective-permute-start.1) | collective-permute-done | bytes 397344 | tf_op jit(solution)/shard_map/ppermute | solution.py:229
  34.6 0.5 collective-permute-start.5
  35.1 6.4 %collective-permute-done.15.refs_17_ = bf16[784,128]{1,0:T(8,128)(2,1)} collective-permute-done((bf16[784,128]{1,0:T(8,128)(2,1)S(1)}, bf16[784,128]{1,0:T(8,128)(2,1)}, u32[]{:S(2)}, u32[]{:S(2)}) %collective-permute-start.15) | collective-permute-done | bytes 200736 | tf_op jit(solution)/shard_map/ppermute | solution.py:215
  41.5 4.3 %collective-permute-done.9.refs_8_ = bf16[784,128]{1,0:T(8,128)(2,1)} collective-permute-done((bf16[784,128]{1,0:T(8,128)(2,1)S(1)}, bf16[784,128]{1,0:T(8,128)(2,1)}, u32[]{:S(2)}, u32[]{:S(2)}) %collective-permute-start.9) | collective-permute-done | bytes 200736 | tf_op jit(solution)/shard_map/ppermute | solution.py:215
  45.8 1.3 %collective-permute-start.17 = (bf16[784,128]{1,0:T(8,128)(2,1)}, bf16[784,128]{1,0:T(8,128)(2,1)}, u32[]{:S(2)}, u32[]{:S(2)}) collective-permute-start(bf16[784,128]{1,0:T(8,128)(2,1)} %copy-done.1), channel_id=1, source_target_pairs={{0,4},{4,0},{1,5},{5,1},{2,6},{6,2},{3,7},{7,3},{8,12},{12,8},{9,1... | collective-permute-start | bytes 602120 | tf_op jit(solution)/shard_map/ppermute | solution.py:230
  47.4 1.1 %collective-permute-start.16 = (bf16[784,128]{1,0:T(8,128)(2,1)}, bf16[784,128]{1,0:T(8,128)(2,1)}, u32[]{:S(2)}, u32[]{:S(2)}) collective-permute-start(bf16[784,128]{1,0:T(8,128)(2,1)} %collective-permute-done.15.refs_17_), channel_id=1, source_target_pairs={{0,32},{4,36},{32,8},{36,12},{8,40},{12,44},{40,16},{44,20},{16,48... | collective-permute-start | bytes 602120 | tf_op jit(solution)/shard_map/ppermute | solution.py:215
  48.6 2.7 %collective-permute-start.21 = (bf16[784,128]{1,0:T(8,128)(2,1)}, bf16[784,128]{1,0:T(8,128)(2,1)}, u32[]{:S(2)}, u32[]{:S(2)}) collective-permute-start(bf16[784,128]{1,0:T(8,128)(2,1)} %collective-permute-done.20.refs_22_), channel_id=1, source_target_pairs={{0,56},{4,60},{32,0},{36,4},{8,32},{12,36},{40,8},{44,12},{16,40},... | collective-permute-start | bytes 602120 | tf_op jit(solution)/shard_map/ppermute | solution.py:215
  51.4 0.5 collective-permute-done.12.refs_14_
  51.9 1.5 %collective-permute-done.16.refs_16_ = bf16[784,128]{1,0:T(8,128)(2,1)} collective-permute-done((bf16[784,128]{1,0:T(8,128)(2,1)}, bf16[784,128]{1,0:T(8,128)(2,1)}, u32[]{:S(2)}, u32[]{:S(2)}) %collective-permute-start.16) | collective-permute-done | bytes 200736 | tf_op jit(solution)/shard_map/ppermute | solution.py:215
  53.5 3.0 %collective-permute-done.13.refs_15_ = bf16[784,128]{1,0:T(8,128)(2,1)} collective-permute-done((bf16[784,128]{1,0:T(8,128)(2,1)}, bf16[784,128]{1,0:T(8,128)(2,1)}, u32[]{:S(2)}, u32[]{:S(2)}) %collective-permute-start.13) | collective-permute-done | bytes 200736 | tf_op jit(solution)/shard_map/ppermute | solution.py:215
  56.5 5.4 %shard_map.30 = bf16[8,4,3,2,32,128]{5,4,3,2,1,0:T(8,128)(2,1)S(1)} custom-call(s32[24,128]{1,0:T(8,128)S(1)} %shard_map.29.columns, s32[4]{0:T(128)S(1)} %pad_add_fusion.1.own, bf16[1552,128]{1,0:T(8,128)(2,1)S(1)} %get-tuple-element.18.refs_0_, bf16[1552,128]{1,0:T(8,128)(2,1)S(1)} %collective-permute-done.refs_1_, ...), custom_call_target="tpu_custom_call" | custom-call | tf_op jit(solution)/shard_map/pallas_call | solution.py:253
  61.9 35.5 %all_to_all.5 = bf16[32,3,2,32,128]{4,3,2,1,0:T(8,128)(2,1)S(1)} all-to-all(bf16[32,3,2,32,128]{4,3,2,1,0:T(8,128)(2,1)S(1)} %bitcast.13), channel_id=1, replica_groups=mesh['y'=4,'z_lo'=2,'z_hi'=4,'core'=2,'x'=4] {'y','core','x'}, dimensions={0} | all-to-all | bytes 3145728 | tf_op jit(solution)/shard_map/all_to_all | solution.py:266
  97.4 0.9 shard_map.31
  (45 shorter events, 1.6 us)
Async XLA Ops:
  1.7 13.5 %collective-permute-start.10 = (bf16[784,128]{1,0:T(8,128)(2,1)S(1)}, bf16[784,128]{1,0:T(8,128)(2,1)S(1)}, u32[]{:S(2)}, u32[]{:S(2)}) collective-permute-start(bf16[784,128]{1,0:T(8,128)(2,1)S(1)} %get-tuple-element.9.refs_11_), channel_id=1, source_target_pairs={{0,56},{4,60},{32,0},{36,4},{8,32},{12,36},{40,8},{44,12},{16,40},... | collective-permute-start | bytes 602120 | tf_op jit(solution)/shard_map/ppermute | solution.py:215
  8.2 8.6 %collective-permute-start.7 = (bf16[784,128]{1,0:T(8,128)(2,1)S(1)}, bf16[784,128]{1,0:T(8,128)(2,1)S(1)}, u32[]{:S(2)}, u32[]{:S(2)}) collective-permute-start(bf16[784,128]{1,0:T(8,128)(2,1)S(1)} %get-tuple-element.9.refs_11_), channel_id=1, source_target_pairs={{0,32},{4,36},{32,8},{36,12},{8,40},{12,44},{40,16},{44,20},{16,48... | collective-permute-start | bytes 602120 | tf_op jit(solution)/shard_map/ppermute | solution.py:215
  8.2 8.7 %collective-permute-start.18 = (bf16[784,128]{1,0:T(8,128)(2,1)S(1)}, bf16[784,128]{1,0:T(8,128)(2,1)}, u32[]{:S(2)}, u32[]{:S(2)}) collective-permute-start(bf16[784,128]{1,0:T(8,128)(2,1)S(1)} %get-tuple-element.10), channel_id=1, source_target_pairs={{0,60},{4,56},{32,4},{36,0},{8,36},{12,32},{40,12},{44,8},{16,44},... | collective-permute-start | bytes 602120 | tf_op jit(solution)/shard_map/ppermute | solution.py:215
  12.3 13.1 %collective-permute-start.2 = (bf16[1552,128]{1,0:T(8,128)(2,1)S(1)}, bf16[1552,128]{1,0:T(8,128)(2,1)S(1)}, u32[]{:S(2)}, u32[]{:S(2)}) collective-permute-start(bf16[1552,128]{1,0:T(8,128)(2,1)S(1)} %get-tuple-element.15), channel_id=1, source_target_pairs={{0,64},{64,128},{128,192},{192,0},{1,65},{65,129},{129,193},{193,1... | collective-permute-start | bytes 1191944 | tf_op jit(solution)/shard_map/ppermute | solution.py:229
  13.7 12.8 %collective-permute-start = (bf16[1552,128]{1,0:T(8,128)(2,1)S(1)}, bf16[1552,128]{1,0:T(8,128)(2,1)S(1)}, u32[]{:S(2)}, u32[]{:S(2)}) collective-permute-start(bf16[1552,128]{1,0:T(8,128)(2,1)S(1)} %get-tuple-element.16), channel_id=1, source_target_pairs={{0,192},{64,0},{128,64},{192,128},{1,193},{65,1},{129,65},{193,129... | collective-permute-start | bytes 1191944 | tf_op jit(solution)/shard_map/ppermute | solution.py:229
  15.2 19.2 %copy-start.3 = (bf16[784,128]{1,0:T(8,128)(2,1)}, bf16[784,128]{1,0:T(8,128)(2,1)S(1)}, u32[]{:S(2)}) copy-start(bf16[784,128]{1,0:T(8,128)(2,1)S(1)} %collective-permute-done.10.refs_12_) | copy-start | bytes 602116
  15.2 18.8 %collective-permute-start.1 = (bf16[1552,128]{1,0:T(8,128)(2,1)S(1)}, bf16[1552,128]{1,0:T(8,128)(2,1)S(1)}, u32[]{:S(2)}, u32[]{:S(2)}) collective-permute-start(bf16[1552,128]{1,0:T(8,128)(2,1)S(1)} %get-tuple-element.17), channel_id=1, source_target_pairs={{0,128},{64,192},{128,0},{192,64},{1,129},{65,193},{129,1},{193,65... | collective-permute-start | bytes 1191944 | tf_op jit(solution)/shard_map/ppermute | solution.py:229
  16.8 8.2 %collective-permute-start.14 = (bf16[784,128]{1,0:T(8,128)(2,1)S(1)}, bf16[784,128]{1,0:T(8,128)(2,1)S(1)}, u32[]{:S(2)}, u32[]{:S(2)}) collective-permute-start(bf16[784,128]{1,0:T(8,128)(2,1)S(1)} %get-tuple-element.10), channel_id=1, source_target_pairs={{0,36},{4,32},{32,12},{36,8},{8,44},{12,40},{40,20},{44,16},{16,52... | collective-permute-start | bytes 602120 | tf_op jit(solution)/shard_map/ppermute | solution.py:215
  16.9 17.2 %collective-permute-start.3 = (bf16[1552,128]{1,0:T(8,128)(2,1)S(1)}, bf16[1552,128]{1,0:T(8,128)(2,1)S(1)}, u32[]{:S(2)}, u32[]{:S(2)}) collective-permute-start(bf16[1552,128]{1,0:T(8,128)(2,1)S(1)} %get-tuple-element.18.refs_0_), channel_id=1, source_target_pairs={{0,4},{4,0},{1,5},{5,1},{2,6},{6,2},{3,7},{7,3},{8,12},{12,8},{9,1... | collective-permute-start | bytes 1191944 | tf_op jit(solution)/shard_map/ppermute | solution.py:231
  25.0 26.4 %copy-start.5 = (bf16[784,128]{1,0:T(8,128)(2,1)}, bf16[784,128]{1,0:T(8,128)(2,1)S(1)}, u32[]{:S(2)}) copy-start(bf16[784,128]{1,0:T(8,128)(2,1)S(1)} %collective-permute-done.14.refs_18_) | copy-start | bytes 602116
  25.0 9.5 %collective-permute-start.11 = (bf16[784,128]{1,0:T(8,128)(2,1)S(1)}, bf16[784,128]{1,0:T(8,128)(2,1)}, u32[]{:S(2)}, u32[]{:S(2)}) collective-permute-start(bf16[784,128]{1,0:T(8,128)(2,1)S(1)} %collective-permute-done.10.refs_12_), channel_id=1, source_target_pairs={{0,56},{4,60},{32,0},{36,4},{8,32},{12,36},{40,8},{44,12},{16,40},... | collective-permute-start | bytes 602120 | tf_op jit(solution)/shard_map/ppermute | solution.py:215
  25.4 9.1 %collective-permute-start.8 = (bf16[784,128]{1,0:T(8,128)(2,1)S(1)}, bf16[784,128]{1,0:T(8,128)(2,1)S(1)}, u32[]{:S(2)}, u32[]{:S(2)}) collective-permute-start(bf16[784,128]{1,0:T(8,128)(2,1)S(1)} %collective-permute-done.7.refs_10_), channel_id=1, source_target_pairs={{0,32},{4,36},{32,8},{36,12},{8,40},{12,44},{40,16},{44,20},{16,48... | collective-permute-start | bytes 602120 | tf_op jit(solution)/shard_map/ppermute | solution.py:215
  26.4 8.6 %collective-permute-start.19 = (bf16[784,128]{1,0:T(8,128)(2,1)}, bf16[784,128]{1,0:T(8,128)(2,1)S(1)}, u32[]{:S(2)}, u32[]{:S(2)}) collective-permute-start(bf16[784,128]{1,0:T(8,128)(2,1)} %collective-permute-done.18.refs_20_), channel_id=1, source_target_pairs={{0,56},{4,60},{32,0},{36,4},{8,32},{12,36},{40,8},{44,12},{16,40},... | collective-permute-start | bytes 602120 | tf_op jit(solution)/shard_map/ppermute | solution.py:215
  34.0 7.5 %collective-permute-start.15 = (bf16[784,128]{1,0:T(8,128)(2,1)S(1)}, bf16[784,128]{1,0:T(8,128)(2,1)}, u32[]{:S(2)}, u32[]{:S(2)}) collective-permute-start(bf16[784,128]{1,0:T(8,128)(2,1)S(1)} %collective-permute-done.14.refs_18_), channel_id=1, source_target_pairs={{0,32},{4,36},{32,8},{36,12},{8,40},{12,44},{40,16},{44,20},{16,48... | collective-permute-start | bytes 602120 | tf_op jit(solution)/shard_map/ppermute | solution.py:215
  34.0 13.4 %collective-permute-start.6 = (bf16[1552,128]{1,0:T(8,128)(2,1)S(1)}, bf16[1552,128]{1,0:T(8,128)(2,1)S(1)}, u32[]{:S(2)}, u32[]{:S(2)}) collective-permute-start(bf16[1552,128]{1,0:T(8,128)(2,1)S(1)} %collective-permute-done.2.refs_3_), channel_id=1, source_target_pairs={{0,4},{4,0},{1,5},{5,1},{2,6},{6,2},{3,7},{7,3},{8,12},{12,8},{9,1... | collective-permute-start | bytes 1191944 | tf_op jit(solution)/shard_map/ppermute | solution.py:233
  34.4 14.1 %collective-permute-start.4 = (bf16[1552,128]{1,0:T(8,128)(2,1)S(1)}, bf16[1552,128]{1,0:T(8,128)(2,1)S(1)}, u32[]{:S(2)}, u32[]{:S(2)}) collective-permute-start(bf16[1552,128]{1,0:T(8,128)(2,1)S(1)} %collective-permute-done.refs_1_), channel_id=1, source_target_pairs={{0,4},{4,0},{1,5},{5,1},{2,6},{6,2},{3,7},{7,3},{8,12},{12,8},{9,1... | collective-permute-start | bytes 1191944 | tf_op jit(solution)/shard_map/ppermute | solution.py:233
  34.6 14.1 %collective-permute-start.5 = (bf16[1552,128]{1,0:T(8,128)(2,1)S(1)}, bf16[1552,128]{1,0:T(8,128)(2,1)S(1)}, u32[]{:S(2)}, u32[]{:S(2)}) collective-permute-start(bf16[1552,128]{1,0:T(8,128)(2,1)S(1)} %collective-permute-done.1.refs_2_), channel_id=1, source_target_pairs={{0,4},{4,0},{1,5},{5,1},{2,6},{6,2},{3,7},{7,3},{8,12},{12,8},{9,1... | collective-permute-start | bytes 1191944 | tf_op jit(solution)/shard_map/ppermute | solution.py:233
  35.0 10.8 %collective-permute-start.9 = (bf16[784,128]{1,0:T(8,128)(2,1)S(1)}, bf16[784,128]{1,0:T(8,128)(2,1)}, u32[]{:S(2)}, u32[]{:S(2)}) collective-permute-start(bf16[784,128]{1,0:T(8,128)(2,1)S(1)} %collective-permute-done.8.refs_9_), channel_id=1, source_target_pairs={{0,32},{4,36},{32,8},{36,12},{8,40},{12,44},{40,16},{44,20},{16,48... | collective-permute-start | bytes 602120 | tf_op jit(solution)/shard_map/ppermute | solution.py:215
  41.5 5.6 %collective-permute-start.20 = (bf16[784,128]{1,0:T(8,128)(2,1)S(1)}, bf16[784,128]{1,0:T(8,128)(2,1)}, u32[]{:S(2)}, u32[]{:S(2)}) collective-permute-start(bf16[784,128]{1,0:T(8,128)(2,1)S(1)} %collective-permute-done.19.refs_21_), channel_id=1, source_target_pairs={{0,56},{4,60},{32,0},{36,4},{8,32},{12,36},{40,8},{44,12},{16,40},... | collective-permute-start | bytes 602120 | tf_op jit(solution)/shard_map/ppermute | solution.py:215
  45.8 5.6 %collective-permute-start.17 = (bf16[784,128]{1,0:T(8,128)(2,1)}, bf16[784,128]{1,0:T(8,128)(2,1)}, u32[]{:S(2)}, u32[]{:S(2)}) collective-permute-start(bf16[784,128]{1,0:T(8,128)(2,1)} %copy-done.1), channel_id=1, source_target_pairs={{0,4},{4,0},{1,5},{5,1},{2,6},{6,2},{3,7},{7,3},{8,12},{12,8},{9,1... | collective-permute-start | bytes 602120 | tf_op jit(solution)/shard_map/ppermute | solution.py:230
  47.1 4.9 %collective-permute-start.12 = (bf16[784,128]{1,0:T(8,128)(2,1)}, bf16[784,128]{1,0:T(8,128)(2,1)}, u32[]{:S(2)}, u32[]{:S(2)}) collective-permute-start(bf16[784,128]{1,0:T(8,128)(2,1)} %collective-permute-done.11.refs_13_), channel_id=1, source_target_pairs={{0,56},{4,60},{32,0},{36,4},{8,32},{12,36},{40,8},{44,12},{16,40},... | collective-permute-start | bytes 602120 | tf_op jit(solution)/shard_map/ppermute | solution.py:215
  47.4 6.1 %collective-permute-start.16 = (bf16[784,128]{1,0:T(8,128)(2,1)}, bf16[784,128]{1,0:T(8,128)(2,1)}, u32[]{:S(2)}, u32[]{:S(2)}) collective-permute-start(bf16[784,128]{1,0:T(8,128)(2,1)} %collective-permute-done.15.refs_17_), channel_id=1, source_target_pairs={{0,32},{4,36},{32,8},{36,12},{8,40},{12,44},{40,16},{44,20},{16,48... | collective-permute-start | bytes 602120 | tf_op jit(solution)/shard_map/ppermute | solution.py:215
  48.5 8.0 %collective-permute-start.13 = (bf16[784,128]{1,0:T(8,128)(2,1)}, bf16[784,128]{1,0:T(8,128)(2,1)}, u32[]{:S(2)}, u32[]{:S(2)}) collective-permute-start(bf16[784,128]{1,0:T(8,128)(2,1)} %collective-permute-done.9.refs_8_), channel_id=1, source_target_pairs={{0,32},{4,36},{32,8},{36,12},{8,40},{12,44},{40,16},{44,20},{16,48... | collective-permute-start | bytes 602120 | tf_op jit(solution)/shard_map/ppermute | solution.py:215
  48.6 7.9 %collective-permute-start.21 = (bf16[784,128]{1,0:T(8,128)(2,1)}, bf16[784,128]{1,0:T(8,128)(2,1)}, u32[]{:S(2)}, u32[]{:S(2)}) collective-permute-start(bf16[784,128]{1,0:T(8,128)(2,1)} %collective-permute-done.20.refs_22_), channel_id=1, source_target_pairs={{0,56},{4,60},{32,0},{36,4},{8,32},{12,36},{40,8},{44,12},{16,40},... | collective-permute-start | bytes 602120 | tf_op jit(solution)/shard_map/ppermute | solution.py:215
  (6 other events, 82.9 us)
where the time goes:
time: 98.5 us; the launch traced here: 98.3 us
  blocking collectives  35.5 us (36%)
  waiting for transfers between devices  29.1 us (30%)
  starting transfers between devices  25.2 us (26%)
  Pallas kernels  7.9 us (8%)
    all_to_all x1, blocking collectives, on_device(): lax.all_to_all(partial.reshape(2 * n_y * n_x, rows, slots, quarter, tb),...  35.5 us
    ppermute x14, waiting for transfers between devices, ring(): chains[flip, way] = lax.ppermute(chains[flip, way], ZC, perm)  23.2 us
    ppermute x14, starting transfers between devices, ring(): chains[flip, way] = lax.ppermute(chains[flip, way], ZC, perm)  17.7 us
    ppermute x3, waiting for transfers between devices, on_device(): left[0, -step % n_y] = lax.ppermute(sent, 'y', perm)  5.94 us
    pallas_call x1, Pallas kernels, on_device(): pl.pallas_call(functools.partial(products, sizes), out_shape=pltpu.VMEM((...  5.37 us
    ppermute x3, starting transfers between devices, on_device(): left[0, -step % n_y] = lax.ppermute(sent, 'y', perm)  4.46 us
  transfers between devices with their start and end apart: 22, of which 7 were waited for; matrix products, arithmetic and copies ran while one was open for 0% of the time, Pallas kernels for 0%

commit v1 on v0

--- a/solution.py
+++ b/solution.py
@@ -50,8 +50,8 @@
         return [(n, row) for n in range(2 * self.n_y) for row in range(self.rows)]
 
     def place(self, n):
-        flip, step = divmod(n, self.n_y)
-        return lax.rem(self.y + step, self.n_y) * 2 + (self.core ^ flip)
+        flip, y = divmod(n, self.n_y)
+        return y * 2 + (self.core ^ flip)
 
     def wanted(self, n, row):
         at = (2 * self.x + self.core) * self.slots
@@ -87,7 +87,8 @@
                     for t in range(slots)
                 ]
                 rows = pl.ds(((row * self.n_lo + group) * slots + slot) * tb, tb)
-                lefts.append(left[n][rows, :])
+                flip, y = divmod(n, self.n_y)
+                lefts.append(left[flip][y, rows, :])
                 rights.append(picked(tiles, listed, numbers))
             part = jnp.dot(
                 jnp.concatenate(lefts, axis=1),
@@ -136,15 +137,17 @@
 
 def listed_columns(rows, *refs):
     left, out = refs[:-1], refs[-1]
-    for n, ref in enumerate(left):
-        tail = ref[pl.ds(ref.shape[0] - TAIL, TAIL), :].astype(jnp.float32).astype(jnp.int32)
-        out[pl.ds(n * rows, rows), :] = tail[:rows]
+    n_y, lines = left[0].shape[:2]
+    for flip, ref in enumerate(left):
+        for y in range(n_y):
+            tail = ref[y, pl.ds(lines - TAIL, TAIL), :].astype(jnp.float32).astype(jnp.int32)
+            out[pl.ds((flip * n_y + y) * rows, rows), :] = tail[:rows]
 
 
 def products(sizes, columns, own, *refs):
     work = Rows(sizes, columns, own)
-    n_left, tb = 2 * work.n_y, work.tb
-    left, right_in = refs[:n_left], refs[n_left:-4]
+    tb = work.tb
+    left, right_in = refs[:2], refs[2:-4]
     out, right, right_columns, arrived = refs[-4:]
     copies = [
         pltpu.make_async_copy(ref, right.at[n], arrived.at[n]) for n, ref in enumerate(right_in)
@@ -218,34 +221,26 @@
     half = n_z // 2
     ring(1, [(0, 1), (0, -1), (1, 1), (1, -1)])
 
-    def left_payload(to_y):
-        tiles = lax.dynamic_slice_in_dim(density_tiles, 2 * to_y, 2, 1)
-        return jnp.concatenate([tiles.reshape(-1, tb), left_tail], axis=0)
-
-    left = {(0, 0): lax.optimization_barrier(left_payload(y))}
-    for step in (2, 1, 3):
-        perm = [(s, (s + step) % n_y) for s in range(n_y)]
-        sent = left_payload((y + step) % n_y)
-        left[0, -step % n_y] = lax.ppermute(sent, "y", perm)
+    by_y = density_tiles.reshape(rows, n_y, -1, tb).transpose(1, 0, 2, 3).reshape(n_y, -1, tb)
+    tails = jnp.broadcast_to(left_tail, (n_y, TAIL, tb))
+    packed = jnp.concatenate([by_y, tails], axis=1)
+    left = [lax.all_to_all(packed, "y", split_axis=0, concat_axis=0, tiled=True)]
     right[1, 0] = lax.ppermute(other, "core", cores)
-    left[1, 0] = lax.ppermute(left[0, 0], "core", cores)
-    for step in range(1, n_y):
-        left[1, step] = lax.ppermute(left[0, step], "core", cores)
+    left.append(lax.ppermute(left[0], "core", cores))
 
     for step in range(2, half):
         ring(step, [(0, 1), (0, -1), (1, 1), (1, -1)])
     ring(half, [(0, 1), (1, -1)])
 
-    left_keys = [(flip, step) for flip in range(2) for step in range(n_y)]
     sizes = (rows, slots, n_y, n_lo, n_hi, tb)
     quarter = tb // n_x
 
     rights = [right[flip, (n + half + 1) % n_z] for flip in range(2) for n in range(n_z)]
-    lefts = [pltpu.with_memory_space_constraint(left[k], pltpu.VMEM) for k in left_keys]
+    lefts = [pltpu.with_memory_space_constraint(a, pltpu.VMEM) for a in left]
     rights = [pltpu.with_memory_space_constraint(r, pltpu.HBM) for r in rights]
     columns = pl.pallas_call(
         functools.partial(listed_columns, rows),
-        out_shape=jax.ShapeDtypeStruct((len(lefts) * rows, tb), jnp.int32),
+        out_shape=jax.ShapeDtypeStruct((2 * n_y * rows, tb), jnp.int32),
         in_specs=[vmem] * len(lefts),
         out_specs=vmem,
         compiler_params=limit,

time: 98.5 us -> 106 us (1.076)
  blocking collectives: 35.5 us -> 55.1 us
  waiting for transfers between devices: 29.1 us -> 14.4 us
  local copies, waits for them, and re-layouts: 0.2 us -> 1.54 us
    all_to_all x0 -> x1, blocking collectives: none -> 24.7 us  [on_device(): lax.all_to_all(packed, 'y', split_axis=0, concat_axis=0, tiled=True)]
    ppermute x14, waiting for transfers between devices: 23.2 us -> 14.4 us  [ring(): chains[flip, way] = lax.ppermute(chains[flip, way], ZC, perm)]
    ppermute x7 -> x1, waiting for transfers between devices: 5.95 us -> 0.01 us  [on_device(): left.append(lax.ppermute(left[0], 'core', cores))]
    ppermute x14, starting transfers between devices: 17.7 us -> 23 us  [ring(): chains[flip, way] = lax.ppermute(chains[flip, way], ZC, perm)]
    all_to_all x1, blocking collectives: 35.5 us -> 30.4 us  [on_device(): lax.all_to_all(partial.reshape(2 * n_y * n_x, rows, slots, quarter, tb),...]
    ppermute x7 -> x1, starting transfers between devices: 6.24 us -> 1.97 us  [on_device(): left.append(lax.ppermute(left[0], 'core', cores))]
    reshape x0 -> x1, local copies, waits for them, and re-layouts: none -> 1.51 us  [on_device(): density_tiles.reshape(rows, n_y, -1, tb).transpose(1, 0, 2, 3)]
  transfers between devices with their start and end apart: 22 -> 16, of which waited for: 7 -> 5; matrix products, arithmetic and copies ran while one was open for 0% -> 0% of each run, Pallas kernels for 0% -> 0%
where the time goes in v1:
time: 106 us
  blocking collectives  55.1 us (52%)
  starting transfers between devices  26.1 us (25%)
  waiting for transfers between devices  14.4 us (14%)
  Pallas kernels  8.56 us (8%)
  local copies, waits for them, and re-layouts  1.54 us (1%)
    all_to_all x1, blocking collectives, on_device(): lax.all_to_all(partial.reshape(2 * n_y * n_x, rows, slots, quarter, tb),...  30.4 us
    all_to_all x1, blocking collectives, on_device(): lax.all_to_all(packed, 'y', split_axis=0, concat_axis=0, tiled=True)  24.7 us
    ppermute x14, starting transfers between devices, ring(): chains[flip, way] = lax.ppermute(chains[flip, way], ZC, perm)  23 us
    ppermute x14, waiting for transfers between devices, ring(): chains[flip, way] = lax.ppermute(chains[flip, way], ZC, perm)  14.4 us
    pallas_call x1, Pallas kernels, on_device(): pl.pallas_call(functools.partial(products, sizes), out_shape=pltpu.VMEM((...  5.36 us
    pallas_call x1, Pallas kernels, on_device(): pl.pallas_call(first_payloads, out_shape=[pltpu.VMEM(shape, jnp.bfloat16)...  2.26 us
  transfers between devices with their start and end apart: 16, of which 5 were waited for; matrix products, arithmetic and copies ran while one was open for 0% of the time, Pallas kernels for 0%

profile of v1, /device:TPU:1, one launch (start us, length us, event | category | flops | bytes accessed | tf_op | source)
XLA Modules:
  0.0 106.2 jit_solution(4045555948925848495)
XLA Ops:
  0.0 1.5 %copy.3 = bf16[3,4,512,128]{3,2,0,1:T(8,128)(2,1)S(1)} copy(bf16[3,4,512,128]{3,2,1,0:T(8,128)(2,1)} %bitcast.15) | data formatting | bytes 3145728 | tf_op jit(solution)/shard_map/reshape | solution.py:224
  1.5 0.1 pad_add_fusion.places
  1.6 2.3 %shard_map.28 = (bf16[784,128]{1,0:T(8,128)(2,1)S(1)}, bf16[784,128]{1,0:T(8,128)(2,1)}, bf16[16,128]{1,0:T(8,128)(2,1)S(1)}) custom-call(s32[2]{0:T(128)S(1)} %pad_add_fusion.places, s32[3,2,8]{2,1,0:T(2,128)} %bitcast.17, bf16[3,8,2,128,128]{4,3,2,1,0:T(8,128)(2,1)} %tiles.1), custom_call_target="tpu_custom_call" | custom-call | tf_op jit(solution)/shard_map/pallas_call | solution.py:195
  3.9 0.1 pad_maximum_fusion
  4.0 24.7 %all_to_all.10.refs_0_ = bf16[4,1552,128]{2,1,0:T(8,128)(2,1)S(1)} all-to-all(bf16[4,1552,128]{2,1,0:T(8,128)(2,1)S(1)} %pad_maximum_fusion), channel_id=1, replica_groups=mesh['y'=4,'z_lo'=2,'z_hi'=4,'core'=2,'x'=4] {'y'}, dimensions={0} | all-to-all | bytes 3178496 | tf_op jit(solution)/shard_map/all_to_all | solution.py:227
  28.7 2.0 %collective-permute-start = (bf16[4,1552,128]{2,1,0:T(8,128)(2,1)S(1)}, bf16[4,1552,128]{2,1,0:T(8,128)(2,1)S(1)}, u32[]{:S(2)}, u32[]{:S(2)}) collective-permute-start(bf16[4,1552,128]{2,1,0:T(8,128)(2,1)S(1)} %all_to_all.10.refs_0_), channel_id=1, source_target_pairs={{0,4},{4,0},{1,5},{5,1},{2,6},{6,2},{3,7},{7,3},{8,12},{12,8},{9,1... | collective-permute-start | bytes 4767752 | tf_op jit(solution)/shard_map/ppermute | solution.py:229
  30.6 1.6 %collective-permute-start.1 = (bf16[784,128]{1,0:T(8,128)(2,1)S(1)}, bf16[784,128]{1,0:T(8,128)(2,1)S(1)}, u32[]{:S(2)}, u32[]{:S(2)}) collective-permute-start(bf16[784,128]{1,0:T(8,128)(2,1)S(1)} %get-tuple-element.9.refs_5_), channel_id=1, source_target_pairs={{0,32},{4,36},{32,8},{36,12},{8,40},{12,44},{40,16},{44,20},{16,48... | collective-permute-start | bytes 602120 | tf_op jit(solution)/shard_map/ppermute | solution.py:218
  32.3 3.8 %collective-permute-start.12 = (bf16[784,128]{1,0:T(8,128)(2,1)}, bf16[784,128]{1,0:T(8,128)(2,1)S(1)}, u32[]{:S(2)}, u32[]{:S(2)}) collective-permute-start(bf16[784,128]{1,0:T(8,128)(2,1)} %get-tuple-element.10), channel_id=1, source_target_pairs={{0,60},{4,56},{32,4},{36,0},{8,36},{12,32},{40,12},{44,8},{16,44},... | collective-permute-start | bytes 602120 | tf_op jit(solution)/shard_map/ppermute | solution.py:218
  36.1 1.7 %collective-permute-start.4 = (bf16[784,128]{1,0:T(8,128)(2,1)S(1)}, bf16[784,128]{1,0:T(8,128)(2,1)S(1)}, u32[]{:S(2)}, u32[]{:S(2)}) collective-permute-start(bf16[784,128]{1,0:T(8,128)(2,1)S(1)} %get-tuple-element.9.refs_5_), channel_id=1, source_target_pairs={{0,56},{4,60},{32,0},{36,4},{8,32},{12,36},{40,8},{44,12},{16,40},... | collective-permute-start | bytes 602120 | tf_op jit(solution)/shard_map/ppermute | solution.py:218
  37.9 0.4 collective-permute-start.8
  38.3 3.3 %collective-permute-done.1.refs_4_ = bf16[784,128]{1,0:T(8,128)(2,1)S(1)} collective-permute-done((bf16[784,128]{1,0:T(8,128)(2,1)S(1)}, bf16[784,128]{1,0:T(8,128)(2,1)S(1)}, u32[]{:S(2)}, u32[]{:S(2)}) %collective-permute-start.1) | collective-permute-done | bytes 200736 | tf_op jit(solution)/shard_map/ppermute | solution.py:218
  41.6 3.3 %collective-permute-start.13 = (bf16[784,128]{1,0:T(8,128)(2,1)S(1)}, bf16[784,128]{1,0:T(8,128)(2,1)S(1)}, u32[]{:S(2)}, u32[]{:S(2)}) collective-permute-start(bf16[784,128]{1,0:T(8,128)(2,1)S(1)} %collective-permute-done.12.refs_14_), channel_id=1, source_target_pairs={{0,56},{4,60},{32,0},{36,4},{8,32},{12,36},{40,8},{44,12},{16,40},... | collective-permute-start | bytes 602120 | tf_op jit(solution)/shard_map/ppermute | solution.py:218
  44.9 3.2 %collective-permute-start.5 = (bf16[784,128]{1,0:T(8,128)(2,1)S(1)}, bf16[784,128]{1,0:T(8,128)(2,1)S(1)}, u32[]{:S(2)}, u32[]{:S(2)}) collective-permute-start(bf16[784,128]{1,0:T(8,128)(2,1)S(1)} %collective-permute-done.4.refs_6_), channel_id=1, source_target_pairs={{0,56},{4,60},{32,0},{36,4},{8,32},{12,36},{40,8},{44,12},{16,40},... | collective-permute-start | bytes 602120 | tf_op jit(solution)/shard_map/ppermute | solution.py:218
  48.2 2.6 %collective-permute-done.2.refs_3_ = bf16[784,128]{1,0:T(8,128)(2,1)S(1)} collective-permute-done((bf16[784,128]{1,0:T(8,128)(2,1)S(1)}, bf16[784,128]{1,0:T(8,128)(2,1)S(1)}, u32[]{:S(2)}, u32[]{:S(2)}) %collective-permute-start.2) | collective-permute-done | bytes 200736 | tf_op jit(solution)/shard_map/ppermute | solution.py:218
  50.8 2.7 %collective-permute-start.14 = (bf16[784,128]{1,0:T(8,128)(2,1)S(1)}, bf16[784,128]{1,0:T(8,128)(2,1)}, u32[]{:S(2)}, u32[]{:S(2)}) collective-permute-start(bf16[784,128]{1,0:T(8,128)(2,1)S(1)} %collective-permute-done.13.refs_15_), channel_id=1, source_target_pairs={{0,56},{4,60},{32,0},{36,4},{8,32},{12,36},{40,8},{44,12},{16,40},... | collective-permute-start | bytes 602120 | tf_op jit(solution)/shard_map/ppermute | solution.py:218
  53.5 1.1 %collective-permute-start.11 = (bf16[784,128]{1,0:T(8,128)(2,1)}, bf16[784,128]{1,0:T(8,128)(2,1)}, u32[]{:S(2)}, u32[]{:S(2)}) collective-permute-start(bf16[784,128]{1,0:T(8,128)(2,1)} %get-tuple-element.10), channel_id=1, source_target_pairs={{0,4},{4,0},{1,5},{5,1},{2,6},{6,2},{3,7},{7,3},{8,12},{12,8},{9,1... | collective-permute-start | bytes 602120 | tf_op jit(solution)/shard_map/ppermute | solution.py:228
  54.7 3.3 %collective-permute-start.6 = (bf16[784,128]{1,0:T(8,128)(2,1)S(1)}, bf16[784,128]{1,0:T(8,128)(2,1)}, u32[]{:S(2)}, u32[]{:S(2)}) collective-permute-start(bf16[784,128]{1,0:T(8,128)(2,1)S(1)} %collective-permute-done.5.refs_7_), channel_id=1, source_target_pairs={{0,56},{4,60},{32,0},{36,4},{8,32},{12,36},{40,8},{44,12},{16,40},... | collective-permute-start | bytes 602120 | tf_op jit(solution)/shard_map/ppermute | solution.py:218
  57.9 1.2 %collective-permute-done.3.refs_2_ = bf16[784,128]{1,0:T(8,128)(2,1)} collective-permute-done((bf16[784,128]{1,0:T(8,128)(2,1)S(1)}, bf16[784,128]{1,0:T(8,128)(2,1)}, u32[]{:S(2)}, u32[]{:S(2)}) %collective-permute-start.3) | collective-permute-done | bytes 200736 | tf_op jit(solution)/shard_map/ppermute | solution.py:218
  59.2 2.9 %collective-permute-start.15 = (bf16[784,128]{1,0:T(8,128)(2,1)}, bf16[784,128]{1,0:T(8,128)(2,1)}, u32[]{:S(2)}, u32[]{:S(2)}) collective-permute-start(bf16[784,128]{1,0:T(8,128)(2,1)} %collective-permute-done.14.refs_16_), channel_id=1, source_target_pairs={{0,56},{4,60},{32,0},{36,4},{8,32},{12,36},{40,8},{44,12},{16,40},... | collective-permute-start | bytes 602120 | tf_op jit(solution)/shard_map/ppermute | solution.py:218
  62.2 3.0 %collective-permute-done.10.refs_10_ = bf16[784,128]{1,0:T(8,128)(2,1)} collective-permute-done((bf16[784,128]{1,0:T(8,128)(2,1)}, bf16[784,128]{1,0:T(8,128)(2,1)}, u32[]{:S(2)}, u32[]{:S(2)}) %collective-permute-start.10) | collective-permute-done | bytes 200736 | tf_op jit(solution)/shard_map/ppermute | solution.py:218
  65.2 4.2 %collective-permute-done.7.refs_9_ = bf16[784,128]{1,0:T(8,128)(2,1)} collective-permute-done((bf16[784,128]{1,0:T(8,128)(2,1)}, bf16[784,128]{1,0:T(8,128)(2,1)}, u32[]{:S(2)}, u32[]{:S(2)}) %collective-permute-start.7) | collective-permute-done | bytes 200736 | tf_op jit(solution)/shard_map/ppermute | solution.py:218
  69.4 5.4 %shard_map.30 = bf16[8,4,3,2,32,128]{5,4,3,2,1,0:T(8,128)(2,1)S(1)} custom-call(s32[24,128]{1,0:T(8,128)S(1)} %shard_map.29.columns, s32[4]{0:T(128)S(1)} %pad_add_fusion.1.own, bf16[4,1552,128]{2,1,0:T(8,128)(2,1)S(1)} %all_to_all.10.refs_0_, bf16[4,1552,128]{2,1,0:T(8,128)(2,1)S(1)} %collective-permute-done.refs_1_, ...), custom_call_target="tpu_custom_call" | custom-call | tf_op jit(solution)/shard_map/pallas_call | solution.py:248
  74.8 30.4 %all_to_all.11 = bf16[32,3,2,32,128]{4,3,2,1,0:T(8,128)(2,1)S(1)} all-to-all(bf16[32,3,2,32,128]{4,3,2,1,0:T(8,128)(2,1)S(1)} %bitcast.13), channel_id=1, replica_groups=mesh['y'=4,'z_lo'=2,'z_hi'=4,'core'=2,'x'=4] {'y','core','x'}, dimensions={0} | all-to-all | bytes 3145728 | tf_op jit(solution)/shard_map/all_to_all | solution.py:261
  105.3 0.9 shard_map.31
  (35 shorter events, 0.2 us)
Async XLA Ops:
  3.9 32.3 %copy-start = (bf16[784,128]{1,0:T(8,128)(2,1)}, bf16[784,128]{1,0:T(8,128)(2,1)S(1)}, u32[]{:S(2)}) copy-start(bf16[784,128]{1,0:T(8,128)(2,1)S(1)} %get-tuple-element.9.refs_5_) | copy-start | bytes 602116
  28.7 30.5 %collective-permute-start = (bf16[4,1552,128]{2,1,0:T(8,128)(2,1)S(1)}, bf16[4,1552,128]{2,1,0:T(8,128)(2,1)S(1)}, u32[]{:S(2)}, u32[]{:S(2)}) collective-permute-start(bf16[4,1552,128]{2,1,0:T(8,128)(2,1)S(1)} %all_to_all.10.refs_0_), channel_id=1, source_target_pairs={{0,4},{4,0},{1,5},{5,1},{2,6},{6,2},{3,7},{7,3},{8,12},{12,8},{9,1... | collective-permute-start | bytes 4767752 | tf_op jit(solution)/shard_map/ppermute | solution.py:229
  30.6 10.9 %collective-permute-start.1 = (bf16[784,128]{1,0:T(8,128)(2,1)S(1)}, bf16[784,128]{1,0:T(8,128)(2,1)S(1)}, u32[]{:S(2)}, u32[]{:S(2)}) collective-permute-start(bf16[784,128]{1,0:T(8,128)(2,1)S(1)} %get-tuple-element.9.refs_5_), channel_id=1, source_target_pairs={{0,32},{4,36},{32,8},{36,12},{8,40},{12,44},{40,16},{44,20},{16,48... | collective-permute-start | bytes 602120 | tf_op jit(solution)/shard_map/ppermute | solution.py:218
  32.3 9.3 %collective-permute-start.12 = (bf16[784,128]{1,0:T(8,128)(2,1)}, bf16[784,128]{1,0:T(8,128)(2,1)S(1)}, u32[]{:S(2)}, u32[]{:S(2)}) collective-permute-start(bf16[784,128]{1,0:T(8,128)(2,1)} %get-tuple-element.10), channel_id=1, source_target_pairs={{0,60},{4,56},{32,4},{36,0},{8,36},{12,32},{40,12},{44,8},{16,44},... | collective-permute-start | bytes 602120 | tf_op jit(solution)/shard_map/ppermute | solution.py:218
  36.1 8.8 %collective-permute-start.4 = (bf16[784,128]{1,0:T(8,128)(2,1)S(1)}, bf16[784,128]{1,0:T(8,128)(2,1)S(1)}, u32[]{:S(2)}, u32[]{:S(2)}) collective-permute-start(bf16[784,128]{1,0:T(8,128)(2,1)S(1)} %get-tuple-element.9.refs_5_), channel_id=1, source_target_pairs={{0,56},{4,60},{32,0},{36,4},{8,32},{12,36},{40,8},{44,12},{16,40},... | collective-permute-start | bytes 602120 | tf_op jit(solution)/shard_map/ppermute | solution.py:218
  37.9 10.3 %collective-permute-start.8 = (bf16[784,128]{1,0:T(8,128)(2,1)}, bf16[784,128]{1,0:T(8,128)(2,1)S(1)}, u32[]{:S(2)}, u32[]{:S(2)}) collective-permute-start(bf16[784,128]{1,0:T(8,128)(2,1)} %get-tuple-element.10), channel_id=1, source_target_pairs={{0,36},{4,32},{32,12},{36,8},{8,44},{12,40},{40,20},{44,16},{16,52... | collective-permute-start | bytes 602120 | tf_op jit(solution)/shard_map/ppermute | solution.py:218
  41.6 17.6 %copy-start.1 = (bf16[784,128]{1,0:T(8,128)(2,1)}, bf16[784,128]{1,0:T(8,128)(2,1)S(1)}, u32[]{:S(2)}) copy-start(bf16[784,128]{1,0:T(8,128)(2,1)S(1)} %collective-permute-done.1.refs_4_) | copy-start | bytes 602116
  41.6 9.2 %collective-permute-start.2 = (bf16[784,128]{1,0:T(8,128)(2,1)S(1)}, bf16[784,128]{1,0:T(8,128)(2,1)S(1)}, u32[]{:S(2)}, u32[]{:S(2)}) collective-permute-start(bf16[784,128]{1,0:T(8,128)(2,1)S(1)} %collective-permute-done.1.refs_4_), channel_id=1, source_target_pairs={{0,32},{4,36},{32,8},{36,12},{8,40},{12,44},{40,16},{44,20},{16,48... | collective-permute-start | bytes 602120 | tf_op jit(solution)/shard_map/ppermute | solution.py:218
  41.6 17.6 %copy-start.2 = (bf16[784,128]{1,0:T(8,128)(2,1)}, bf16[784,128]{1,0:T(8,128)(2,1)S(1)}, u32[]{:S(2)}) copy-start(bf16[784,128]{1,0:T(8,128)(2,1)S(1)} %collective-permute-done.12.refs_14_) | copy-start | bytes 602116
  41.6 9.2 %collective-permute-start.13 = (bf16[784,128]{1,0:T(8,128)(2,1)S(1)}, bf16[784,128]{1,0:T(8,128)(2,1)S(1)}, u32[]{:S(2)}, u32[]{:S(2)}) collective-permute-start(bf16[784,128]{1,0:T(8,128)(2,1)S(1)} %collective-permute-done.12.refs_14_), channel_id=1, source_target_pairs={{0,56},{4,60},{32,0},{36,4},{8,32},{12,36},{40,8},{44,12},{16,40},... | collective-permute-start | bytes 602120 | tf_op jit(solution)/shard_map/ppermute | solution.py:218
  44.9 14.2 %copy-start.3 = (bf16[784,128]{1,0:T(8,128)(2,1)}, bf16[784,128]{1,0:T(8,128)(2,1)S(1)}, u32[]{:S(2)}) copy-start(bf16[784,128]{1,0:T(8,128)(2,1)S(1)} %collective-permute-done.4.refs_6_) | copy-start | bytes 602116
  44.9 8.5 %collective-permute-start.5 = (bf16[784,128]{1,0:T(8,128)(2,1)S(1)}, bf16[784,128]{1,0:T(8,128)(2,1)S(1)}, u32[]{:S(2)}, u32[]{:S(2)}) collective-permute-start(bf16[784,128]{1,0:T(8,128)(2,1)S(1)} %collective-permute-done.4.refs_6_), channel_id=1, source_target_pairs={{0,56},{4,60},{32,0},{36,4},{8,32},{12,36},{40,8},{44,12},{16,40},... | collective-permute-start | bytes 602120 | tf_op jit(solution)/shard_map/ppermute | solution.py:218
  48.2 11.0 %copy-start.4 = (bf16[784,128]{1,0:T(8,128)(2,1)}, bf16[784,128]{1,0:T(8,128)(2,1)S(1)}, u32[]{:S(2)}) copy-start(bf16[784,128]{1,0:T(8,128)(2,1)S(1)} %collective-permute-done.8.refs_12_) | copy-start | bytes 602116
  48.2 6.5 %collective-permute-start.9 = (bf16[784,128]{1,0:T(8,128)(2,1)S(1)}, bf16[784,128]{1,0:T(8,128)(2,1)}, u32[]{:S(2)}, u32[]{:S(2)}) collective-permute-start(bf16[784,128]{1,0:T(8,128)(2,1)S(1)} %collective-permute-done.8.refs_12_), channel_id=1, source_target_pairs={{0,32},{4,36},{32,8},{36,12},{8,40},{12,44},{40,16},{44,20},{16,48... | collective-permute-start | bytes 602120 | tf_op jit(solution)/shard_map/ppermute | solution.py:218
  50.8 8.4 %copy-start.5 = (bf16[784,128]{1,0:T(8,128)(2,1)}, bf16[784,128]{1,0:T(8,128)(2,1)S(1)}, u32[]{:S(2)}) copy-start(bf16[784,128]{1,0:T(8,128)(2,1)S(1)} %collective-permute-done.2.refs_3_) | copy-start | bytes 602116
  50.8 8.3 %collective-permute-start.3 = (bf16[784,128]{1,0:T(8,128)(2,1)S(1)}, bf16[784,128]{1,0:T(8,128)(2,1)}, u32[]{:S(2)}, u32[]{:S(2)}) collective-permute-start(bf16[784,128]{1,0:T(8,128)(2,1)S(1)} %collective-permute-done.2.refs_3_), channel_id=1, source_target_pairs={{0,32},{4,36},{32,8},{36,12},{8,40},{12,44},{40,16},{44,20},{16,48... | collective-permute-start | bytes 602120 | tf_op jit(solution)/shard_map/ppermute | solution.py:218
  50.8 8.4 %copy-start.6 = (bf16[784,128]{1,0:T(8,128)(2,1)}, bf16[784,128]{1,0:T(8,128)(2,1)S(1)}, u32[]{:S(2)}) copy-start(bf16[784,128]{1,0:T(8,128)(2,1)S(1)} %collective-permute-done.13.refs_15_) | copy-start | bytes 602116
  50.8 8.3 %collective-permute-start.14 = (bf16[784,128]{1,0:T(8,128)(2,1)S(1)}, bf16[784,128]{1,0:T(8,128)(2,1)}, u32[]{:S(2)}, u32[]{:S(2)}) collective-permute-start(bf16[784,128]{1,0:T(8,128)(2,1)S(1)} %collective-permute-done.13.refs_15_), channel_id=1, source_target_pairs={{0,56},{4,60},{32,0},{36,4},{8,32},{12,36},{40,8},{44,12},{16,40},... | collective-permute-start | bytes 602120 | tf_op jit(solution)/shard_map/ppermute | solution.py:218
  53.5 8.7 %copy-start.7 = (bf16[784,128]{1,0:T(8,128)(2,1)}, bf16[784,128]{1,0:T(8,128)(2,1)S(1)}, u32[]{:S(2)}) copy-start(bf16[784,128]{1,0:T(8,128)(2,1)S(1)} %collective-permute-done.5.refs_7_) | copy-start | bytes 602116
  53.5 8.7 %collective-permute-start.11 = (bf16[784,128]{1,0:T(8,128)(2,1)}, bf16[784,128]{1,0:T(8,128)(2,1)}, u32[]{:S(2)}, u32[]{:S(2)}) collective-permute-start(bf16[784,128]{1,0:T(8,128)(2,1)} %get-tuple-element.10), channel_id=1, source_target_pairs={{0,4},{4,0},{1,5},{5,1},{2,6},{6,2},{3,7},{7,3},{8,12},{12,8},{9,1... | collective-permute-start | bytes 602120 | tf_op jit(solution)/shard_map/ppermute | solution.py:228
  54.7 7.6 %collective-permute-start.6 = (bf16[784,128]{1,0:T(8,128)(2,1)S(1)}, bf16[784,128]{1,0:T(8,128)(2,1)}, u32[]{:S(2)}, u32[]{:S(2)}) collective-permute-start(bf16[784,128]{1,0:T(8,128)(2,1)S(1)} %collective-permute-done.5.refs_7_), channel_id=1, source_target_pairs={{0,56},{4,60},{32,0},{36,4},{8,32},{12,36},{40,8},{44,12},{16,40},... | collective-permute-start | bytes 602120 | tf_op jit(solution)/shard_map/ppermute | solution.py:218
  59.1 6.1 %collective-permute-start.10 = (bf16[784,128]{1,0:T(8,128)(2,1)}, bf16[784,128]{1,0:T(8,128)(2,1)}, u32[]{:S(2)}, u32[]{:S(2)}) collective-permute-start(bf16[784,128]{1,0:T(8,128)(2,1)} %collective-permute-done.9.refs_11_), channel_id=1, source_target_pairs={{0,32},{4,36},{32,8},{36,12},{8,40},{12,44},{40,16},{44,20},{16,48... | collective-permute-start | bytes 602120 | tf_op jit(solution)/shard_map/ppermute | solution.py:218
  59.1 10.3 %collective-permute-start.7 = (bf16[784,128]{1,0:T(8,128)(2,1)}, bf16[784,128]{1,0:T(8,128)(2,1)}, u32[]{:S(2)}, u32[]{:S(2)}) collective-permute-start(bf16[784,128]{1,0:T(8,128)(2,1)} %collective-permute-done.3.refs_2_), channel_id=1, source_target_pairs={{0,32},{4,36},{32,8},{36,12},{8,40},{12,44},{40,16},{44,20},{16,48... | collective-permute-start | bytes 602120 | tf_op jit(solution)/shard_map/ppermute | solution.py:218
  59.2 10.2 %collective-permute-start.15 = (bf16[784,128]{1,0:T(8,128)(2,1)}, bf16[784,128]{1,0:T(8,128)(2,1)}, u32[]{:S(2)}, u32[]{:S(2)}) collective-permute-start(bf16[784,128]{1,0:T(8,128)(2,1)} %collective-permute-done.14.refs_16_), channel_id=1, source_target_pairs={{0,56},{4,60},{32,0},{36,4},{8,32},{12,36},{40,8},{44,12},{16,40},... | collective-permute-start | bytes 602120 | tf_op jit(solution)/shard_map/ppermute | solution.py:218

commit v2 on v1

--- a/solution.py
+++ b/solution.py
@@ -41,10 +41,11 @@
 
 
 class Rows:
-    def __init__(self, sizes, columns, own):
+    def __init__(self, sizes, columns):
         self.rows, self.slots, self.n_y, self.n_lo, self.n_hi, self.tb = sizes
         self.columns = columns
-        self.x, self.y, self.z, self.core = (own[n] for n in range(4))
+        place = 2 * self.n_y * self.rows
+        self.x, self.y, self.z, self.core = (columns[place + n, 0] for n in range(4))
 
     def all(self):
         return [(n, row) for n in range(2 * self.n_y) for row in range(self.rows)]
@@ -135,8 +136,10 @@
         copy.wait()
 
 
-def listed_columns(rows, *refs):
+def listed_columns(rows, place, *refs):
     left, out = refs[:-1], refs[-1]
+    for n in range(4):
+        out[pl.ds(2 * left[0].shape[0] * rows + n, 1), :] = jnp.full((1, out.shape[1]), place[n], jnp.int32)
     n_y, lines = left[0].shape[:2]
     for flip, ref in enumerate(left):
         for y in range(n_y):
@@ -144,16 +147,19 @@
             out[pl.ds((flip * n_y + y) * rows, rows), :] = tail[:rows]
 
 
-def products(sizes, columns, own, *refs):
-    work = Rows(sizes, columns, own)
-    tb = work.tb
-    left, right_in = refs[:2], refs[2:-4]
-    out, right, right_columns, arrived = refs[-4:]
+def products(sizes, columns_in, *refs):
+    left, right_in = refs[:2], refs[2:-6]
+    out, right, right_columns, arrived, columns, listed = refs[-6:]
+    fetch = pltpu.make_async_copy(columns_in, columns, listed)
+    fetch.start()
     copies = [
         pltpu.make_async_copy(ref, right.at[n], arrived.at[n]) for n, ref in enumerate(right_in)
     ]
     for copy in copies:
         copy.start()
+    fetch.wait()
+    work = Rows(sizes, columns)
+    tb = work.tb
     for n, copy in enumerate(copies):
         copy.wait()
         tail = right[n, pl.ds(work.rows * work.slots * tb, TAIL), :]
@@ -240,23 +246,25 @@
     rights = [pltpu.with_memory_space_constraint(r, pltpu.HBM) for r in rights]
     columns = pl.pallas_call(
         functools.partial(listed_columns, rows),
-        out_shape=jax.ShapeDtypeStruct((2 * n_y * rows, tb), jnp.int32),
-        in_specs=[vmem] * len(lefts),
+        out_shape=pltpu.VMEM((2 * n_y * rows + 8, tb), jnp.int32),
+        in_specs=[smem] + [vmem] * len(lefts),
         out_specs=vmem,
         compiler_params=limit,
-    )(*lefts)
+    )(jnp.stack([x, y, z, core]).astype(jnp.int32), *lefts)
     partial = pl.pallas_call(
         functools.partial(products, sizes),
         out_shape=pltpu.VMEM((2 * n_y, n_x, rows, slots, quarter, tb), jnp.bfloat16),
-        in_specs=[smem] * 2 + [vmem] * len(lefts) + [hbm] * len(rights),
+        in_specs=[vmem] * (1 + len(lefts)) + [hbm] * len(rights),
         out_specs=vmem,
         scratch_shapes=[
             pltpu.VMEM((len(rights), *payload), jnp.bfloat16),
             pltpu.VMEM((len(rights) * TAIL, tb), jnp.float32),
             pltpu.SemaphoreType.DMA((len(rights),)),
+            pltpu.SMEM((2 * n_y * rows + 8, tb), jnp.int32),
+            pltpu.SemaphoreType.DMA,
         ],
         compiler_params=pltpu.CompilerParams(vmem_limit_bytes=12 * 2**20),
-    )(columns, jnp.stack([x, y, z, core]).astype(jnp.int32), *lefts, *rights)
+    )(pltpu.with_memory_space_constraint(columns, pltpu.VMEM), *lefts, *rights)
 
     arrived = lax.all_to_all(
         partial.reshape(2 * n_y * n_x, rows, slots, quarter, tb),

time: 106 us -> 106 us (level)
  transfers between devices with their start and end apart: 16 -> 16, of which waited for: 5 -> 5; matrix products, arithmetic and copies ran while one was open for 0% -> 0% of each run, Pallas kernels for 0% -> 1%
where the time goes in v2:
time: 106 us; the launch traced here: 105 us
  blocking collectives  55.1 us (52%)
  starting transfers between devices  26.1 us (25%)
  waiting for transfers between devices  13.9 us (13%)
  Pallas kernels  8.37 us (8%)
  local copies, waits for them, and re-layouts  1.54 us (1%)
    all_to_all x1, blocking collectives, on_device(): lax.all_to_all(partial.reshape(2 * n_y * n_x, rows, slots, quarter, tb),...  30.4 us
    all_to_all x1, blocking collectives, on_device(): lax.all_to_all(packed, 'y', split_axis=0, concat_axis=0, tiled=True)  24.7 us
    ppermute x14, starting transfers between devices, ring(): chains[flip, way] = lax.ppermute(chains[flip, way], ZC, perm)  23 us
    ppermute x14, waiting for transfers between devices, ring(): chains[flip, way] = lax.ppermute(chains[flip, way], ZC, perm)  13.9 us
    pallas_call x1, Pallas kernels, on_device(): pl.pallas_call(functools.partial(products, sizes), out_shape=pltpu.VMEM((...  4.62 us
    pallas_call x1, Pallas kernels, on_device(): pl.pallas_call(first_payloads, out_shape=[pltpu.VMEM(shape, jnp.bfloat16)...  2.26 us
  transfers between devices with their start and end apart: 16, of which 5 were waited for; matrix products, arithmetic and copies ran while one was open for 0% of the time, Pallas kernels for 1%

profile of v2, /device:TPU:1, one launch (start us, length us, event | category | flops | bytes accessed | tf_op | source)
XLA Modules:
  0.0 105.5 jit_solution(5326603150746285161)
XLA Ops:
  0.0 1.5 %copy.3 = bf16[3,4,512,128]{3,2,0,1:T(8,128)(2,1)S(1)} copy(bf16[3,4,512,128]{3,2,1,0:T(8,128)(2,1)} %bitcast.15) | data formatting | bytes 3145728 | tf_op jit(solution)/shard_map/reshape | solution.py:230
  1.6 2.3 %shard_map.28 = (bf16[784,128]{1,0:T(8,128)(2,1)S(1)}, bf16[784,128]{1,0:T(8,128)(2,1)}, bf16[16,128]{1,0:T(8,128)(2,1)S(1)}) custom-call(s32[2]{0:T(128)S(1)} %pad_add_fusion.1.places, s32[3,2,8]{2,1,0:T(2,128)} %bitcast.17, bf16[3,8,2,128,128]{4,3,2,1,0:T(8,128)(2,1)} %tiles.1), custom_call_target="tpu_custom_call" | custom-call | tf_op jit(solution)/shard_map/pallas_call | solution.py:201
  3.9 0.1 pad_maximum_fusion
  4.0 24.7 %all_to_all.10.refs_0_ = bf16[4,1552,128]{2,1,0:T(8,128)(2,1)S(1)} all-to-all(bf16[4,1552,128]{2,1,0:T(8,128)(2,1)S(1)} %pad_maximum_fusion), channel_id=1, replica_groups=mesh['y'=4,'z_lo'=2,'z_hi'=4,'core'=2,'x'=4] {'y'}, dimensions={0} | all-to-all | bytes 3178496 | tf_op jit(solution)/shard_map/all_to_all | solution.py:233
  28.7 2.0 %collective-permute-start = (bf16[4,1552,128]{2,1,0:T(8,128)(2,1)S(1)}, bf16[4,1552,128]{2,1,0:T(8,128)(2,1)S(1)}, u32[]{:S(2)}, u32[]{:S(2)}) collective-permute-start(bf16[4,1552,128]{2,1,0:T(8,128)(2,1)S(1)} %all_to_all.10.refs_0_), channel_id=1, source_target_pairs={{0,4},{4,0},{1,5},{5,1},{2,6},{6,2},{3,7},{7,3},{8,12},{12,8},{9,1... | collective-permute-start | bytes 4767752 | tf_op jit(solution)/shard_map/ppermute | solution.py:235
  30.6 1.6 %collective-permute-start.1 = (bf16[784,128]{1,0:T(8,128)(2,1)S(1)}, bf16[784,128]{1,0:T(8,128)(2,1)S(1)}, u32[]{:S(2)}, u32[]{:S(2)}) collective-permute-start(bf16[784,128]{1,0:T(8,128)(2,1)S(1)} %get-tuple-element.9.refs_5_), channel_id=1, source_target_pairs={{0,32},{4,36},{32,8},{36,12},{8,40},{12,44},{40,16},{44,20},{16,48... | collective-permute-start | bytes 602120 | tf_op jit(solution)/shard_map/ppermute | solution.py:224
  32.3 3.8 %collective-permute-start.12 = (bf16[784,128]{1,0:T(8,128)(2,1)}, bf16[784,128]{1,0:T(8,128)(2,1)S(1)}, u32[]{:S(2)}, u32[]{:S(2)}) collective-permute-start(bf16[784,128]{1,0:T(8,128)(2,1)} %get-tuple-element.10), channel_id=1, source_target_pairs={{0,60},{4,56},{32,4},{36,0},{8,36},{12,32},{40,12},{44,8},{16,44},... | collective-permute-start | bytes 602120 | tf_op jit(solution)/shard_map/ppermute | solution.py:224
  36.1 1.7 %collective-permute-start.4 = (bf16[784,128]{1,0:T(8,128)(2,1)S(1)}, bf16[784,128]{1,0:T(8,128)(2,1)S(1)}, u32[]{:S(2)}, u32[]{:S(2)}) collective-permute-start(bf16[784,128]{1,0:T(8,128)(2,1)S(1)} %get-tuple-element.9.refs_5_), channel_id=1, source_target_pairs={{0,56},{4,60},{32,0},{36,4},{8,32},{12,36},{40,8},{44,12},{16,40},... | collective-permute-start | bytes 602120 | tf_op jit(solution)/shard_map/ppermute | solution.py:224
  37.9 0.4 collective-permute-start.8
  38.3 3.3 %collective-permute-done.1.refs_4_ = bf16[784,128]{1,0:T(8,128)(2,1)S(1)} collective-permute-done((bf16[784,128]{1,0:T(8,128)(2,1)S(1)}, bf16[784,128]{1,0:T(8,128)(2,1)S(1)}, u32[]{:S(2)}, u32[]{:S(2)}) %collective-permute-start.1) | collective-permute-done | bytes 200736 | tf_op jit(solution)/shard_map/ppermute | solution.py:224
  41.6 3.3 %collective-permute-start.13 = (bf16[784,128]{1,0:T(8,128)(2,1)S(1)}, bf16[784,128]{1,0:T(8,128)(2,1)S(1)}, u32[]{:S(2)}, u32[]{:S(2)}) collective-permute-start(bf16[784,128]{1,0:T(8,128)(2,1)S(1)} %collective-permute-done.12.refs_14_), channel_id=1, source_target_pairs={{0,56},{4,60},{32,0},{36,4},{8,32},{12,36},{40,8},{44,12},{16,40},... | collective-permute-start | bytes 602120 | tf_op jit(solution)/shard_map/ppermute | solution.py:224
  44.9 3.2 %collective-permute-start.5 = (bf16[784,128]{1,0:T(8,128)(2,1)S(1)}, bf16[784,128]{1,0:T(8,128)(2,1)S(1)}, u32[]{:S(2)}, u32[]{:S(2)}) collective-permute-start(bf16[784,128]{1,0:T(8,128)(2,1)S(1)} %collective-permute-done.4.refs_6_), channel_id=1, source_target_pairs={{0,56},{4,60},{32,0},{36,4},{8,32},{12,36},{40,8},{44,12},{16,40},... | collective-permute-start | bytes 602120 | tf_op jit(solution)/shard_map/ppermute | solution.py:224
  48.2 2.6 %collective-permute-done.2.refs_3_ = bf16[784,128]{1,0:T(8,128)(2,1)S(1)} collective-permute-done((bf16[784,128]{1,0:T(8,128)(2,1)S(1)}, bf16[784,128]{1,0:T(8,128)(2,1)S(1)}, u32[]{:S(2)}, u32[]{:S(2)}) %collective-permute-start.2) | collective-permute-done | bytes 200736 | tf_op jit(solution)/shard_map/ppermute | solution.py:224
  50.8 2.7 %collective-permute-start.14 = (bf16[784,128]{1,0:T(8,128)(2,1)S(1)}, bf16[784,128]{1,0:T(8,128)(2,1)}, u32[]{:S(2)}, u32[]{:S(2)}) collective-permute-start(bf16[784,128]{1,0:T(8,128)(2,1)S(1)} %collective-permute-done.13.refs_15_), channel_id=1, source_target_pairs={{0,56},{4,60},{32,0},{36,4},{8,32},{12,36},{40,8},{44,12},{16,40},... | collective-permute-start | bytes 602120 | tf_op jit(solution)/shard_map/ppermute | solution.py:224
  53.5 1.1 %collective-permute-start.11 = (bf16[784,128]{1,0:T(8,128)(2,1)}, bf16[784,128]{1,0:T(8,128)(2,1)}, u32[]{:S(2)}, u32[]{:S(2)}) collective-permute-start(bf16[784,128]{1,0:T(8,128)(2,1)} %get-tuple-element.10), channel_id=1, source_target_pairs={{0,4},{4,0},{1,5},{5,1},{2,6},{6,2},{3,7},{7,3},{8,12},{12,8},{9,1... | collective-permute-start | bytes 602120 | tf_op jit(solution)/shard_map/ppermute | solution.py:234
  54.7 3.3 %collective-permute-start.6 = (bf16[784,128]{1,0:T(8,128)(2,1)S(1)}, bf16[784,128]{1,0:T(8,128)(2,1)}, u32[]{:S(2)}, u32[]{:S(2)}) collective-permute-start(bf16[784,128]{1,0:T(8,128)(2,1)S(1)} %collective-permute-done.5.refs_7_), channel_id=1, source_target_pairs={{0,56},{4,60},{32,0},{36,4},{8,32},{12,36},{40,8},{44,12},{16,40},... | collective-permute-start | bytes 602120 | tf_op jit(solution)/shard_map/ppermute | solution.py:224
  57.9 1.2 %collective-permute-done.3.refs_2_ = bf16[784,128]{1,0:T(8,128)(2,1)} collective-permute-done((bf16[784,128]{1,0:T(8,128)(2,1)S(1)}, bf16[784,128]{1,0:T(8,128)(2,1)}, u32[]{:S(2)}, u32[]{:S(2)}) %collective-permute-start.3) | collective-permute-done | bytes 200736 | tf_op jit(solution)/shard_map/ppermute | solution.py:224
  59.2 2.9 %collective-permute-start.15 = (bf16[784,128]{1,0:T(8,128)(2,1)}, bf16[784,128]{1,0:T(8,128)(2,1)}, u32[]{:S(2)}, u32[]{:S(2)}) collective-permute-start(bf16[784,128]{1,0:T(8,128)(2,1)} %collective-permute-done.14.refs_16_), channel_id=1, source_target_pairs={{0,56},{4,60},{32,0},{36,4},{8,32},{12,36},{40,8},{44,12},{16,40},... | collective-permute-start | bytes 602120 | tf_op jit(solution)/shard_map/ppermute | solution.py:224
  62.2 0.5 shard_map.29.columns_in
  62.8 2.4 %collective-permute-done.10.refs_10_ = bf16[784,128]{1,0:T(8,128)(2,1)} collective-permute-done((bf16[784,128]{1,0:T(8,128)(2,1)}, bf16[784,128]{1,0:T(8,128)(2,1)}, u32[]{:S(2)}, u32[]{:S(2)}) %collective-permute-start.10) | collective-permute-done | bytes 200736 | tf_op jit(solution)/shard_map/ppermute | solution.py:224
  65.2 4.2 %collective-permute-done.7.refs_9_ = bf16[784,128]{1,0:T(8,128)(2,1)} collective-permute-done((bf16[784,128]{1,0:T(8,128)(2,1)}, bf16[784,128]{1,0:T(8,128)(2,1)}, u32[]{:S(2)}, u32[]{:S(2)}) %collective-permute-start.7) | collective-permute-done | bytes 200736 | tf_op jit(solution)/shard_map/ppermute | solution.py:224
  69.4 4.6 %shard_map.30 = bf16[8,4,3,2,32,128]{5,4,3,2,1,0:T(8,128)(2,1)S(1)} custom-call(s32[32,128]{1,0:T(8,128)S(1)} %shard_map.29.columns_in, bf16[4,1552,128]{2,1,0:T(8,128)(2,1)S(1)} %all_to_all.10.refs_0_, bf16[4,1552,128]{2,1,0:T(8,128)(2,1)S(1)} %collective-permute-done.refs_1_, bf16[784,128]{1,0:T(8,128)(2,1)} %collective-permute-done.3.refs_2_, ...), custom_call_target="tpu_custom_call" | custom-call | tf_op jit(solution)/shard_map/pallas_call | solution.py:254
  74.1 30.4 %all_to_all.11 = bf16[32,3,2,32,128]{4,3,2,1,0:T(8,128)(2,1)S(1)} all-to-all(bf16[32,3,2,32,128]{4,3,2,1,0:T(8,128)(2,1)S(1)} %bitcast.14), channel_id=1, replica_groups=mesh['y'=4,'z_lo'=2,'z_hi'=4,'core'=2,'x'=4] {'y','core','x'}, dimensions={0} | all-to-all | bytes 3145728 | tf_op jit(solution)/shard_map/all_to_all | solution.py:269
  104.5 0.9 shard_map.31
  (35 shorter events, 0.3 us)
Async XLA Ops:
  3.9 32.3 %copy-start = (bf16[784,128]{1,0:T(8,128)(2,1)}, bf16[784,128]{1,0:T(8,128)(2,1)S(1)}, u32[]{:S(2)}) copy-start(bf16[784,128]{1,0:T(8,128)(2,1)S(1)} %get-tuple-element.9.refs_5_) | copy-start | bytes 602116
  28.7 30.5 %collective-permute-start = (bf16[4,1552,128]{2,1,0:T(8,128)(2,1)S(1)}, bf16[4,1552,128]{2,1,0:T(8,128)(2,1)S(1)}, u32[]{:S(2)}, u32[]{:S(2)}) collective-permute-start(bf16[4,1552,128]{2,1,0:T(8,128)(2,1)S(1)} %all_to_all.10.refs_0_), channel_id=1, source_target_pairs={{0,4},{4,0},{1,5},{5,1},{2,6},{6,2},{3,7},{7,3},{8,12},{12,8},{9,1... | collective-permute-start | bytes 4767752 | tf_op jit(solution)/shard_map/ppermute | solution.py:235
  30.6 10.9 %collective-permute-start.1 = (bf16[784,128]{1,0:T(8,128)(2,1)S(1)}, bf16[784,128]{1,0:T(8,128)(2,1)S(1)}, u32[]{:S(2)}, u32[]{:S(2)}) collective-permute-start(bf16[784,128]{1,0:T(8,128)(2,1)S(1)} %get-tuple-element.9.refs_5_), channel_id=1, source_target_pairs={{0,32},{4,36},{32,8},{36,12},{8,40},{12,44},{40,16},{44,20},{16,48... | collective-permute-start | bytes 602120 | tf_op jit(solution)/shard_map/ppermute | solution.py:224
  32.3 9.3 %collective-permute-start.12 = (bf16[784,128]{1,0:T(8,128)(2,1)}, bf16[784,128]{1,0:T(8,128)(2,1)S(1)}, u32[]{:S(2)}, u32[]{:S(2)}) collective-permute-start(bf16[784,128]{1,0:T(8,128)(2,1)} %get-tuple-element.10), channel_id=1, source_target_pairs={{0,60},{4,56},{32,4},{36,0},{8,36},{12,32},{40,12},{44,8},{16,44},... | collective-permute-start | bytes 602120 | tf_op jit(solution)/shard_map/ppermute | solution.py:224
  36.1 8.8 %collective-permute-start.4 = (bf16[784,128]{1,0:T(8,128)(2,1)S(1)}, bf16[784,128]{1,0:T(8,128)(2,1)S(1)}, u32[]{:S(2)}, u32[]{:S(2)}) collective-permute-start(bf16[784,128]{1,0:T(8,128)(2,1)S(1)} %get-tuple-element.9.refs_5_), channel_id=1, source_target_pairs={{0,56},{4,60},{32,0},{36,4},{8,32},{12,36},{40,8},{44,12},{16,40},... | collective-permute-start | bytes 602120 | tf_op jit(solution)/shard_map/ppermute | solution.py:224
  37.9 10.3 %collective-permute-start.8 = (bf16[784,128]{1,0:T(8,128)(2,1)}, bf16[784,128]{1,0:T(8,128)(2,1)S(1)}, u32[]{:S(2)}, u32[]{:S(2)}) collective-permute-start(bf16[784,128]{1,0:T(8,128)(2,1)} %get-tuple-element.10), channel_id=1, source_target_pairs={{0,36},{4,32},{32,12},{36,8},{8,44},{12,40},{40,20},{44,16},{16,52... | collective-permute-start | bytes 602120 | tf_op jit(solution)/shard_map/ppermute | solution.py:224
  41.6 17.6 %copy-start.1 = (bf16[784,128]{1,0:T(8,128)(2,1)}, bf16[784,128]{1,0:T(8,128)(2,1)S(1)}, u32[]{:S(2)}) copy-start(bf16[784,128]{1,0:T(8,128)(2,1)S(1)} %collective-permute-done.1.refs_4_) | copy-start | bytes 602116
  41.6 9.2 %collective-permute-start.2 = (bf16[784,128]{1,0:T(8,128)(2,1)S(1)}, bf16[784,128]{1,0:T(8,128)(2,1)S(1)}, u32[]{:S(2)}, u32[]{:S(2)}) collective-permute-start(bf16[784,128]{1,0:T(8,128)(2,1)S(1)} %collective-permute-done.1.refs_4_), channel_id=1, source_target_pairs={{0,32},{4,36},{32,8},{36,12},{8,40},{12,44},{40,16},{44,20},{16,48... | collective-permute-start | bytes 602120 | tf_op jit(solution)/shard_map/ppermute | solution.py:224
  41.6 17.6 %copy-start.2 = (bf16[784,128]{1,0:T(8,128)(2,1)}, bf16[784,128]{1,0:T(8,128)(2,1)S(1)}, u32[]{:S(2)}) copy-start(bf16[784,128]{1,0:T(8,128)(2,1)S(1)} %collective-permute-done.12.refs_14_) | copy-start | bytes 602116
  41.6 9.2 %collective-permute-start.13 = (bf16[784,128]{1,0:T(8,128)(2,1)S(1)}, bf16[784,128]{1,0:T(8,128)(2,1)S(1)}, u32[]{:S(2)}, u32[]{:S(2)}) collective-permute-start(bf16[784,128]{1,0:T(8,128)(2,1)S(1)} %collective-permute-done.12.refs_14_), channel_id=1, source_target_pairs={{0,56},{4,60},{32,0},{36,4},{8,32},{12,36},{40,8},{44,12},{16,40},... | collective-permute-start | bytes 602120 | tf_op jit(solution)/shard_map/ppermute | solution.py:224
  44.9 14.2 %copy-start.3 = (bf16[784,128]{1,0:T(8,128)(2,1)}, bf16[784,128]{1,0:T(8,128)(2,1)S(1)}, u32[]{:S(2)}) copy-start(bf16[784,128]{1,0:T(8,128)(2,1)S(1)} %collective-permute-done.4.refs_6_) | copy-start | bytes 602116
  44.9 8.5 %collective-permute-start.5 = (bf16[784,128]{1,0:T(8,128)(2,1)S(1)}, bf16[784,128]{1,0:T(8,128)(2,1)S(1)}, u32[]{:S(2)}, u32[]{:S(2)}) collective-permute-start(bf16[784,128]{1,0:T(8,128)(2,1)S(1)} %collective-permute-done.4.refs_6_), channel_id=1, source_target_pairs={{0,56},{4,60},{32,0},{36,4},{8,32},{12,36},{40,8},{44,12},{16,40},... | collective-permute-start | bytes 602120 | tf_op jit(solution)/shard_map/ppermute | solution.py:224
  48.2 11.0 %copy-start.4 = (bf16[784,128]{1,0:T(8,128)(2,1)}, bf16[784,128]{1,0:T(8,128)(2,1)S(1)}, u32[]{:S(2)}) copy-start(bf16[784,128]{1,0:T(8,128)(2,1)S(1)} %collective-permute-done.8.refs_12_) | copy-start | bytes 602116
  48.2 6.5 %collective-permute-start.9 = (bf16[784,128]{1,0:T(8,128)(2,1)S(1)}, bf16[784,128]{1,0:T(8,128)(2,1)}, u32[]{:S(2)}, u32[]{:S(2)}) collective-permute-start(bf16[784,128]{1,0:T(8,128)(2,1)S(1)} %collective-permute-done.8.refs_12_), channel_id=1, source_target_pairs={{0,32},{4,36},{32,8},{36,12},{8,40},{12,44},{40,16},{44,20},{16,48... | collective-permute-start | bytes 602120 | tf_op jit(solution)/shard_map/ppermute | solution.py:224
  50.8 8.4 %copy-start.5 = (bf16[784,128]{1,0:T(8,128)(2,1)}, bf16[784,128]{1,0:T(8,128)(2,1)S(1)}, u32[]{:S(2)}) copy-start(bf16[784,128]{1,0:T(8,128)(2,1)S(1)} %collective-permute-done.2.refs_3_) | copy-start | bytes 602116
  50.8 8.3 %collective-permute-start.3 = (bf16[784,128]{1,0:T(8,128)(2,1)S(1)}, bf16[784,128]{1,0:T(8,128)(2,1)}, u32[]{:S(2)}, u32[]{:S(2)}) collective-permute-start(bf16[784,128]{1,0:T(8,128)(2,1)S(1)} %collective-permute-done.2.refs_3_), channel_id=1, source_target_pairs={{0,32},{4,36},{32,8},{36,12},{8,40},{12,44},{40,16},{44,20},{16,48... | collective-permute-start | bytes 602120 | tf_op jit(solution)/shard_map/ppermute | solution.py:224
  50.8 8.4 %copy-start.6 = (bf16[784,128]{1,0:T(8,128)(2,1)}, bf16[784,128]{1,0:T(8,128)(2,1)S(1)}, u32[]{:S(2)}) copy-start(bf16[784,128]{1,0:T(8,128)(2,1)S(1)} %collective-permute-done.13.refs_15_) | copy-start | bytes 602116
  50.8 8.3 %collective-permute-start.14 = (bf16[784,128]{1,0:T(8,128)(2,1)S(1)}, bf16[784,128]{1,0:T(8,128)(2,1)}, u32[]{:S(2)}, u32[]{:S(2)}) collective-permute-start(bf16[784,128]{1,0:T(8,128)(2,1)S(1)} %collective-permute-done.13.refs_15_), channel_id=1, source_target_pairs={{0,56},{4,60},{32,0},{36,4},{8,32},{12,36},{40,8},{44,12},{16,40},... | collective-permute-start | bytes 602120 | tf_op jit(solution)/shard_map/ppermute | solution.py:224
  53.5 9.3 %copy-start.7 = (bf16[784,128]{1,0:T(8,128)(2,1)}, bf16[784,128]{1,0:T(8,128)(2,1)S(1)}, u32[]{:S(2)}) copy-start(bf16[784,128]{1,0:T(8,128)(2,1)S(1)} %collective-permute-done.5.refs_7_) | copy-start | bytes 602116
  53.5 9.3 %collective-permute-start.11 = (bf16[784,128]{1,0:T(8,128)(2,1)}, bf16[784,128]{1,0:T(8,128)(2,1)}, u32[]{:S(2)}, u32[]{:S(2)}) collective-permute-start(bf16[784,128]{1,0:T(8,128)(2,1)} %get-tuple-element.10), channel_id=1, source_target_pairs={{0,4},{4,0},{1,5},{5,1},{2,6},{6,2},{3,7},{7,3},{8,12},{12,8},{9,1... | collective-permute-start | bytes 602120 | tf_op jit(solution)/shard_map/ppermute | solution.py:234
  54.7 8.1 %collective-permute-start.6 = (bf16[784,128]{1,0:T(8,128)(2,1)S(1)}, bf16[784,128]{1,0:T(8,128)(2,1)}, u32[]{:S(2)}, u32[]{:S(2)}) collective-permute-start(bf16[784,128]{1,0:T(8,128)(2,1)S(1)} %collective-permute-done.5.refs_7_), channel_id=1, source_target_pairs={{0,56},{4,60},{32,0},{36,4},{8,32},{12,36},{40,8},{44,12},{16,40},... | collective-permute-start | bytes 602120 | tf_op jit(solution)/shard_map/ppermute | solution.py:224
  59.1 6.1 %collective-permute-start.10 = (bf16[784,128]{1,0:T(8,128)(2,1)}, bf16[784,128]{1,0:T(8,128)(2,1)}, u32[]{:S(2)}, u32[]{:S(2)}) collective-permute-start(bf16[784,128]{1,0:T(8,128)(2,1)} %collective-permute-done.9.refs_11_), channel_id=1, source_target_pairs={{0,32},{4,36},{32,8},{36,12},{8,40},{12,44},{40,16},{44,20},{16,48... | collective-permute-start | bytes 602120 | tf_op jit(solution)/shard_map/ppermute | solution.py:224
  59.1 10.3 %collective-permute-start.7 = (bf16[784,128]{1,0:T(8,128)(2,1)}, bf16[784,128]{1,0:T(8,128)(2,1)}, u32[]{:S(2)}, u32[]{:S(2)}) collective-permute-start(bf16[784,128]{1,0:T(8,128)(2,1)} %collective-permute-done.3.refs_2_), channel_id=1, source_target_pairs={{0,32},{4,36},{32,8},{36,12},{8,40},{12,44},{40,16},{44,20},{16,48... | collective-permute-start | bytes 602120 | tf_op jit(solution)/shard_map/ppermute | solution.py:224
  59.2 10.2 %collective-permute-start.15 = (bf16[784,128]{1,0:T(8,128)(2,1)}, bf16[784,128]{1,0:T(8,128)(2,1)}, u32[]{:S(2)}, u32[]{:S(2)}) collective-permute-start(bf16[784,128]{1,0:T(8,128)(2,1)} %collective-permute-done.14.refs_16_), channel_id=1, source_target_pairs={{0,56},{4,60},{32,0},{36,4},{8,32},{12,36},{40,8},{44,12},{16,40},... | collective-permute-start | bytes 602120 | tf_op jit(solution)/shard_map/ppermute | solution.py:224

commit v3 on v0

--- a/solution.py
+++ b/solution.py
@@ -20,13 +20,15 @@
     return (z % n_lo) * n_hi + z // n_lo
 
 
-def z_steps(step, flip, n_hi, n_lo):
+def z_pairs(odd, flip, n_hi, n_lo):
     n = n_hi * n_lo
-    return [
-        (z_place(z, n_hi, n_lo) * 2 + c, z_place(z + step, n_hi, n_lo) * 2 + (c ^ flip))
-        for z in range(n)
-        for c in range(2)
-    ]
+    pairs = []
+    for z in range(n):
+        to = z + 1 if (z + odd) % 2 == 0 else z - 1
+        pairs += [
+            (z_place(z, n_hi, n_lo) * 2 + c, z_place(to, n_hi, n_lo) * 2 + (c ^ flip)) for c in range(2)
+        ]
+    return pairs
 
 
 def picked(tiles, columns, wanted):
@@ -41,10 +43,11 @@
 
 
 class Rows:
-    def __init__(self, sizes, columns, own):
+    def __init__(self, sizes, columns):
         self.rows, self.slots, self.n_y, self.n_lo, self.n_hi, self.tb = sizes
         self.columns = columns
-        self.x, self.y, self.z, self.core = (own[n] for n in range(4))
+        place = 2 * self.n_y * self.rows
+        self.x, self.y, self.z, self.core = (columns[place + n, 0] for n in range(4))
 
     def all(self):
         return [(n, row) for n in range(2 * self.n_y) for row in range(self.rows)]
@@ -65,8 +68,11 @@
         local = jnp.where(listed, column - first * (self.rows * 2 * self.n_hi), 0)
         owner = lax.div(local, self.rows)
         inner_z = lax.div(owner, 2) * self.n_lo + group
-        behind = lax.rem(inner_z - self.z - n_z // 2 - 1 + 2 * n_z, n_z)
-        source = (lax.rem(owner, 2) ^ self.core) * n_z + behind
+        ahead = lax.rem(inner_z - self.z + n_z, n_z)
+        steps = jnp.minimum(ahead, n_z - ahead)
+        chain = lax.rem(self.z + steps + jnp.where(ahead < n_z // 2, 1, 0), 2)
+        at = jnp.where(ahead == 0, 0, jnp.where(ahead == n_z // 2, n_z - 1, 2 * steps - 1 + chain))
+        source = (lax.rem(owner, 2) ^ self.core) * n_z + at
         return listed, source, (local - owner * self.rows) * self.slots
 
     def product(self, left, right, right_columns, n, row):
@@ -134,23 +140,28 @@
         copy.wait()
 
 
-def listed_columns(rows, *refs):
+def listed_columns(rows, place, *refs):
     left, out = refs[:-1], refs[-1]
+    for n in range(4):
+        out[pl.ds(len(left) * rows + n, 1), :] = jnp.full((1, out.shape[1]), place[n], jnp.int32)
     for n, ref in enumerate(left):
         tail = ref[pl.ds(ref.shape[0] - TAIL, TAIL), :].astype(jnp.float32).astype(jnp.int32)
         out[pl.ds(n * rows, rows), :] = tail[:rows]
 
 
-def products(sizes, columns, own, *refs):
-    work = Rows(sizes, columns, own)
-    n_left, tb = 2 * work.n_y, work.tb
-    left, right_in = refs[:n_left], refs[n_left:-4]
-    out, right, right_columns, arrived = refs[-4:]
+def products(n_left, sizes, columns_in, *refs):
+    left, right_in = refs[:n_left], refs[n_left:-6]
+    out, right, right_columns, arrived, columns, listed = refs[-6:]
+    fetch = pltpu.make_async_copy(columns_in, columns, listed)
+    fetch.start()
     copies = [
         pltpu.make_async_copy(ref, right.at[n], arrived.at[n]) for n, ref in enumerate(right_in)
     ]
     for copy in copies:
         copy.start()
+    fetch.wait()
+    work = Rows(sizes, columns)
+    tb = work.tb
     for n, copy in enumerate(copies):
         copy.wait()
         tail = right[n, pl.ds(work.rows * work.slots * tb, TAIL), :]
@@ -205,18 +216,18 @@
         pltpu.with_memory_space_constraint(tile_columns.transpose(0, 2, 1), pltpu.HBM),
         pltpu.with_memory_space_constraint(density_tiles, pltpu.HBM),
     )
-    right = {}
-    right[0, 0] = own
-    chains = {(0, 1): own, (0, -1): own, (1, 1): other, (1, -1): other}
+    right = {(0, 0, 0): own}
+    held = {(flip, chain): (own, other)[flip] for flip in range(2) for chain in range(2)}
 
     def ring(step, keys):
-        for flip, way in keys:
-            perm = z_steps(way, flip if step == 1 else 0, n_hi, n_lo)
-            chains[flip, way] = lax.ppermute(chains[flip, way], ZC, perm)
-            right[flip, (-way * step) % n_z] = chains[flip, way]
+        for flip, chain in keys:
+            perm = z_pairs((chain + step - 1) % 2, flip if step == 1 else 0, n_hi, n_lo)
+            held[flip, chain] = lax.ppermute(held[flip, chain], ZC, perm)
+            right[flip, step, chain] = held[flip, chain]
 
     half = n_z // 2
-    ring(1, [(0, 1), (0, -1), (1, 1), (1, -1)])
+    every = [(flip, chain) for flip in range(2) for chain in range(2)]
+    ring(1, every)
 
     def left_payload(to_y):
         tiles = lax.dynamic_slice_in_dim(density_tiles, 2 * to_y, 2, 1)
@@ -227,41 +238,49 @@
         perm = [(s, (s + step) % n_y) for s in range(n_y)]
         sent = left_payload((y + step) % n_y)
         left[0, -step % n_y] = lax.ppermute(sent, "y", perm)
-    right[1, 0] = lax.ppermute(other, "core", cores)
+    right[1, 0, 0] = lax.ppermute(other, "core", cores)
     left[1, 0] = lax.ppermute(left[0, 0], "core", cores)
     for step in range(1, n_y):
         left[1, step] = lax.ppermute(left[0, step], "core", cores)
 
     for step in range(2, half):
-        ring(step, [(0, 1), (0, -1), (1, 1), (1, -1)])
-    ring(half, [(0, 1), (1, -1)])
+        ring(step, every)
+    ring(half, [(0, 0), (1, 1)])
 
     left_keys = [(flip, step) for flip in range(2) for step in range(n_y)]
     sizes = (rows, slots, n_y, n_lo, n_hi, tb)
     quarter = tb // n_x
 
-    rights = [right[flip, (n + half + 1) % n_z] for flip in range(2) for n in range(n_z)]
+    rights = [
+        right[key]
+        for flip in range(2)
+        for key in [(flip, 0, 0)]
+        + [(flip, step, chain) for step in range(1, half) for chain in range(2)]
+        + [(flip, half, flip)]
+    ]
     lefts = [pltpu.with_memory_space_constraint(left[k], pltpu.VMEM) for k in left_keys]
     rights = [pltpu.with_memory_space_constraint(r, pltpu.HBM) for r in rights]
     columns = pl.pallas_call(
         functools.partial(listed_columns, rows),
-        out_shape=jax.ShapeDtypeStruct((len(lefts) * rows, tb), jnp.int32),
-        in_specs=[vmem] * len(lefts),
+        out_shape=pltpu.VMEM((2 * n_y * rows + 8, tb), jnp.int32),
+        in_specs=[smem] + [vmem] * len(lefts),
         out_specs=vmem,
         compiler_params=limit,
-    )(*lefts)
+    )(jnp.stack([x, y, z, core]).astype(jnp.int32), *lefts)
     partial = pl.pallas_call(
-        functools.partial(products, sizes),
+        functools.partial(products, len(lefts), sizes),
         out_shape=pltpu.VMEM((2 * n_y, n_x, rows, slots, quarter, tb), jnp.bfloat16),
-        in_specs=[smem] * 2 + [vmem] * len(lefts) + [hbm] * len(rights),
+        in_specs=[vmem] * (1 + len(lefts)) + [hbm] * len(rights),
         out_specs=vmem,
         scratch_shapes=[
             pltpu.VMEM((len(rights), *payload), jnp.bfloat16),
             pltpu.VMEM((len(rights) * TAIL, tb), jnp.float32),
             pltpu.SemaphoreType.DMA((len(rights),)),
+            pltpu.SMEM((2 * n_y * rows + 8, tb), jnp.int32),
+            pltpu.SemaphoreType.DMA,
         ],
         compiler_params=pltpu.CompilerParams(vmem_limit_bytes=12 * 2**20),
-    )(columns, jnp.stack([x, y, z, core]).astype(jnp.int32), *lefts, *rights)
+    )(pltpu.with_memory_space_constraint(columns, pltpu.VMEM), *lefts, *rights)
 
     arrived = lax.all_to_all(
         partial.reshape(2 * n_y * n_x, rows, slots, quarter, tb),

time: 98.5 us -> 98.4 us (level)
  starting transfers between devices: 25.2 us -> 35.7 us
  waiting for transfers between devices: 29.1 us -> 18.8 us
    ppermute x15, starting transfers between devices: 19 us -> 29.4 us  [the longest x14 28.3 us: ring(): held[flip, chain] = lax.ppermute(held[flip, chain], ZC, perm)]
    ppermute x3, waiting for transfers between devices: 5.94 us -> 0.54 us  [on_device(): left[0, -step % n_y] = lax.ppermute(sent, 'y', perm)]
    ppermute x15, waiting for transfers between devices: 23.2 us -> 18.2 us  [the longest x14 18.2 us: ring(): held[flip, chain] = lax.ppermute(held[flip, chain], ZC, perm)]
  transfers between devices with their start and end apart: 22 -> 22, of which waited for: 7 -> 9; matrix products, arithmetic and copies ran while one was open for 0% -> 0% of each run, Pallas kernels for 0% -> 1%
where the time goes in v3:
time: 98.4 us; the launch traced here: 98.3 us
  starting transfers between devices  35.7 us (36%)
  blocking collectives  35.5 us (36%)
  waiting for transfers between devices  18.8 us (19%)
  Pallas kernels  7.78 us (8%)
    all_to_all x1, blocking collectives, on_device(): lax.all_to_all(partial.reshape(2 * n_y * n_x, rows, slots, quarter, tb),...  35.5 us
    ppermute x14, starting transfers between devices, ring(): held[flip, chain] = lax.ppermute(held[flip, chain], ZC, perm)  28.3 us
    ppermute x14, waiting for transfers between devices, ring(): held[flip, chain] = lax.ppermute(held[flip, chain], ZC, perm)  18.2 us
    pallas_call x1, Pallas kernels, on_device(): pl.pallas_call(functools.partial(products, len(lefts), sizes), out_shape=...  4.7 us
    ppermute x3, starting transfers between devices, on_device(): left[0, -step % n_y] = lax.ppermute(sent, 'y', perm)  4.68 us
  transfers between devices with their start and end apart: 22, of which 9 were waited for; matrix products, arithmetic and copies ran while one was open for 0% of the time, Pallas kernels for 1%

profile of v3, /device:TPU:1, one launch (start us, length us, event | category | flops | bytes accessed | tf_op | source)
XLA Modules:
  0.0 98.3 jit_solution(11053619162822329447)
XLA Ops:
  0.1 1.6 %shard_map.28 = (bf16[784,128]{1,0:T(8,128)(2,1)S(1)}, bf16[784,128]{1,0:T(8,128)(2,1)S(1)}, bf16[16,128]{1,0:T(8,128)(2,1)S(1)}) custom-call(s32[2]{0:T(128)S(1)} %pad_add_fusion.1.places, s32[3,2,8]{2,1,0:T(2,128)} %bitcast.19, bf16[3,8,2,128,128]{4,3,2,1,0:T(8,128)(2,1)} %tiles.1), custom_call_target="tpu_custom_call" | custom-call | tf_op jit(solution)/shard_map/pallas_call | solution.py:203
  1.7 6.5 %collective-permute-start.8 = (bf16[784,128]{1,0:T(8,128)(2,1)S(1)}, bf16[784,128]{1,0:T(8,128)(2,1)S(1)}, u32[]{:S(2)}, u32[]{:S(2)}) collective-permute-start(bf16[784,128]{1,0:T(8,128)(2,1)S(1)} %get-tuple-element.9.refs_8_), channel_id=1, source_target_pairs={{0,56},{4,60},{32,8},{36,12},{8,32},{12,36},{40,16},{44,20},{16,40... | collective-permute-start | bytes 602120 | tf_op jit(solution)/shard_map/ppermute | solution.py:225
  8.2 2.6 %collective-permute-start.16 = (bf16[784,128]{1,0:T(8,128)(2,1)S(1)}, bf16[784,128]{1,0:T(8,128)(2,1)}, u32[]{:S(2)}, u32[]{:S(2)}) collective-permute-start(bf16[784,128]{1,0:T(8,128)(2,1)S(1)} %get-tuple-element.10), channel_id=1, source_target_pairs={{0,60},{4,56},{32,12},{36,8},{8,36},{12,32},{40,20},{44,16},{16,44... | collective-permute-start | bytes 602120 | tf_op jit(solution)/shard_map/ppermute | solution.py:225
  11.1 1.4 %collective-permute-start.2 = (bf16[1552,128]{1,0:T(8,128)(2,1)S(1)}, bf16[1552,128]{1,0:T(8,128)(2,1)S(1)}, u32[]{:S(2)}, u32[]{:S(2)}) collective-permute-start(bf16[1552,128]{1,0:T(8,128)(2,1)S(1)} %get-tuple-element.15), channel_id=1, source_target_pairs={{0,64},{64,128},{128,192},{192,0},{1,65},{65,129},{129,193},{193,1... | collective-permute-start | bytes 1191944 | tf_op jit(solution)/shard_map/ppermute | solution.py:240
  12.5 1.5 %collective-permute-start = (bf16[1552,128]{1,0:T(8,128)(2,1)S(1)}, bf16[1552,128]{1,0:T(8,128)(2,1)S(1)}, u32[]{:S(2)}, u32[]{:S(2)}) collective-permute-start(bf16[1552,128]{1,0:T(8,128)(2,1)S(1)} %get-tuple-element.16), channel_id=1, source_target_pairs={{0,192},{64,0},{128,64},{192,128},{1,193},{65,1},{129,65},{193,129... | collective-permute-start | bytes 1191944 | tf_op jit(solution)/shard_map/ppermute | solution.py:240
  14.0 1.8 %collective-permute-start.1 = (bf16[1552,128]{1,0:T(8,128)(2,1)S(1)}, bf16[1552,128]{1,0:T(8,128)(2,1)S(1)}, u32[]{:S(2)}, u32[]{:S(2)}) collective-permute-start(bf16[1552,128]{1,0:T(8,128)(2,1)S(1)} %get-tuple-element.17), channel_id=1, source_target_pairs={{0,128},{64,192},{128,0},{192,64},{1,129},{65,193},{129,1},{193,65... | collective-permute-start | bytes 1191944 | tf_op jit(solution)/shard_map/ppermute | solution.py:240
  16.5 1.5 %collective-permute-done.16.refs_18_ = bf16[784,128]{1,0:T(8,128)(2,1)} collective-permute-done((bf16[784,128]{1,0:T(8,128)(2,1)S(1)}, bf16[784,128]{1,0:T(8,128)(2,1)}, u32[]{:S(2)}, u32[]{:S(2)}) %collective-permute-start.16) | collective-permute-done | bytes 200736 | tf_op jit(solution)/shard_map/ppermute | solution.py:225
  18.3 3.5 %collective-permute-done.15.refs_17_ = bf16[784,128]{1,0:T(8,128)(2,1)S(1)} collective-permute-done((bf16[784,128]{1,0:T(8,128)(2,1)S(1)}, bf16[784,128]{1,0:T(8,128)(2,1)S(1)}, u32[]{:S(2)}, u32[]{:S(2)}) %collective-permute-start.15) | collective-permute-done | bytes 200736 | tf_op jit(solution)/shard_map/ppermute | solution.py:225
  21.8 1.7 %collective-permute-start.10 = (bf16[784,128]{1,0:T(8,128)(2,1)S(1)}, bf16[784,128]{1,0:T(8,128)(2,1)}, u32[]{:S(2)}, u32[]{:S(2)}) collective-permute-start(bf16[784,128]{1,0:T(8,128)(2,1)S(1)} %collective-permute-done.8.refs_10_), channel_id=1, source_target_pairs={{0,32},{4,36},{32,0},{36,4},{8,40},{12,44},{40,8},{44,12},{16,48},... | collective-permute-start | bytes 602120 | tf_op jit(solution)/shard_map/ppermute | solution.py:225
  23.5 4.1 %collective-permute-start.9 = (bf16[784,128]{1,0:T(8,128)(2,1)S(1)}, bf16[784,128]{1,0:T(8,128)(2,1)S(1)}, u32[]{:S(2)}, u32[]{:S(2)}) collective-permute-start(bf16[784,128]{1,0:T(8,128)(2,1)S(1)} %collective-permute-done.7.refs_9_), channel_id=1, source_target_pairs={{0,56},{4,60},{32,8},{36,12},{8,32},{12,36},{40,16},{44,20},{16,40... | collective-permute-start | bytes 602120 | tf_op jit(solution)/shard_map/ppermute | solution.py:225
  27.6 4.7 %collective-permute-start.18 = (bf16[784,128]{1,0:T(8,128)(2,1)}, bf16[784,128]{1,0:T(8,128)(2,1)S(1)}, u32[]{:S(2)}, u32[]{:S(2)}) collective-permute-start(bf16[784,128]{1,0:T(8,128)(2,1)} %collective-permute-done.16.refs_18_), channel_id=1, source_target_pairs={{0,32},{4,36},{32,0},{36,4},{8,40},{12,44},{40,8},{44,12},{16,48},... | collective-permute-start | bytes 602120 | tf_op jit(solution)/shard_map/ppermute | solution.py:225
  32.8 1.5 %collective-permute-start.17 = (bf16[784,128]{1,0:T(8,128)(2,1)S(1)}, bf16[784,128]{1,0:T(8,128)(2,1)}, u32[]{:S(2)}, u32[]{:S(2)}) collective-permute-start(bf16[784,128]{1,0:T(8,128)(2,1)S(1)} %collective-permute-done.15.refs_17_), channel_id=1, source_target_pairs={{0,56},{4,60},{32,8},{36,12},{8,32},{12,36},{40,16},{44,20},{16,40... | collective-permute-start | bytes 602120 | tf_op jit(solution)/shard_map/ppermute | solution.py:225
  35.6 1.5 %collective-permute-start.11 = (bf16[784,128]{1,0:T(8,128)(2,1)S(1)}, bf16[784,128]{1,0:T(8,128)(2,1)}, u32[]{:S(2)}, u32[]{:S(2)}) collective-permute-start(bf16[784,128]{1,0:T(8,128)(2,1)S(1)} %collective-permute-done.9.refs_11_), channel_id=1, source_target_pairs={{0,32},{4,36},{32,0},{36,4},{8,40},{12,44},{40,8},{44,12},{16,48},... | collective-permute-start | bytes 602120 | tf_op jit(solution)/shard_map/ppermute | solution.py:225
  37.1 3.2 %collective-permute-done.17.refs_19_ = bf16[784,128]{1,0:T(8,128)(2,1)} collective-permute-done((bf16[784,128]{1,0:T(8,128)(2,1)S(1)}, bf16[784,128]{1,0:T(8,128)(2,1)}, u32[]{:S(2)}, u32[]{:S(2)}) %collective-permute-start.17) | collective-permute-done | bytes 200736 | tf_op jit(solution)/shard_map/ppermute | solution.py:225
  40.3 1.4 %collective-permute-start.20 = (bf16[784,128]{1,0:T(8,128)(2,1)S(1)}, bf16[784,128]{1,0:T(8,128)(2,1)}, u32[]{:S(2)}, u32[]{:S(2)}) collective-permute-start(bf16[784,128]{1,0:T(8,128)(2,1)S(1)} %collective-permute-done.18.refs_20_), channel_id=1, source_target_pairs={{0,56},{4,60},{32,8},{36,12},{8,32},{12,36},{40,16},{44,20},{16,40... | collective-permute-start | bytes 602120 | tf_op jit(solution)/shard_map/ppermute | solution.py:225
  42.1 1.1 %collective-permute-start.14 = (bf16[784,128]{1,0:T(8,128)(2,1)}, bf16[784,128]{1,0:T(8,128)(2,1)}, u32[]{:S(2)}, u32[]{:S(2)}) collective-permute-start(bf16[784,128]{1,0:T(8,128)(2,1)} %copy-done.1), channel_id=1, source_target_pairs={{0,4},{4,0},{1,5},{5,1},{2,6},{6,2},{3,7},{7,3},{8,12},{12,8},{9,1... | collective-permute-start | bytes 602120 | tf_op jit(solution)/shard_map/ppermute | solution.py:241
  43.3 3.6 %collective-permute-done.20.refs_22_ = bf16[784,128]{1,0:T(8,128)(2,1)} collective-permute-done((bf16[784,128]{1,0:T(8,128)(2,1)S(1)}, bf16[784,128]{1,0:T(8,128)(2,1)}, u32[]{:S(2)}, u32[]{:S(2)}) %collective-permute-start.20) | collective-permute-done | bytes 200736 | tf_op jit(solution)/shard_map/ppermute | solution.py:225
  46.9 1.4 %collective-permute-start.12 = (bf16[784,128]{1,0:T(8,128)(2,1)}, bf16[784,128]{1,0:T(8,128)(2,1)}, u32[]{:S(2)}, u32[]{:S(2)}) collective-permute-start(bf16[784,128]{1,0:T(8,128)(2,1)} %collective-permute-done.10.refs_12_), channel_id=1, source_target_pairs={{0,56},{4,60},{32,8},{36,12},{8,32},{12,36},{40,16},{44,20},{16,40... | collective-permute-start | bytes 602120 | tf_op jit(solution)/shard_map/ppermute | solution.py:225
  48.3 1.5 %collective-permute-start.13 = (bf16[784,128]{1,0:T(8,128)(2,1)}, bf16[784,128]{1,0:T(8,128)(2,1)}, u32[]{:S(2)}, u32[]{:S(2)}) collective-permute-start(bf16[784,128]{1,0:T(8,128)(2,1)} %collective-permute-done.11.refs_13_), channel_id=1, source_target_pairs={{0,56},{4,60},{32,8},{36,12},{8,32},{12,36},{40,16},{44,20},{16,40... | collective-permute-start | bytes 602120 | tf_op jit(solution)/shard_map/ppermute | solution.py:225
  51.3 1.7 %collective-permute-done.12.refs_14_ = bf16[784,128]{1,0:T(8,128)(2,1)} collective-permute-done((bf16[784,128]{1,0:T(8,128)(2,1)}, bf16[784,128]{1,0:T(8,128)(2,1)}, u32[]{:S(2)}, u32[]{:S(2)}) %collective-permute-start.12) | collective-permute-done | bytes 200736 | tf_op jit(solution)/shard_map/ppermute | solution.py:225
  53.2 4.0 %collective-permute-done.13.refs_15_ = bf16[784,128]{1,0:T(8,128)(2,1)} collective-permute-done((bf16[784,128]{1,0:T(8,128)(2,1)}, bf16[784,128]{1,0:T(8,128)(2,1)}, u32[]{:S(2)}, u32[]{:S(2)}) %collective-permute-start.13) | collective-permute-done | bytes 200736 | tf_op jit(solution)/shard_map/ppermute | solution.py:225
  57.2 4.7 %shard_map.30 = bf16[8,4,3,2,32,128]{5,4,3,2,1,0:T(8,128)(2,1)S(1)} custom-call(s32[32,128]{1,0:T(8,128)S(1)} %shard_map.29.columns_in, bf16[1552,128]{1,0:T(8,128)(2,1)S(1)} %get-tuple-element.18.refs_0_, bf16[1552,128]{1,0:T(8,128)(2,1)S(1)} %collective-permute-done.refs_1_, bf16[1552,128]{1,0:T(8,128)(2,1)S(1)} %collective-permute-done.1.refs_2_, ...), custom_call_target="tpu_custom_call" | custom-call | tf_op jit(solution)/shard_map/pallas_call | solution.py:270
  61.9 35.5 %all_to_all.5 = bf16[32,3,2,32,128]{4,3,2,1,0:T(8,128)(2,1)S(1)} all-to-all(bf16[32,3,2,32,128]{4,3,2,1,0:T(8,128)(2,1)S(1)} %bitcast.14), channel_id=1, replica_groups=mesh['y'=4,'z_lo'=2,'z_hi'=4,'core'=2,'x'=4] {'y','core','x'}, dimensions={0} | all-to-all | bytes 3145728 | tf_op jit(solution)/shard_map/all_to_all | solution.py:285
  97.3 0.9 shard_map.31
  (45 shorter events, 5.3 us)
Async XLA Ops:
  1.7 12.3 %collective-permute-start.8 = (bf16[784,128]{1,0:T(8,128)(2,1)S(1)}, bf16[784,128]{1,0:T(8,128)(2,1)S(1)}, u32[]{:S(2)}, u32[]{:S(2)}) collective-permute-start(bf16[784,128]{1,0:T(8,128)(2,1)S(1)} %get-tuple-element.9.refs_8_), channel_id=1, source_target_pairs={{0,56},{4,60},{32,8},{36,12},{8,32},{12,36},{40,16},{44,20},{16,40... | collective-permute-start | bytes 602120 | tf_op jit(solution)/shard_map/ppermute | solution.py:225
  8.2 7.6 %collective-permute-start.7 = (bf16[784,128]{1,0:T(8,128)(2,1)S(1)}, bf16[784,128]{1,0:T(8,128)(2,1)S(1)}, u32[]{:S(2)}, u32[]{:S(2)}) collective-permute-start(bf16[784,128]{1,0:T(8,128)(2,1)S(1)} %get-tuple-element.9.refs_8_), channel_id=1, source_target_pairs={{0,32},{4,36},{32,0},{36,4},{8,40},{12,44},{40,8},{44,12},{16,48},... | collective-permute-start | bytes 602120 | tf_op jit(solution)/shard_map/ppermute | solution.py:225
  8.2 9.8 %collective-permute-start.16 = (bf16[784,128]{1,0:T(8,128)(2,1)S(1)}, bf16[784,128]{1,0:T(8,128)(2,1)}, u32[]{:S(2)}, u32[]{:S(2)}) collective-permute-start(bf16[784,128]{1,0:T(8,128)(2,1)S(1)} %get-tuple-element.10), channel_id=1, source_target_pairs={{0,60},{4,56},{32,12},{36,8},{8,36},{12,32},{40,20},{44,16},{16,44... | collective-permute-start | bytes 602120 | tf_op jit(solution)/shard_map/ppermute | solution.py:225
  11.1 12.4 %collective-permute-start.2 = (bf16[1552,128]{1,0:T(8,128)(2,1)S(1)}, bf16[1552,128]{1,0:T(8,128)(2,1)S(1)}, u32[]{:S(2)}, u32[]{:S(2)}) collective-permute-start(bf16[1552,128]{1,0:T(8,128)(2,1)S(1)} %get-tuple-element.15), channel_id=1, source_target_pairs={{0,64},{64,128},{128,192},{192,0},{1,65},{65,129},{129,193},{193,1... | collective-permute-start | bytes 1191944 | tf_op jit(solution)/shard_map/ppermute | solution.py:240
  12.5 15.2 %collective-permute-start = (bf16[1552,128]{1,0:T(8,128)(2,1)S(1)}, bf16[1552,128]{1,0:T(8,128)(2,1)S(1)}, u32[]{:S(2)}, u32[]{:S(2)}) collective-permute-start(bf16[1552,128]{1,0:T(8,128)(2,1)S(1)} %get-tuple-element.16), channel_id=1, source_target_pairs={{0,192},{64,0},{128,64},{192,128},{1,193},{65,1},{129,65},{193,129... | collective-permute-start | bytes 1191944 | tf_op jit(solution)/shard_map/ppermute | solution.py:240
  14.0 21.0 %copy-start.3 = (bf16[784,128]{1,0:T(8,128)(2,1)}, bf16[784,128]{1,0:T(8,128)(2,1)S(1)}, u32[]{:S(2)}) copy-start(bf16[784,128]{1,0:T(8,128)(2,1)S(1)} %collective-permute-done.8.refs_10_) | copy-start | bytes 602116
  14.0 18.8 %collective-permute-start.1 = (bf16[1552,128]{1,0:T(8,128)(2,1)S(1)}, bf16[1552,128]{1,0:T(8,128)(2,1)S(1)}, u32[]{:S(2)}, u32[]{:S(2)}) collective-permute-start(bf16[1552,128]{1,0:T(8,128)(2,1)S(1)} %get-tuple-element.17), channel_id=1, source_target_pairs={{0,128},{64,192},{128,0},{192,64},{1,129},{65,193},{129,1},{193,65... | collective-permute-start | bytes 1191944 | tf_op jit(solution)/shard_map/ppermute | solution.py:240
  15.8 6.0 %collective-permute-start.15 = (bf16[784,128]{1,0:T(8,128)(2,1)S(1)}, bf16[784,128]{1,0:T(8,128)(2,1)S(1)}, u32[]{:S(2)}, u32[]{:S(2)}) collective-permute-start(bf16[784,128]{1,0:T(8,128)(2,1)S(1)} %get-tuple-element.10), channel_id=1, source_target_pairs={{0,36},{4,32},{32,4},{36,0},{8,44},{12,40},{40,12},{44,8},{16,52},... | collective-permute-start | bytes 602120 | tf_op jit(solution)/shard_map/ppermute | solution.py:225
  18.0 16.3 %collective-permute-start.3 = (bf16[1552,128]{1,0:T(8,128)(2,1)S(1)}, bf16[1552,128]{1,0:T(8,128)(2,1)S(1)}, u32[]{:S(2)}, u32[]{:S(2)}) collective-permute-start(bf16[1552,128]{1,0:T(8,128)(2,1)S(1)} %get-tuple-element.18.refs_0_), channel_id=1, source_target_pairs={{0,4},{4,0},{1,5},{5,1},{2,6},{6,2},{3,7},{7,3},{8,12},{12,8},{9,1... | collective-permute-start | bytes 1191944 | tf_op jit(solution)/shard_map/ppermute | solution.py:242
  21.8 29.4 %copy-start.5 = (bf16[784,128]{1,0:T(8,128)(2,1)}, bf16[784,128]{1,0:T(8,128)(2,1)S(1)}, u32[]{:S(2)}) copy-start(bf16[784,128]{1,0:T(8,128)(2,1)S(1)} %collective-permute-done.15.refs_17_) | copy-start | bytes 602116
  21.8 13.2 %collective-permute-start.10 = (bf16[784,128]{1,0:T(8,128)(2,1)S(1)}, bf16[784,128]{1,0:T(8,128)(2,1)}, u32[]{:S(2)}, u32[]{:S(2)}) collective-permute-start(bf16[784,128]{1,0:T(8,128)(2,1)S(1)} %collective-permute-done.8.refs_10_), channel_id=1, source_target_pairs={{0,32},{4,36},{32,0},{36,4},{8,40},{12,44},{40,8},{44,12},{16,48},... | collective-permute-start | bytes 602120 | tf_op jit(solution)/shard_map/ppermute | solution.py:225
  23.5 11.6 %collective-permute-start.9 = (bf16[784,128]{1,0:T(8,128)(2,1)S(1)}, bf16[784,128]{1,0:T(8,128)(2,1)S(1)}, u32[]{:S(2)}, u32[]{:S(2)}) collective-permute-start(bf16[784,128]{1,0:T(8,128)(2,1)S(1)} %collective-permute-done.7.refs_9_), channel_id=1, source_target_pairs={{0,56},{4,60},{32,8},{36,12},{8,32},{12,36},{40,16},{44,20},{16,40... | collective-permute-start | bytes 602120 | tf_op jit(solution)/shard_map/ppermute | solution.py:225
  27.6 8.0 %collective-permute-start.18 = (bf16[784,128]{1,0:T(8,128)(2,1)}, bf16[784,128]{1,0:T(8,128)(2,1)S(1)}, u32[]{:S(2)}, u32[]{:S(2)}) collective-permute-start(bf16[784,128]{1,0:T(8,128)(2,1)} %collective-permute-done.16.refs_18_), channel_id=1, source_target_pairs={{0,32},{4,36},{32,0},{36,4},{8,40},{12,44},{40,8},{44,12},{16,48},... | collective-permute-start | bytes 602120 | tf_op jit(solution)/shard_map/ppermute | solution.py:225
  32.8 7.5 %collective-permute-start.17 = (bf16[784,128]{1,0:T(8,128)(2,1)S(1)}, bf16[784,128]{1,0:T(8,128)(2,1)}, u32[]{:S(2)}, u32[]{:S(2)}) collective-permute-start(bf16[784,128]{1,0:T(8,128)(2,1)S(1)} %collective-permute-done.15.refs_17_), channel_id=1, source_target_pairs={{0,56},{4,60},{32,8},{36,12},{8,32},{12,36},{40,16},{44,20},{16,40... | collective-permute-start | bytes 602120 | tf_op jit(solution)/shard_map/ppermute | solution.py:225
  34.3 14.1 %collective-permute-start.6 = (bf16[1552,128]{1,0:T(8,128)(2,1)S(1)}, bf16[1552,128]{1,0:T(8,128)(2,1)S(1)}, u32[]{:S(2)}, u32[]{:S(2)}) collective-permute-start(bf16[1552,128]{1,0:T(8,128)(2,1)S(1)} %collective-permute-done.2.refs_3_), channel_id=1, source_target_pairs={{0,4},{4,0},{1,5},{5,1},{2,6},{6,2},{3,7},{7,3},{8,12},{12,8},{9,1... | collective-permute-start | bytes 1191944 | tf_op jit(solution)/shard_map/ppermute | solution.py:244
  35.0 13.4 %collective-permute-start.4 = (bf16[1552,128]{1,0:T(8,128)(2,1)S(1)}, bf16[1552,128]{1,0:T(8,128)(2,1)S(1)}, u32[]{:S(2)}, u32[]{:S(2)}) collective-permute-start(bf16[1552,128]{1,0:T(8,128)(2,1)S(1)} %collective-permute-done.refs_1_), channel_id=1, source_target_pairs={{0,4},{4,0},{1,5},{5,1},{2,6},{6,2},{3,7},{7,3},{8,12},{12,8},{9,1... | collective-permute-start | bytes 1191944 | tf_op jit(solution)/shard_map/ppermute | solution.py:244
  35.1 14.8 %collective-permute-start.5 = (bf16[1552,128]{1,0:T(8,128)(2,1)S(1)}, bf16[1552,128]{1,0:T(8,128)(2,1)S(1)}, u32[]{:S(2)}, u32[]{:S(2)}) collective-permute-start(bf16[1552,128]{1,0:T(8,128)(2,1)S(1)} %collective-permute-done.1.refs_2_), channel_id=1, source_target_pairs={{0,4},{4,0},{1,5},{5,1},{2,6},{6,2},{3,7},{7,3},{8,12},{12,8},{9,1... | collective-permute-start | bytes 1191944 | tf_op jit(solution)/shard_map/ppermute | solution.py:244
  35.6 6.5 %collective-permute-start.11 = (bf16[784,128]{1,0:T(8,128)(2,1)S(1)}, bf16[784,128]{1,0:T(8,128)(2,1)}, u32[]{:S(2)}, u32[]{:S(2)}) collective-permute-start(bf16[784,128]{1,0:T(8,128)(2,1)S(1)} %collective-permute-done.9.refs_11_), channel_id=1, source_target_pairs={{0,32},{4,36},{32,0},{36,4},{8,40},{12,44},{40,8},{44,12},{16,48},... | collective-permute-start | bytes 602120 | tf_op jit(solution)/shard_map/ppermute | solution.py:225
  40.3 6.6 %collective-permute-start.20 = (bf16[784,128]{1,0:T(8,128)(2,1)S(1)}, bf16[784,128]{1,0:T(8,128)(2,1)}, u32[]{:S(2)}, u32[]{:S(2)}) collective-permute-start(bf16[784,128]{1,0:T(8,128)(2,1)S(1)} %collective-permute-done.18.refs_20_), channel_id=1, source_target_pairs={{0,56},{4,60},{32,8},{36,12},{8,32},{12,36},{40,16},{44,20},{16,40... | collective-permute-start | bytes 602120 | tf_op jit(solution)/shard_map/ppermute | solution.py:225
  42.1 9.1 %collective-permute-start.14 = (bf16[784,128]{1,0:T(8,128)(2,1)}, bf16[784,128]{1,0:T(8,128)(2,1)}, u32[]{:S(2)}, u32[]{:S(2)}) collective-permute-start(bf16[784,128]{1,0:T(8,128)(2,1)} %copy-done.1), channel_id=1, source_target_pairs={{0,4},{4,0},{1,5},{5,1},{2,6},{6,2},{3,7},{7,3},{8,12},{12,8},{9,1... | collective-permute-start | bytes 602120 | tf_op jit(solution)/shard_map/ppermute | solution.py:241
  46.9 6.1 %collective-permute-start.12 = (bf16[784,128]{1,0:T(8,128)(2,1)}, bf16[784,128]{1,0:T(8,128)(2,1)}, u32[]{:S(2)}, u32[]{:S(2)}) collective-permute-start(bf16[784,128]{1,0:T(8,128)(2,1)} %collective-permute-done.10.refs_12_), channel_id=1, source_target_pairs={{0,56},{4,60},{32,8},{36,12},{8,32},{12,36},{40,16},{44,20},{16,40... | collective-permute-start | bytes 602120 | tf_op jit(solution)/shard_map/ppermute | solution.py:225
  48.3 4.9 %collective-permute-start.19 = (bf16[784,128]{1,0:T(8,128)(2,1)}, bf16[784,128]{1,0:T(8,128)(2,1)}, u32[]{:S(2)}, u32[]{:S(2)}) collective-permute-start(bf16[784,128]{1,0:T(8,128)(2,1)} %collective-permute-done.17.refs_19_), channel_id=1, source_target_pairs={{0,32},{4,36},{32,0},{36,4},{8,40},{12,44},{40,8},{44,12},{16,48},... | collective-permute-start | bytes 602120 | tf_op jit(solution)/shard_map/ppermute | solution.py:225
  48.3 8.8 %collective-permute-start.13 = (bf16[784,128]{1,0:T(8,128)(2,1)}, bf16[784,128]{1,0:T(8,128)(2,1)}, u32[]{:S(2)}, u32[]{:S(2)}) collective-permute-start(bf16[784,128]{1,0:T(8,128)(2,1)} %collective-permute-done.11.refs_13_), channel_id=1, source_target_pairs={{0,56},{4,60},{32,8},{36,12},{8,32},{12,36},{40,16},{44,20},{16,40... | collective-permute-start | bytes 602120 | tf_op jit(solution)/shard_map/ppermute | solution.py:225
  49.9 7.3 %collective-permute-start.21 = (bf16[784,128]{1,0:T(8,128)(2,1)}, bf16[784,128]{1,0:T(8,128)(2,1)}, u32[]{:S(2)}, u32[]{:S(2)}) collective-permute-start(bf16[784,128]{1,0:T(8,128)(2,1)} %collective-permute-done.20.refs_22_), channel_id=1, source_target_pairs={{0,32},{4,36},{32,0},{36,4},{8,40},{12,44},{40,8},{44,12},{16,48},... | collective-permute-start | bytes 602120 | tf_op jit(solution)/shard_map/ppermute | solution.py:225
  (6 other events, 82.5 us)

commit v4 on v3

--- a/solution.py
+++ b/solution.py
@@ -104,10 +104,10 @@
         return total
 
 
-def first_payloads(places, columns, tiles, own, other, left_tail, held, arrived, listed):
+def first_payloads(place, columns, tiles, own, other, left_tail, held, arrived, listed):
     rows, groups, slots, tb, _ = tiles.shape
     copies = [
-        pltpu.make_async_copy(tiles.at[row, places[g], slot], out.at[pl.ds((row * slots + slot) * tb, tb)], arrived)
+        pltpu.make_async_copy(tiles.at[row, place[4 + g], slot], out.at[pl.ds((row * slots + slot) * tb, tb)], arrived)
         for g, out in enumerate((own, other))
         for row in range(rows)
         for slot in range(slots)
@@ -122,7 +122,7 @@
     numbers = [held[row].astype(jnp.float32) for row in range(rows)]
     for g, out in enumerate((own, other)):
         tail = jnp.zeros((TAIL, tb), jnp.float32)
-        chosen = lax.broadcasted_iota(jnp.int32, (slots, groups), 1) == places[g]
+        chosen = lax.broadcasted_iota(jnp.int32, (slots, groups), 1) == place[4 + g]
         for row in range(rows):
             of_group = jnp.sum(jnp.where(chosen, numbers[row], 0.0), axis=1, keepdims=True)
             for slot in range(slots):
@@ -140,6 +140,19 @@
         copy.wait()
 
 
+def left_payloads(n_y, place, tiles, left_tail, *outs):
+    rows, groups, slots, tb, _ = tiles.shape
+    per_y = groups // n_y
+    for step, out in enumerate(outs):
+        to_y = lax.rem(place[1] + step, n_y)
+        for row in range(rows):
+            for g in range(per_y):
+                for slot in range(slots):
+                    at = ((row * per_y + g) * slots + slot) * tb
+                    out[pl.ds(at, tb), :] = tiles[row, to_y * per_y + g, slot]
+        out[pl.ds(rows * per_y * slots * tb, TAIL), :] = left_tail[...]
+
+
 def listed_columns(rows, place, *refs):
     left, out = refs[:-1], refs[-1]
     for n in range(4):
@@ -150,22 +163,17 @@
 
 
 def products(n_left, sizes, columns_in, *refs):
-    left, right_in = refs[:n_left], refs[n_left:-6]
-    out, right, right_columns, arrived, columns, listed = refs[-6:]
+    left, right_in = refs[:n_left], refs[n_left:-5]
+    out, right, right_columns, columns, listed = refs[-5:]
     fetch = pltpu.make_async_copy(columns_in, columns, listed)
     fetch.start()
-    copies = [
-        pltpu.make_async_copy(ref, right.at[n], arrived.at[n]) for n, ref in enumerate(right_in)
-    ]
-    for copy in copies:
-        copy.start()
+    tiles_end = right.shape[1]
+    for n, ref in enumerate(right_in):
+        right[n] = ref[pl.ds(0, tiles_end), :]
+        right_columns[pl.ds(n * TAIL, TAIL), :] = ref[pl.ds(tiles_end, TAIL), :].astype(jnp.float32)
     fetch.wait()
     work = Rows(sizes, columns)
     tb = work.tb
-    for n, copy in enumerate(copies):
-        copy.wait()
-        tail = right[n, pl.ds(work.rows * work.slots * tb, TAIL), :]
-        right_columns[pl.ds(n * TAIL, TAIL), :] = tail.astype(jnp.float32)
     quarters, quarter = out.shape[1], out.shape[4]
     for n, row in work.all():
         rounded = work.product(left, right, right_columns, n, row).astype(out.dtype)
@@ -200,19 +208,18 @@
     hbm = pl.BlockSpec(memory_space=pltpu.HBM)
     limit = pltpu.CompilerParams(vmem_limit_bytes=4 * 2**20)
     payload = (rows * slots * tb + TAIL, tb)
+    place = jnp.zeros((6,), jnp.int32)
+    for n, number in enumerate((x, y, z, core, 2 * x + core, 2 * x + 1 - core)):
+        place = jnp.where(lax.iota(jnp.int32, 6) == n, number, place)
     own, other, left_tail = pl.pallas_call(
         first_payloads,
         out_shape=[pltpu.VMEM(shape, jnp.bfloat16) for shape in (payload, payload, (TAIL, tb))],
         in_specs=[smem, hbm, hbm],
         out_specs=[vmem] * 3,
-        scratch_shapes=[
-            pltpu.VMEM((rows, slots, groups), jnp.int32),
-            pltpu.SemaphoreType.DMA,
-            pltpu.SemaphoreType.DMA,
-        ],
+        scratch_shapes=[pltpu.VMEM((rows, slots, groups), jnp.int32), pltpu.SemaphoreType.DMA, pltpu.SemaphoreType.DMA],
         compiler_params=limit,
     )(
-        jnp.stack([2 * x + core, 2 * x + 1 - core]).astype(jnp.int32),
+        place,
         pltpu.with_memory_space_constraint(tile_columns.transpose(0, 2, 1), pltpu.HBM),
         pltpu.with_memory_space_constraint(density_tiles, pltpu.HBM),
     )
@@ -229,15 +236,18 @@
     every = [(flip, chain) for flip in range(2) for chain in range(2)]
     ring(1, every)
 
-    def left_payload(to_y):
-        tiles = lax.dynamic_slice_in_dim(density_tiles, 2 * to_y, 2, 1)
-        return jnp.concatenate([tiles.reshape(-1, tb), left_tail], axis=0)
-
-    left = {(0, 0): lax.optimization_barrier(left_payload(y))}
+    left_payload = (rows * groups // n_y * slots * tb + TAIL, tb)
+    sent = pl.pallas_call(
+        functools.partial(left_payloads, n_y),
+        out_shape=[pltpu.VMEM(left_payload, jnp.bfloat16)] * n_y,
+        in_specs=[smem, vmem, vmem],
+        out_specs=[vmem] * n_y,
+        compiler_params=limit,
+    )(place, *[pltpu.with_memory_space_constraint(a, pltpu.VMEM) for a in (density_tiles, left_tail)])
+    left = {(0, 0): sent[0]}
     for step in (2, 1, 3):
         perm = [(s, (s + step) % n_y) for s in range(n_y)]
-        sent = left_payload((y + step) % n_y)
-        left[0, -step % n_y] = lax.ppermute(sent, "y", perm)
+        left[0, -step % n_y] = lax.ppermute(sent[step], "y", perm)
     right[1, 0, 0] = lax.ppermute(other, "core", cores)
     left[1, 0] = lax.ppermute(left[0, 0], "core", cores)
     for step in range(1, n_y):
@@ -259,23 +269,22 @@
         + [(flip, half, flip)]
     ]
     lefts = [pltpu.with_memory_space_constraint(left[k], pltpu.VMEM) for k in left_keys]
-    rights = [pltpu.with_memory_space_constraint(r, pltpu.HBM) for r in rights]
+    rights = [pltpu.with_memory_space_constraint(r, pltpu.VMEM) for r in rights]
     columns = pl.pallas_call(
         functools.partial(listed_columns, rows),
         out_shape=pltpu.VMEM((2 * n_y * rows + 8, tb), jnp.int32),
         in_specs=[smem] + [vmem] * len(lefts),
         out_specs=vmem,
         compiler_params=limit,
-    )(jnp.stack([x, y, z, core]).astype(jnp.int32), *lefts)
+    )(place, *lefts)
     partial = pl.pallas_call(
         functools.partial(products, len(lefts), sizes),
         out_shape=pltpu.VMEM((2 * n_y, n_x, rows, slots, quarter, tb), jnp.bfloat16),
-        in_specs=[vmem] * (1 + len(lefts)) + [hbm] * len(rights),
+        in_specs=[vmem] * (1 + len(lefts) + len(rights)),
         out_specs=vmem,
         scratch_shapes=[
-            pltpu.VMEM((len(rights), *payload), jnp.bfloat16),
+            pltpu.VMEM((len(rights), payload[0] - TAIL, tb), jnp.bfloat16),
             pltpu.VMEM((len(rights) * TAIL, tb), jnp.float32),
-            pltpu.SemaphoreType.DMA((len(rights),)),
             pltpu.SMEM((2 * n_y * rows + 8, tb), jnp.int32),
             pltpu.SemaphoreType.DMA,
         ],

time: 98.4 us -> 97 us (0.986)
  waiting for transfers between devices: 18.8 us -> 33.5 us
  starting transfers between devices: 35.7 us -> 24.1 us
  blocking collectives: 35.5 us -> 32 us
    ppermute x14, starting transfers between devices: 28.3 us -> 17.3 us  [ring(): held[flip, chain] = lax.ppermute(held[flip, chain], ZC, perm)]
    ppermute x3, waiting for transfers between devices: 0.54 us -> 10.7 us  [on_device(): left[0, -step % n_y] = lax.ppermute(sent[step], 'y', perm)]
    ppermute x14, waiting for transfers between devices: 18.2 us -> 22.8 us  [ring(): held[flip, chain] = lax.ppermute(held[flip, chain], ZC, perm)]
    all_to_all x1, blocking collectives: 35.5 us -> 32 us  [on_device(): lax.all_to_all(partial.reshape(2 * n_y * n_x, rows, slots, quarter, tb),...]
    pallas_call x1, Pallas kernels: 4.7 us -> 3.46 us  [on_device(): pl.pallas_call(functools.partial(products, len(lefts), sizes), out_shape=...]
  transfers between devices with their start and end apart: 22 -> 22, of which waited for: 9 -> 10; matrix products, arithmetic and copies ran while one was open for 0% -> 0% of each run, Pallas kernels for 1% -> 1%
where the time goes in v4:
time: 97 us; the launch traced here: 96.9 us
  waiting for transfers between devices  33.5 us (35%)
  blocking collectives  32 us (33%)
  starting transfers between devices  24.1 us (25%)
  Pallas kernels  7.18 us (7%)
    all_to_all x1, blocking collectives, on_device(): lax.all_to_all(partial.reshape(2 * n_y * n_x, rows, slots, quarter, tb),...  32 us
    ppermute x14, waiting for transfers between devices, ring(): held[flip, chain] = lax.ppermute(held[flip, chain], ZC, perm)  22.8 us
    ppermute x14, starting transfers between devices, ring(): held[flip, chain] = lax.ppermute(held[flip, chain], ZC, perm)  17.3 us
    ppermute x3, waiting for transfers between devices, on_device(): left[0, -step % n_y] = lax.ppermute(sent[step], 'y', perm)  10.7 us
    ppermute x3, starting transfers between devices, on_device(): left[0, -step % n_y] = lax.ppermute(sent[step], 'y', perm)  3.85 us
    pallas_call x1, Pallas kernels, on_device(): pl.pallas_call(functools.partial(products, len(lefts), sizes), out_shape=...  3.46 us
    ppermute x3, starting transfers between devices, on_device(): left[1, step] = lax.ppermute(left[0, step], 'core', cores)  2.11 us
  transfers between devices with their start and end apart: 22, of which 10 were waited for; matrix products, arithmetic and copies ran while one was open for 0% of the time, Pallas kernels for 1%

profile of v4, /device:TPU:1, one launch (start us, length us, event | category | flops | bytes accessed | tf_op | source)
XLA Modules:
  0.0 96.9 jit_solution(7642138582087186899)
XLA Ops:
  0.0 1.6 %shard_map.28 = (bf16[784,128]{1,0:T(8,128)(2,1)S(1)}, bf16[784,128]{1,0:T(8,128)(2,1)S(1)}, bf16[16,128]{1,0:T(8,128)(2,1)S(1)}) custom-call(s32[6]{0:T(128)S(1)} %compare_select_fusion.5.place, s32[3,2,8]{2,1,0:T(2,128)} %bitcast.5, bf16[3,8,2,128,128]{4,3,2,1,0:T(8,128)(2,1)} %tiles.3), custom_call_target="tpu_custom_call" | custom-call | tf_op jit(solution)/shard_map/pallas_call | solution.py:214
  1.6 6.5 %collective-permute-start.8 = (bf16[784,128]{1,0:T(8,128)(2,1)S(1)}, bf16[784,128]{1,0:T(8,128)(2,1)S(1)}, u32[]{:S(2)}, u32[]{:S(2)}) collective-permute-start(bf16[784,128]{1,0:T(8,128)(2,1)S(1)} %get-tuple-element.17.refs_8_), channel_id=1, source_target_pairs={{0,56},{4,60},{32,8},{36,12},{8,32},{12,36},{40,16},{44,20},{16,40... | collective-permute-start | bytes 602120 | tf_op jit(solution)/shard_map/ppermute | solution.py:232
  8.1 2.6 %collective-permute-start.16 = (bf16[784,128]{1,0:T(8,128)(2,1)S(1)}, bf16[784,128]{1,0:T(8,128)(2,1)S(1)}, u32[]{:S(2)}, u32[]{:S(2)}) collective-permute-start(bf16[784,128]{1,0:T(8,128)(2,1)S(1)} %get-tuple-element.18), channel_id=1, source_target_pairs={{0,60},{4,56},{32,12},{36,8},{8,36},{12,32},{40,20},{44,16},{16,44... | collective-permute-start | bytes 602120 | tf_op jit(solution)/shard_map/ppermute | solution.py:232
  11.3 2.8 %collective-permute-start = (bf16[1552,128]{1,0:T(8,128)(2,1)S(1)}, bf16[1552,128]{1,0:T(8,128)(2,1)S(1)}, u32[]{:S(2)}, u32[]{:S(2)}) collective-permute-start(bf16[1552,128]{1,0:T(8,128)(2,1)S(1)} %get-tuple-element.14), channel_id=1, source_target_pairs={{0,192},{64,0},{128,64},{192,128},{1,193},{65,1},{129,65},{193,129... | collective-permute-start | bytes 1191944 | tf_op jit(solution)/shard_map/ppermute | solution.py:250
  16.0 1.6 %collective-permute-done.16.refs_18_ = bf16[784,128]{1,0:T(8,128)(2,1)S(1)} collective-permute-done((bf16[784,128]{1,0:T(8,128)(2,1)S(1)}, bf16[784,128]{1,0:T(8,128)(2,1)S(1)}, u32[]{:S(2)}, u32[]{:S(2)}) %collective-permute-start.16) | collective-permute-done | bytes 200736 | tf_op jit(solution)/shard_map/ppermute | solution.py:232
  17.6 4.6 %collective-permute-done.15.refs_17_ = bf16[784,128]{1,0:T(8,128)(2,1)S(1)} collective-permute-done((bf16[784,128]{1,0:T(8,128)(2,1)S(1)}, bf16[784,128]{1,0:T(8,128)(2,1)S(1)}, u32[]{:S(2)}, u32[]{:S(2)}) %collective-permute-start.15) | collective-permute-done | bytes 200736 | tf_op jit(solution)/shard_map/ppermute | solution.py:232
  23.0 8.4 %collective-permute-done.refs_1_ = bf16[1552,128]{1,0:T(8,128)(2,1)S(1)} collective-permute-done((bf16[1552,128]{1,0:T(8,128)(2,1)S(1)}, bf16[1552,128]{1,0:T(8,128)(2,1)S(1)}, u32[]{:S(2)}, u32[]{:S(2)}) %collective-permute-start) | collective-permute-done | bytes 397344 | tf_op jit(solution)/shard_map/ppermute | solution.py:250
  31.4 1.2 %collective-permute-start.9 = (bf16[784,128]{1,0:T(8,128)(2,1)S(1)}, bf16[784,128]{1,0:T(8,128)(2,1)S(1)}, u32[]{:S(2)}, u32[]{:S(2)}) collective-permute-start(bf16[784,128]{1,0:T(8,128)(2,1)S(1)} %collective-permute-done.7.refs_9_), channel_id=1, source_target_pairs={{0,56},{4,60},{32,8},{36,12},{8,32},{12,36},{40,16},{44,20},{16,40... | collective-permute-start | bytes 602120 | tf_op jit(solution)/shard_map/ppermute | solution.py:232
  33.0 2.3 %collective-permute-done.2.refs_3_ = bf16[1552,128]{1,0:T(8,128)(2,1)S(1)} collective-permute-done((bf16[1552,128]{1,0:T(8,128)(2,1)S(1)}, bf16[1552,128]{1,0:T(8,128)(2,1)S(1)}, u32[]{:S(2)}, u32[]{:S(2)}) %collective-permute-start.2) | collective-permute-done | bytes 397344 | tf_op jit(solution)/shard_map/ppermute | solution.py:250
  35.3 0.9 collective-permute-start.17
  37.1 2.1 %collective-permute-done.9.refs_11_ = bf16[784,128]{1,0:T(8,128)(2,1)S(1)} collective-permute-done((bf16[784,128]{1,0:T(8,128)(2,1)S(1)}, bf16[784,128]{1,0:T(8,128)(2,1)S(1)}, u32[]{:S(2)}, u32[]{:S(2)}) %collective-permute-start.9) | collective-permute-done | bytes 200736 | tf_op jit(solution)/shard_map/ppermute | solution.py:232
  39.2 1.2 %collective-permute-start.6 = (bf16[1552,128]{1,0:T(8,128)(2,1)S(1)}, bf16[1552,128]{1,0:T(8,128)(2,1)S(1)}, u32[]{:S(2)}, u32[]{:S(2)}) collective-permute-start(bf16[1552,128]{1,0:T(8,128)(2,1)S(1)} %collective-permute-done.2.refs_3_), channel_id=1, source_target_pairs={{0,4},{4,0},{1,5},{5,1},{2,6},{6,2},{3,7},{7,3},{8,12},{12,8},{9,1... | collective-permute-start | bytes 1191944 | tf_op jit(solution)/shard_map/ppermute | solution.py:254
  40.4 3.0 %collective-permute-done.17.refs_19_ = bf16[784,128]{1,0:T(8,128)(2,1)S(1)} collective-permute-done((bf16[784,128]{1,0:T(8,128)(2,1)S(1)}, bf16[784,128]{1,0:T(8,128)(2,1)S(1)}, u32[]{:S(2)}, u32[]{:S(2)}) %collective-permute-start.17) | collective-permute-done | bytes 200736 | tf_op jit(solution)/shard_map/ppermute | solution.py:232
  43.4 1.0 %collective-permute-start.20 = (bf16[784,128]{1,0:T(8,128)(2,1)S(1)}, bf16[784,128]{1,0:T(8,128)(2,1)S(1)}, u32[]{:S(2)}, u32[]{:S(2)}) collective-permute-start(bf16[784,128]{1,0:T(8,128)(2,1)S(1)} %collective-permute-done.18.refs_20_), channel_id=1, source_target_pairs={{0,56},{4,60},{32,8},{36,12},{8,32},{12,36},{40,16},{44,20},{16,40... | collective-permute-start | bytes 602120 | tf_op jit(solution)/shard_map/ppermute | solution.py:232
  44.4 2.5 %collective-permute-done.11.refs_13_ = bf16[784,128]{1,0:T(8,128)(2,1)S(1)} collective-permute-done((bf16[784,128]{1,0:T(8,128)(2,1)S(1)}, bf16[784,128]{1,0:T(8,128)(2,1)S(1)}, u32[]{:S(2)}, u32[]{:S(2)}) %collective-permute-start.11) | collective-permute-done | bytes 200736 | tf_op jit(solution)/shard_map/ppermute | solution.py:232
  47.0 0.9 collective-permute-start.14
  47.8 2.4 %collective-permute-done.20.refs_22_ = bf16[784,128]{1,0:T(8,128)(2,1)S(1)} collective-permute-done((bf16[784,128]{1,0:T(8,128)(2,1)S(1)}, bf16[784,128]{1,0:T(8,128)(2,1)S(1)}, u32[]{:S(2)}, u32[]{:S(2)}) %collective-permute-start.20) | collective-permute-done | bytes 200736 | tf_op jit(solution)/shard_map/ppermute | solution.py:232
  50.2 0.9 collective-permute-start.12
  51.1 2.1 %collective-permute-start.13 = (bf16[784,128]{1,0:T(8,128)(2,1)S(1)}, bf16[784,128]{1,0:T(8,128)(2,1)S(1)}, u32[]{:S(2)}, u32[]{:S(2)}) collective-permute-start(bf16[784,128]{1,0:T(8,128)(2,1)S(1)} %collective-permute-done.11.refs_13_), channel_id=1, source_target_pairs={{0,56},{4,60},{32,8},{36,12},{8,32},{12,36},{40,16},{44,20},{16,40... | collective-permute-start | bytes 602120 | tf_op jit(solution)/shard_map/ppermute | solution.py:232
  53.9 2.1 %collective-permute-done.12.refs_14_ = bf16[784,128]{1,0:T(8,128)(2,1)S(1)} collective-permute-done((bf16[784,128]{1,0:T(8,128)(2,1)S(1)}, bf16[784,128]{1,0:T(8,128)(2,1)S(1)}, u32[]{:S(2)}, u32[]{:S(2)}) %collective-permute-start.12) | collective-permute-done | bytes 200736 | tf_op jit(solution)/shard_map/ppermute | solution.py:232
  56.0 4.5 %collective-permute-done.13.refs_15_ = bf16[784,128]{1,0:T(8,128)(2,1)S(1)} collective-permute-done((bf16[784,128]{1,0:T(8,128)(2,1)S(1)}, bf16[784,128]{1,0:T(8,128)(2,1)S(1)}, u32[]{:S(2)}, u32[]{:S(2)}) %collective-permute-start.13) | collective-permute-done | bytes 200736 | tf_op jit(solution)/shard_map/ppermute | solution.py:232
  60.5 3.5 %shard_map.31 = bf16[8,4,3,2,32,128]{5,4,3,2,1,0:T(8,128)(2,1)S(1)} custom-call(s32[32,128]{1,0:T(8,128)S(1)} %shard_map.30.columns_in, bf16[1552,128]{1,0:T(8,128)(2,1)S(1)} %get-tuple-element.13.refs_0_, bf16[1552,128]{1,0:T(8,128)(2,1)S(1)} %collective-permute-done.refs_1_, bf16[1552,128]{1,0:T(8,128)(2,1)S(1)} %collective-permute-done.1.refs_2_, ...), custom_call_target="tpu_custom_call" | custom-call | tf_op jit(solution)/shard_map/pallas_call | solution.py:280
  64.0 32.0 %all_to_all.5 = bf16[32,3,2,32,128]{4,3,2,1,0:T(8,128)(2,1)S(1)} all-to-all(bf16[32,3,2,32,128]{4,3,2,1,0:T(8,128)(2,1)S(1)} %bitcast.4), channel_id=1, replica_groups=mesh['y'=4,'z_lo'=2,'z_hi'=4,'core'=2,'x'=4] {'y','core','x'}, dimensions={0} | all-to-all | bytes 3145728 | tf_op jit(solution)/shard_map/all_to_all | solution.py:294
  96.0 0.9 shard_map.32
  (29 shorter events, 5.3 us)
Async XLA Ops:
  0.0 10.7 %copy-start = (bf16[3,8,2,128,128]{4,3,2,1,0:T(8,128)(2,1)S(1)}, bf16[3,8,2,128,128]{4,3,2,1,0:T(8,128)(2,1)}, u32[]{:S(2)}) copy-start(bf16[3,8,2,128,128]{4,3,2,1,0:T(8,128)(2,1)} %tiles.3) | copy-start | bytes 4718596
  1.6 12.9 %collective-permute-start.8 = (bf16[784,128]{1,0:T(8,128)(2,1)S(1)}, bf16[784,128]{1,0:T(8,128)(2,1)S(1)}, u32[]{:S(2)}, u32[]{:S(2)}) collective-permute-start(bf16[784,128]{1,0:T(8,128)(2,1)S(1)} %get-tuple-element.17.refs_8_), channel_id=1, source_target_pairs={{0,56},{4,60},{32,8},{36,12},{8,32},{12,36},{40,16},{44,20},{16,40... | collective-permute-start | bytes 602120 | tf_op jit(solution)/shard_map/ppermute | solution.py:232
  8.1 7.1 %collective-permute-start.7 = (bf16[784,128]{1,0:T(8,128)(2,1)S(1)}, bf16[784,128]{1,0:T(8,128)(2,1)S(1)}, u32[]{:S(2)}, u32[]{:S(2)}) collective-permute-start(bf16[784,128]{1,0:T(8,128)(2,1)S(1)} %get-tuple-element.17.refs_8_), channel_id=1, source_target_pairs={{0,32},{4,36},{32,0},{36,4},{8,40},{12,44},{40,8},{44,12},{16,48},... | collective-permute-start | bytes 602120 | tf_op jit(solution)/shard_map/ppermute | solution.py:232
  8.1 9.6 %collective-permute-start.16 = (bf16[784,128]{1,0:T(8,128)(2,1)S(1)}, bf16[784,128]{1,0:T(8,128)(2,1)S(1)}, u32[]{:S(2)}, u32[]{:S(2)}) collective-permute-start(bf16[784,128]{1,0:T(8,128)(2,1)S(1)} %get-tuple-element.18), channel_id=1, source_target_pairs={{0,60},{4,56},{32,12},{36,8},{8,36},{12,32},{40,20},{44,16},{16,44... | collective-permute-start | bytes 602120 | tf_op jit(solution)/shard_map/ppermute | solution.py:232
  11.3 20.1 %collective-permute-start = (bf16[1552,128]{1,0:T(8,128)(2,1)S(1)}, bf16[1552,128]{1,0:T(8,128)(2,1)S(1)}, u32[]{:S(2)}, u32[]{:S(2)}) collective-permute-start(bf16[1552,128]{1,0:T(8,128)(2,1)S(1)} %get-tuple-element.14), channel_id=1, source_target_pairs={{0,192},{64,0},{128,64},{192,128},{1,193},{65,1},{129,65},{193,129... | collective-permute-start | bytes 1191944 | tf_op jit(solution)/shard_map/ppermute | solution.py:250
  14.1 18.5 %collective-permute-start.1 = (bf16[1552,128]{1,0:T(8,128)(2,1)S(1)}, bf16[1552,128]{1,0:T(8,128)(2,1)S(1)}, u32[]{:S(2)}, u32[]{:S(2)}) collective-permute-start(bf16[1552,128]{1,0:T(8,128)(2,1)S(1)} %get-tuple-element.15), channel_id=1, source_target_pairs={{0,128},{64,192},{128,0},{192,64},{1,129},{65,193},{129,1},{193,65... | collective-permute-start | bytes 1191944 | tf_op jit(solution)/shard_map/ppermute | solution.py:250
  14.5 20.8 %collective-permute-start.2 = (bf16[1552,128]{1,0:T(8,128)(2,1)S(1)}, bf16[1552,128]{1,0:T(8,128)(2,1)S(1)}, u32[]{:S(2)}, u32[]{:S(2)}) collective-permute-start(bf16[1552,128]{1,0:T(8,128)(2,1)S(1)} %get-tuple-element.16), channel_id=1, source_target_pairs={{0,64},{64,128},{128,192},{192,0},{1,65},{65,129},{129,193},{193,1... | collective-permute-start | bytes 1191944 | tf_op jit(solution)/shard_map/ppermute | solution.py:250
  15.2 7.1 %collective-permute-start.15 = (bf16[784,128]{1,0:T(8,128)(2,1)S(1)}, bf16[784,128]{1,0:T(8,128)(2,1)S(1)}, u32[]{:S(2)}, u32[]{:S(2)}) collective-permute-start(bf16[784,128]{1,0:T(8,128)(2,1)S(1)} %get-tuple-element.18), channel_id=1, source_target_pairs={{0,36},{4,32},{32,4},{36,0},{8,44},{12,40},{40,12},{44,8},{16,52},... | collective-permute-start | bytes 602120 | tf_op jit(solution)/shard_map/ppermute | solution.py:232
  17.6 18.6 %collective-permute-start.3 = (bf16[1552,128]{1,0:T(8,128)(2,1)S(1)}, bf16[1552,128]{1,0:T(8,128)(2,1)S(1)}, u32[]{:S(2)}, u32[]{:S(2)}) collective-permute-start(bf16[1552,128]{1,0:T(8,128)(2,1)S(1)} %get-tuple-element.13.refs_0_), channel_id=1, source_target_pairs={{0,4},{4,0},{1,5},{5,1},{2,6},{6,2},{3,7},{7,3},{8,12},{12,8},{9,1... | collective-permute-start | bytes 1191944 | tf_op jit(solution)/shard_map/ppermute | solution.py:252
  22.2 14.8 %collective-permute-start.10 = (bf16[784,128]{1,0:T(8,128)(2,1)S(1)}, bf16[784,128]{1,0:T(8,128)(2,1)S(1)}, u32[]{:S(2)}, u32[]{:S(2)}) collective-permute-start(bf16[784,128]{1,0:T(8,128)(2,1)S(1)} %collective-permute-done.8.refs_10_), channel_id=1, source_target_pairs={{0,32},{4,36},{32,0},{36,4},{8,40},{12,44},{40,8},{44,12},{16,48},... | collective-permute-start | bytes 602120 | tf_op jit(solution)/shard_map/ppermute | solution.py:232
  31.4 7.8 %collective-permute-start.9 = (bf16[784,128]{1,0:T(8,128)(2,1)S(1)}, bf16[784,128]{1,0:T(8,128)(2,1)S(1)}, u32[]{:S(2)}, u32[]{:S(2)}) collective-permute-start(bf16[784,128]{1,0:T(8,128)(2,1)S(1)} %collective-permute-done.7.refs_9_), channel_id=1, source_target_pairs={{0,56},{4,60},{32,8},{36,12},{8,32},{12,36},{40,16},{44,20},{16,40... | collective-permute-start | bytes 602120 | tf_op jit(solution)/shard_map/ppermute | solution.py:232
  32.6 7.8 %collective-permute-start.18 = (bf16[784,128]{1,0:T(8,128)(2,1)S(1)}, bf16[784,128]{1,0:T(8,128)(2,1)S(1)}, u32[]{:S(2)}, u32[]{:S(2)}) collective-permute-start(bf16[784,128]{1,0:T(8,128)(2,1)S(1)} %collective-permute-done.16.refs_18_), channel_id=1, source_target_pairs={{0,32},{4,36},{32,0},{36,4},{8,40},{12,44},{40,8},{44,12},{16,48},... | collective-permute-start | bytes 602120 | tf_op jit(solution)/shard_map/ppermute | solution.py:232
  35.3 8.1 %collective-permute-start.17 = (bf16[784,128]{1,0:T(8,128)(2,1)S(1)}, bf16[784,128]{1,0:T(8,128)(2,1)S(1)}, u32[]{:S(2)}, u32[]{:S(2)}) collective-permute-start(bf16[784,128]{1,0:T(8,128)(2,1)S(1)} %collective-permute-done.15.refs_17_), channel_id=1, source_target_pairs={{0,56},{4,60},{32,8},{36,12},{8,32},{12,36},{40,16},{44,20},{16,40... | collective-permute-start | bytes 602120 | tf_op jit(solution)/shard_map/ppermute | solution.py:232
  36.2 14.9 %collective-permute-start.4 = (bf16[1552,128]{1,0:T(8,128)(2,1)S(1)}, bf16[1552,128]{1,0:T(8,128)(2,1)S(1)}, u32[]{:S(2)}, u32[]{:S(2)}) collective-permute-start(bf16[1552,128]{1,0:T(8,128)(2,1)S(1)} %collective-permute-done.refs_1_), channel_id=1, source_target_pairs={{0,4},{4,0},{1,5},{5,1},{2,6},{6,2},{3,7},{7,3},{8,12},{12,8},{9,1... | collective-permute-start | bytes 1191944 | tf_op jit(solution)/shard_map/ppermute | solution.py:254
  37.0 14.1 %collective-permute-start.5 = (bf16[1552,128]{1,0:T(8,128)(2,1)S(1)}, bf16[1552,128]{1,0:T(8,128)(2,1)S(1)}, u32[]{:S(2)}, u32[]{:S(2)}) collective-permute-start(bf16[1552,128]{1,0:T(8,128)(2,1)S(1)} %collective-permute-done.1.refs_2_), channel_id=1, source_target_pairs={{0,4},{4,0},{1,5},{5,1},{2,6},{6,2},{3,7},{7,3},{8,12},{12,8},{9,1... | collective-permute-start | bytes 1191944 | tf_op jit(solution)/shard_map/ppermute | solution.py:254
  39.2 14.0 %collective-permute-start.6 = (bf16[1552,128]{1,0:T(8,128)(2,1)S(1)}, bf16[1552,128]{1,0:T(8,128)(2,1)S(1)}, u32[]{:S(2)}, u32[]{:S(2)}) collective-permute-start(bf16[1552,128]{1,0:T(8,128)(2,1)S(1)} %collective-permute-done.2.refs_3_), channel_id=1, source_target_pairs={{0,4},{4,0},{1,5},{5,1},{2,6},{6,2},{3,7},{7,3},{8,12},{12,8},{9,1... | collective-permute-start | bytes 1191944 | tf_op jit(solution)/shard_map/ppermute | solution.py:254
  40.4 6.5 %collective-permute-start.11 = (bf16[784,128]{1,0:T(8,128)(2,1)S(1)}, bf16[784,128]{1,0:T(8,128)(2,1)S(1)}, u32[]{:S(2)}, u32[]{:S(2)}) collective-permute-start(bf16[784,128]{1,0:T(8,128)(2,1)S(1)} %collective-permute-done.9.refs_11_), channel_id=1, source_target_pairs={{0,32},{4,36},{32,0},{36,4},{8,40},{12,44},{40,8},{44,12},{16,48},... | collective-permute-start | bytes 602120 | tf_op jit(solution)/shard_map/ppermute | solution.py:232
  43.4 6.8 %collective-permute-start.20 = (bf16[784,128]{1,0:T(8,128)(2,1)S(1)}, bf16[784,128]{1,0:T(8,128)(2,1)S(1)}, u32[]{:S(2)}, u32[]{:S(2)}) collective-permute-start(bf16[784,128]{1,0:T(8,128)(2,1)S(1)} %collective-permute-done.18.refs_20_), channel_id=1, source_target_pairs={{0,56},{4,60},{32,8},{36,12},{8,32},{12,36},{40,16},{44,20},{16,40... | collective-permute-start | bytes 602120 | tf_op jit(solution)/shard_map/ppermute | solution.py:232
  47.0 6.9 %collective-permute-start.14 = (bf16[784,128]{1,0:T(8,128)(2,1)S(1)}, bf16[784,128]{1,0:T(8,128)(2,1)S(1)}, u32[]{:S(2)}, u32[]{:S(2)}) collective-permute-start(bf16[784,128]{1,0:T(8,128)(2,1)S(1)} %get-tuple-element.18), channel_id=1, source_target_pairs={{0,4},{4,0},{1,5},{5,1},{2,6},{6,2},{3,7},{7,3},{8,12},{12,8},{9,1... | collective-permute-start | bytes 602120 | tf_op jit(solution)/shard_map/ppermute | solution.py:251
  50.2 5.8 %collective-permute-start.12 = (bf16[784,128]{1,0:T(8,128)(2,1)S(1)}, bf16[784,128]{1,0:T(8,128)(2,1)S(1)}, u32[]{:S(2)}, u32[]{:S(2)}) collective-permute-start(bf16[784,128]{1,0:T(8,128)(2,1)S(1)} %collective-permute-done.10.refs_12_), channel_id=1, source_target_pairs={{0,56},{4,60},{32,8},{36,12},{8,32},{12,36},{40,16},{44,20},{16,40... | collective-permute-start | bytes 602120 | tf_op jit(solution)/shard_map/ppermute | solution.py:232
  51.1 4.9 %collective-permute-start.19 = (bf16[784,128]{1,0:T(8,128)(2,1)S(1)}, bf16[784,128]{1,0:T(8,128)(2,1)S(1)}, u32[]{:S(2)}, u32[]{:S(2)}) collective-permute-start(bf16[784,128]{1,0:T(8,128)(2,1)S(1)} %collective-permute-done.17.refs_19_), channel_id=1, source_target_pairs={{0,32},{4,36},{32,0},{36,4},{8,40},{12,44},{40,8},{44,12},{16,48},... | collective-permute-start | bytes 602120 | tf_op jit(solution)/shard_map/ppermute | solution.py:232
  51.1 9.4 %collective-permute-start.13 = (bf16[784,128]{1,0:T(8,128)(2,1)S(1)}, bf16[784,128]{1,0:T(8,128)(2,1)S(1)}, u32[]{:S(2)}, u32[]{:S(2)}) collective-permute-start(bf16[784,128]{1,0:T(8,128)(2,1)S(1)} %collective-permute-done.11.refs_13_), channel_id=1, source_target_pairs={{0,56},{4,60},{32,8},{36,12},{8,32},{12,36},{40,16},{44,20},{16,40... | collective-permute-start | bytes 602120 | tf_op jit(solution)/shard_map/ppermute | solution.py:232
  53.2 7.3 %collective-permute-start.21 = (bf16[784,128]{1,0:T(8,128)(2,1)S(1)}, bf16[784,128]{1,0:T(8,128)(2,1)S(1)}, u32[]{:S(2)}, u32[]{:S(2)}) collective-permute-start(bf16[784,128]{1,0:T(8,128)(2,1)S(1)} %collective-permute-done.20.refs_22_), channel_id=1, source_target_pairs={{0,32},{4,36},{32,0},{36,4},{8,40},{12,44},{40,8},{44,12},{16,48},... | collective-permute-start | bytes 602120 | tf_op jit(solution)/shard_map/ppermute | solution.py:232

commit v5 on v4

--- a/solution.py
+++ b/solution.py
@@ -11,7 +11,7 @@
 
 ROWS_COLS = ("y", "z_lo", "z_hi", "core")
 ZC = ("z_lo", "z_hi", "core")
-TAIL = 16
+TAIL = 8
 NO_TARGET = -3
 
 
@@ -168,9 +168,13 @@
     fetch = pltpu.make_async_copy(columns_in, columns, listed)
     fetch.start()
     tiles_end = right.shape[1]
-    for n, ref in enumerate(right_in):
+    for n, ref in enumerate(right_in[:-2]):
         right[n] = ref[pl.ds(0, tiles_end), :]
         right_columns[pl.ds(n * TAIL, TAIL), :] = ref[pl.ds(tiles_end, TAIL), :].astype(jnp.float32)
+    n, (top, bottom), cut = len(right_in) - 2, right_in[-2:], tiles_end // 2
+    right[n, pl.ds(0, cut), :] = top[...]
+    right[n, pl.ds(cut, cut), :] = bottom[pl.ds(0, cut), :]
+    right_columns[pl.ds(n * TAIL, TAIL), :] = bottom[pl.ds(cut, TAIL), :].astype(jnp.float32)
     fetch.wait()
     work = Rows(sizes, columns)
     tb = work.tb
@@ -255,7 +259,12 @@
 
     for step in range(2, half):
         ring(step, every)
-    ring(half, [(0, 0), (1, 1)])
+    ring(half, [(0, 0)])
+    cut = rows * slots * tb // 2
+    far = []
+    parts = held[1, 0][:cut], held[1, 1][cut:]
+    for chain, part in enumerate(parts):
+        far.append(lax.ppermute(part, ZC, z_pairs((chain + half - 1) % 2, 0, n_hi, n_lo)))
 
     left_keys = [(flip, step) for flip in range(2) for step in range(n_y)]
     sizes = (rows, slots, n_y, n_lo, n_hi, tb)
@@ -266,8 +275,8 @@
         for flip in range(2)
         for key in [(flip, 0, 0)]
         + [(flip, step, chain) for step in range(1, half) for chain in range(2)]
-        + [(flip, half, flip)]
-    ]
+        + ([(flip, half, flip)] if flip == 0 else [])
+    ] + far
     lefts = [pltpu.with_memory_space_constraint(left[k], pltpu.VMEM) for k in left_keys]
     rights = [pltpu.with_memory_space_constraint(r, pltpu.VMEM) for r in rights]
     columns = pl.pallas_call(
@@ -283,8 +292,8 @@
         in_specs=[vmem] * (1 + len(lefts) + len(rights)),
         out_specs=vmem,
         scratch_shapes=[
-            pltpu.VMEM((len(rights), payload[0] - TAIL, tb), jnp.bfloat16),
-            pltpu.VMEM((len(rights) * TAIL, tb), jnp.float32),
+            pltpu.VMEM((2 * n_z, payload[0] - TAIL, tb), jnp.bfloat16),
+            pltpu.VMEM((2 * n_z * TAIL, tb), jnp.float32),
             pltpu.SMEM((2 * n_y * rows + 8, tb), jnp.int32),
             pltpu.SemaphoreType.DMA,
         ],

time: 97 us -> 102 us (1.052)
  starting transfers between devices: 24.1 us -> 28.1 us
    ppermute x14 -> x13, waiting for transfers between devices: 22.8 us -> 14.6 us  [ring(): held[flip, chain] = lax.ppermute(held[flip, chain], ZC, perm)]
    ppermute x0 -> x2, waiting for transfers between devices: none -> 6.63 us  [on_device(): lax.ppermute(part, ZC, z_pairs((chain + half - 1) % 2, 0, n_hi, n_lo))]
    ppermute x0 -> x2, starting transfers between devices: none -> 1.74 us  [on_device(): lax.ppermute(part, ZC, z_pairs((chain + half - 1) % 2, 0, n_hi, n_lo))]
    ppermute x3, starting transfers between devices: 2.11 us -> 3.58 us  [on_device(): left[1, step] = lax.ppermute(left[0, step], 'core', cores)]
    ppermute x3, waiting for transfers between devices: 10.7 us -> 12.1 us  [on_device(): left[0, -step % n_y] = lax.ppermute(sent[step], 'y', perm)]
    ppermute x14 -> x13, starting transfers between devices: 17.3 us -> 17.7 us  [ring(): held[flip, chain] = lax.ppermute(held[flip, chain], ZC, perm)]
  transfers between devices with their start and end apart: 22 -> 23, of which waited for: 10 -> 11; matrix products, arithmetic and copies ran while one was open for 0% -> 0% of each run, Pallas kernels for 1% -> 1%
where the time goes in v5:
time: 102 us; the launch traced here: 101 us
  waiting for transfers between devices  33.4 us (33%)
  blocking collectives  32.7 us (32%)
  starting transfers between devices  28.1 us (28%)
  Pallas kernels  7.19 us (7%)
    all_to_all x1, blocking collectives, on_device(): lax.all_to_all(partial.reshape(2 * n_y * n_x, rows, slots, quarter, tb),...  32.7 us
    ppermute x13, starting transfers between devices, ring(): held[flip, chain] = lax.ppermute(held[flip, chain], ZC, perm)  17.7 us
    ppermute x13, waiting for transfers between devices, ring(): held[flip, chain] = lax.ppermute(held[flip, chain], ZC, perm)  14.6 us
    ppermute x3, waiting for transfers between devices, on_device(): left[0, -step % n_y] = lax.ppermute(sent[step], 'y', perm)  12.1 us
    ppermute x2, waiting for transfers between devices, on_device(): lax.ppermute(part, ZC, z_pairs((chain + half - 1) % 2, 0, n_hi, n_lo))  6.63 us
    ppermute x3, starting transfers between devices, on_device(): left[0, -step % n_y] = lax.ppermute(sent[step], 'y', perm)  3.85 us
    ppermute x3, starting transfers between devices, on_device(): left[1, step] = lax.ppermute(left[0, step], 'core', cores)  3.58 us
    pallas_call x1, Pallas kernels, on_device(): pl.pallas_call(functools.partial(products, len(lefts), sizes), out_shape=...  3.47 us
  transfers between devices with their start and end apart: 23, of which 11 were waited for; matrix products, arithmetic and copies ran while one was open for 0% of the time, Pallas kernels for 1%

profile of v5, /device:TPU:1, one launch (start us, length us, event | category | flops | bytes accessed | tf_op | source)
XLA Modules:
  0.0 101.5 jit_solution(18157439787720857107)
XLA Ops:
  0.0 1.6 %shard_map.28 = (bf16[776,128]{1,0:T(8,128)(2,1)S(1)}, bf16[776,128]{1,0:T(8,128)(2,1)S(1)}, bf16[8,128]{1,0:T(8,128)(2,1)S(1)}) custom-call(s32[6]{0:T(128)S(1)} %compare_select_fusion.5.place, s32[3,2,8]{2,1,0:T(2,128)} %bitcast.5, bf16[3,8,2,128,128]{4,3,2,1,0:T(8,128)(2,1)} %tiles.3), custom_call_target="tpu_custom_call" | custom-call | tf_op jit(solution)/shard_map/pallas_call | solution.py:218
  1.6 6.5 %collective-permute-start.8 = (bf16[776,128]{1,0:T(8,128)(2,1)S(1)}, bf16[776,128]{1,0:T(8,128)(2,1)S(1)}, u32[]{:S(2)}, u32[]{:S(2)}) collective-permute-start(bf16[776,128]{1,0:T(8,128)(2,1)S(1)} %get-tuple-element.17.refs_8_), channel_id=1, source_target_pairs={{0,56},{4,60},{32,8},{36,12},{8,32},{12,36},{40,16},{44,20},{16,40... | collective-permute-start | bytes 595976 | tf_op jit(solution)/shard_map/ppermute | solution.py:236
  8.1 2.6 %collective-permute-start.16 = (bf16[776,128]{1,0:T(8,128)(2,1)S(1)}, bf16[776,128]{1,0:T(8,128)(2,1)S(1)}, u32[]{:S(2)}, u32[]{:S(2)}) collective-permute-start(bf16[776,128]{1,0:T(8,128)(2,1)S(1)} %get-tuple-element.18), channel_id=1, source_target_pairs={{0,60},{4,56},{32,12},{36,8},{8,36},{12,32},{40,20},{44,16},{16,44... | collective-permute-start | bytes 595976 | tf_op jit(solution)/shard_map/ppermute | solution.py:236
  11.3 2.8 %collective-permute-start = (bf16[1544,128]{1,0:T(8,128)(2,1)S(1)}, bf16[1544,128]{1,0:T(8,128)(2,1)S(1)}, u32[]{:S(2)}, u32[]{:S(2)}) collective-permute-start(bf16[1544,128]{1,0:T(8,128)(2,1)S(1)} %get-tuple-element.14), channel_id=1, source_target_pairs={{0,192},{64,0},{128,64},{192,128},{1,193},{65,1},{129,65},{193,129... | collective-permute-start | bytes 1185800 | tf_op jit(solution)/shard_map/ppermute | solution.py:254
  15.8 1.8 %collective-permute-done.16.refs_18_ = bf16[776,128]{1,0:T(8,128)(2,1)S(1)} collective-permute-done((bf16[776,128]{1,0:T(8,128)(2,1)S(1)}, bf16[776,128]{1,0:T(8,128)(2,1)S(1)}, u32[]{:S(2)}, u32[]{:S(2)}) %collective-permute-start.16) | collective-permute-done | bytes 198688 | tf_op jit(solution)/shard_map/ppermute | solution.py:236
  17.6 4.0 %collective-permute-done.15.refs_17_ = bf16[776,128]{1,0:T(8,128)(2,1)S(1)} collective-permute-done((bf16[776,128]{1,0:T(8,128)(2,1)S(1)}, bf16[776,128]{1,0:T(8,128)(2,1)S(1)}, u32[]{:S(2)}, u32[]{:S(2)}) %collective-permute-start.15) | collective-permute-done | bytes 198688 | tf_op jit(solution)/shard_map/ppermute | solution.py:236
  21.6 9.7 %collective-permute-done.refs_1_ = bf16[1544,128]{1,0:T(8,128)(2,1)S(1)} collective-permute-done((bf16[1544,128]{1,0:T(8,128)(2,1)S(1)}, bf16[1544,128]{1,0:T(8,128)(2,1)S(1)}, u32[]{:S(2)}, u32[]{:S(2)}) %collective-permute-start) | collective-permute-done | bytes 395296 | tf_op jit(solution)/shard_map/ppermute | solution.py:254
  32.8 2.4 %collective-permute-done.2.refs_3_ = bf16[1544,128]{1,0:T(8,128)(2,1)S(1)} collective-permute-done((bf16[1544,128]{1,0:T(8,128)(2,1)S(1)}, bf16[1544,128]{1,0:T(8,128)(2,1)S(1)}, u32[]{:S(2)}, u32[]{:S(2)}) %collective-permute-start.2) | collective-permute-done | bytes 395296 | tf_op jit(solution)/shard_map/ppermute | solution.py:254
  35.2 0.9 collective-permute-start.17
  36.7 1.0 %collective-permute-start.4 = (bf16[1544,128]{1,0:T(8,128)(2,1)S(1)}, bf16[1544,128]{1,0:T(8,128)(2,1)S(1)}, u32[]{:S(2)}, u32[]{:S(2)}) collective-permute-start(bf16[1544,128]{1,0:T(8,128)(2,1)S(1)} %collective-permute-done.refs_1_), channel_id=1, source_target_pairs={{0,4},{4,0},{1,5},{5,1},{2,6},{6,2},{3,7},{7,3},{8,12},{12,8},{9,1... | collective-permute-start | bytes 1185800 | tf_op jit(solution)/shard_map/ppermute | solution.py:258
  37.8 1.3 %collective-permute-start.5 = (bf16[1544,128]{1,0:T(8,128)(2,1)S(1)}, bf16[1544,128]{1,0:T(8,128)(2,1)S(1)}, u32[]{:S(2)}, u32[]{:S(2)}) collective-permute-start(bf16[1544,128]{1,0:T(8,128)(2,1)S(1)} %collective-permute-done.1.refs_2_), channel_id=1, source_target_pairs={{0,4},{4,0},{1,5},{5,1},{2,6},{6,2},{3,7},{7,3},{8,12},{12,8},{9,1... | collective-permute-start | bytes 1185800 | tf_op jit(solution)/shard_map/ppermute | solution.py:258
  39.1 3.0 %collective-permute-done.18.refs_20_ = bf16[776,128]{1,0:T(8,128)(2,1)S(1)} collective-permute-done((bf16[776,128]{1,0:T(8,128)(2,1)S(1)}, bf16[776,128]{1,0:T(8,128)(2,1)S(1)}, u32[]{:S(2)}, u32[]{:S(2)}) %collective-permute-start.18) | collective-permute-done | bytes 198688 | tf_op jit(solution)/shard_map/ppermute | solution.py:236
  42.1 1.3 %collective-permute-start.6 = (bf16[1544,128]{1,0:T(8,128)(2,1)S(1)}, bf16[1544,128]{1,0:T(8,128)(2,1)S(1)}, u32[]{:S(2)}, u32[]{:S(2)}) collective-permute-start(bf16[1544,128]{1,0:T(8,128)(2,1)S(1)} %collective-permute-done.2.refs_3_), channel_id=1, source_target_pairs={{0,4},{4,0},{1,5},{5,1},{2,6},{6,2},{3,7},{7,3},{8,12},{12,8},{9,1... | collective-permute-start | bytes 1185800 | tf_op jit(solution)/shard_map/ppermute | solution.py:258
  43.4 1.6 %collective-permute-start.20 = (bf16[776,128]{1,0:T(8,128)(2,1)S(1)}, bf16[776,128]{1,0:T(8,128)(2,1)S(1)}, u32[]{:S(2)}, u32[]{:S(2)}) collective-permute-start(bf16[776,128]{1,0:T(8,128)(2,1)S(1)} %collective-permute-done.18.refs_20_), channel_id=1, source_target_pairs={{0,56},{4,60},{32,8},{36,12},{8,32},{12,36},{40,16},{44,20},{16,40... | collective-permute-start | bytes 595976 | tf_op jit(solution)/shard_map/ppermute | solution.py:236
  45.0 1.3 %collective-permute-done.11.refs_13_ = bf16[776,128]{1,0:T(8,128)(2,1)S(1)} collective-permute-done((bf16[776,128]{1,0:T(8,128)(2,1)S(1)}, bf16[776,128]{1,0:T(8,128)(2,1)S(1)}, u32[]{:S(2)}, u32[]{:S(2)}) %collective-permute-start.11) | collective-permute-done | bytes 198688 | tf_op jit(solution)/shard_map/ppermute | solution.py:236
  47.1 3.6 %collective-permute-done.20.refs_22_ = bf16[776,128]{1,0:T(8,128)(2,1)S(1)} collective-permute-done((bf16[776,128]{1,0:T(8,128)(2,1)S(1)}, bf16[776,128]{1,0:T(8,128)(2,1)S(1)}, u32[]{:S(2)}, u32[]{:S(2)}) %collective-permute-start.20) | collective-permute-done | bytes 198688 | tf_op jit(solution)/shard_map/ppermute | solution.py:236
  50.7 1.2 %collective-permute-start.14 = (bf16[776,128]{1,0:T(8,128)(2,1)S(1)}, bf16[776,128]{1,0:T(8,128)(2,1)S(1)}, u32[]{:S(2)}, u32[]{:S(2)}) collective-permute-start(bf16[776,128]{1,0:T(8,128)(2,1)S(1)} %get-tuple-element.18), channel_id=1, source_target_pairs={{0,4},{4,0},{1,5},{5,1},{2,6},{6,2},{3,7},{7,3},{8,12},{12,8},{9,1... | collective-permute-start | bytes 595976 | tf_op jit(solution)/shard_map/ppermute | solution.py:255
  52.0 1.6 %collective-permute-start.12 = (bf16[776,128]{1,0:T(8,128)(2,1)S(1)}, bf16[776,128]{1,0:T(8,128)(2,1)S(1)}, u32[]{:S(2)}, u32[]{:S(2)}) collective-permute-start(bf16[776,128]{1,0:T(8,128)(2,1)S(1)} %collective-permute-done.10.refs_12_), channel_id=1, source_target_pairs={{0,56},{4,60},{32,8},{36,12},{8,32},{12,36},{40,16},{44,20},{16,40... | collective-permute-start | bytes 595976 | tf_op jit(solution)/shard_map/ppermute | solution.py:236
  53.6 1.1 %collective-permute-start.13 = (bf16[776,128]{1,0:T(8,128)(2,1)S(1)}, bf16[776,128]{1,0:T(8,128)(2,1)S(1)}, u32[]{:S(2)}, u32[]{:S(2)}) collective-permute-start(bf16[776,128]{1,0:T(8,128)(2,1)S(1)} %collective-permute-done.11.refs_13_), channel_id=1, source_target_pairs={{0,56},{4,60},{32,8},{36,12},{8,32},{12,36},{40,16},{44,20},{16,40... | collective-permute-start | bytes 595976 | tf_op jit(solution)/shard_map/ppermute | solution.py:236
  54.9 1.7 %collective-permute-start.21 = (bf16[384,128]{1,0:T(8,128)(2,1)S(1)}, bf16[384,128]{1,0:T(8,128)(2,1)S(1)}, u32[]{:S(2)}, u32[]{:S(2)}) collective-permute-start(bf16[384,128]{1,0:T(8,128)(2,1)S(1)} %slice.8), channel_id=1, source_target_pairs={{0,56},{4,60},{32,8},{36,12},{8,32},{12,36},{40,16},{44,20},{16,40... | collective-permute-start | bytes 294920 | tf_op jit(solution)/shard_map/ppermute | solution.py:267
  57.8 6.6 %collective-permute-done.21.refs_23_ = bf16[384,128]{1,0:T(8,128)(2,1)S(1)} collective-permute-done((bf16[384,128]{1,0:T(8,128)(2,1)S(1)}, bf16[384,128]{1,0:T(8,128)(2,1)S(1)}, u32[]{:S(2)}, u32[]{:S(2)}) %collective-permute-start.21) | collective-permute-done | bytes 98336 | tf_op jit(solution)/shard_map/ppermute | solution.py:267
  64.4 3.5 %shard_map.31 = bf16[8,4,3,2,32,128]{5,4,3,2,1,0:T(8,128)(2,1)S(1)} custom-call(s32[32,128]{1,0:T(8,128)S(1)} %shard_map.30.columns_in, bf16[1544,128]{1,0:T(8,128)(2,1)S(1)} %get-tuple-element.13.refs_0_, bf16[1544,128]{1,0:T(8,128)(2,1)S(1)} %collective-permute-done.refs_1_, bf16[1544,128]{1,0:T(8,128)(2,1)S(1)} %collective-permute-done.1.refs_2_, ...), custom_call_target="tpu_custom_call" | custom-call | tf_op jit(solution)/shard_map/pallas_call | solution.py:289
  67.9 32.7 %all_to_all.5 = bf16[32,3,2,32,128]{4,3,2,1,0:T(8,128)(2,1)S(1)} all-to-all(bf16[32,3,2,32,128]{4,3,2,1,0:T(8,128)(2,1)S(1)} %bitcast.4), channel_id=1, replica_groups=mesh['y'=4,'z_lo'=2,'z_hi'=4,'core'=2,'x'=4] {'y','core','x'}, dimensions={0} | all-to-all | bytes 3145728 | tf_op jit(solution)/shard_map/all_to_all | solution.py:303
  100.6 0.9 shard_map.32
  (33 shorter events, 6.7 us)
Async XLA Ops:
  0.0 10.7 %copy-start = (bf16[3,8,2,128,128]{4,3,2,1,0:T(8,128)(2,1)S(1)}, bf16[3,8,2,128,128]{4,3,2,1,0:T(8,128)(2,1)}, u32[]{:S(2)}) copy-start(bf16[3,8,2,128,128]{4,3,2,1,0:T(8,128)(2,1)} %tiles.3) | copy-start | bytes 4718596
  1.6 12.9 %collective-permute-start.8 = (bf16[776,128]{1,0:T(8,128)(2,1)S(1)}, bf16[776,128]{1,0:T(8,128)(2,1)S(1)}, u32[]{:S(2)}, u32[]{:S(2)}) collective-permute-start(bf16[776,128]{1,0:T(8,128)(2,1)S(1)} %get-tuple-element.17.refs_8_), channel_id=1, source_target_pairs={{0,56},{4,60},{32,8},{36,12},{8,32},{12,36},{40,16},{44,20},{16,40... | collective-permute-start | bytes 595976 | tf_op jit(solution)/shard_map/ppermute | solution.py:236
  8.1 7.0 %collective-permute-start.7 = (bf16[776,128]{1,0:T(8,128)(2,1)S(1)}, bf16[776,128]{1,0:T(8,128)(2,1)S(1)}, u32[]{:S(2)}, u32[]{:S(2)}) collective-permute-start(bf16[776,128]{1,0:T(8,128)(2,1)S(1)} %get-tuple-element.17.refs_8_), channel_id=1, source_target_pairs={{0,32},{4,36},{32,0},{36,4},{8,40},{12,44},{40,8},{44,12},{16,48},... | collective-permute-start | bytes 595976 | tf_op jit(solution)/shard_map/ppermute | solution.py:236
  8.1 9.5 %collective-permute-start.16 = (bf16[776,128]{1,0:T(8,128)(2,1)S(1)}, bf16[776,128]{1,0:T(8,128)(2,1)S(1)}, u32[]{:S(2)}, u32[]{:S(2)}) collective-permute-start(bf16[776,128]{1,0:T(8,128)(2,1)S(1)} %get-tuple-element.18), channel_id=1, source_target_pairs={{0,60},{4,56},{32,12},{36,8},{8,36},{12,32},{40,20},{44,16},{16,44... | collective-permute-start | bytes 595976 | tf_op jit(solution)/shard_map/ppermute | solution.py:236
  11.3 20.0 %collective-permute-start = (bf16[1544,128]{1,0:T(8,128)(2,1)S(1)}, bf16[1544,128]{1,0:T(8,128)(2,1)S(1)}, u32[]{:S(2)}, u32[]{:S(2)}) collective-permute-start(bf16[1544,128]{1,0:T(8,128)(2,1)S(1)} %get-tuple-element.14), channel_id=1, source_target_pairs={{0,192},{64,0},{128,64},{192,128},{1,193},{65,1},{129,65},{193,129... | collective-permute-start | bytes 1185800 | tf_op jit(solution)/shard_map/ppermute | solution.py:254
  14.1 18.1 %collective-permute-start.1 = (bf16[1544,128]{1,0:T(8,128)(2,1)S(1)}, bf16[1544,128]{1,0:T(8,128)(2,1)S(1)}, u32[]{:S(2)}, u32[]{:S(2)}) collective-permute-start(bf16[1544,128]{1,0:T(8,128)(2,1)S(1)} %get-tuple-element.15), channel_id=1, source_target_pairs={{0,128},{64,192},{128,0},{192,64},{1,129},{65,193},{129,1},{193,65... | collective-permute-start | bytes 1185800 | tf_op jit(solution)/shard_map/ppermute | solution.py:254
  14.5 7.1 %collective-permute-start.15 = (bf16[776,128]{1,0:T(8,128)(2,1)S(1)}, bf16[776,128]{1,0:T(8,128)(2,1)S(1)}, u32[]{:S(2)}, u32[]{:S(2)}) collective-permute-start(bf16[776,128]{1,0:T(8,128)(2,1)S(1)} %get-tuple-element.18), channel_id=1, source_target_pairs={{0,36},{4,32},{32,4},{36,0},{8,44},{12,40},{40,12},{44,8},{16,52},... | collective-permute-start | bytes 595976 | tf_op jit(solution)/shard_map/ppermute | solution.py:236
  15.1 20.1 %collective-permute-start.2 = (bf16[1544,128]{1,0:T(8,128)(2,1)S(1)}, bf16[1544,128]{1,0:T(8,128)(2,1)S(1)}, u32[]{:S(2)}, u32[]{:S(2)}) collective-permute-start(bf16[1544,128]{1,0:T(8,128)(2,1)S(1)} %get-tuple-element.16), channel_id=1, source_target_pairs={{0,64},{64,128},{128,192},{192,0},{1,65},{65,129},{129,193},{193,1... | collective-permute-start | bytes 1185800 | tf_op jit(solution)/shard_map/ppermute | solution.py:254
  17.6 19.2 %collective-permute-start.3 = (bf16[1544,128]{1,0:T(8,128)(2,1)S(1)}, bf16[1544,128]{1,0:T(8,128)(2,1)S(1)}, u32[]{:S(2)}, u32[]{:S(2)}) collective-permute-start(bf16[1544,128]{1,0:T(8,128)(2,1)S(1)} %get-tuple-element.13.refs_0_), channel_id=1, source_target_pairs={{0,4},{4,0},{1,5},{5,1},{2,6},{6,2},{3,7},{7,3},{8,12},{12,8},{9,1... | collective-permute-start | bytes 1185800 | tf_op jit(solution)/shard_map/ppermute | solution.py:256
  21.6 14.6 %collective-permute-start.9 = (bf16[776,128]{1,0:T(8,128)(2,1)S(1)}, bf16[776,128]{1,0:T(8,128)(2,1)S(1)}, u32[]{:S(2)}, u32[]{:S(2)}) collective-permute-start(bf16[776,128]{1,0:T(8,128)(2,1)S(1)} %collective-permute-done.7.refs_9_), channel_id=1, source_target_pairs={{0,56},{4,60},{32,8},{36,12},{8,32},{12,36},{40,16},{44,20},{16,40... | collective-permute-start | bytes 595976 | tf_op jit(solution)/shard_map/ppermute | solution.py:236
  31.3 6.5 %collective-permute-start.10 = (bf16[776,128]{1,0:T(8,128)(2,1)S(1)}, bf16[776,128]{1,0:T(8,128)(2,1)S(1)}, u32[]{:S(2)}, u32[]{:S(2)}) collective-permute-start(bf16[776,128]{1,0:T(8,128)(2,1)S(1)} %collective-permute-done.8.refs_10_), channel_id=1, source_target_pairs={{0,32},{4,36},{32,0},{36,4},{8,40},{12,44},{40,8},{44,12},{16,48},... | collective-permute-start | bytes 595976 | tf_op jit(solution)/shard_map/ppermute | solution.py:236
  32.2 9.9 %collective-permute-start.18 = (bf16[776,128]{1,0:T(8,128)(2,1)S(1)}, bf16[776,128]{1,0:T(8,128)(2,1)S(1)}, u32[]{:S(2)}, u32[]{:S(2)}) collective-permute-start(bf16[776,128]{1,0:T(8,128)(2,1)S(1)} %collective-permute-done.16.refs_18_), channel_id=1, source_target_pairs={{0,32},{4,36},{32,0},{36,4},{8,40},{12,44},{40,8},{44,12},{16,48},... | collective-permute-start | bytes 595976 | tf_op jit(solution)/shard_map/ppermute | solution.py:236
  35.2 8.2 %collective-permute-start.17 = (bf16[776,128]{1,0:T(8,128)(2,1)S(1)}, bf16[776,128]{1,0:T(8,128)(2,1)S(1)}, u32[]{:S(2)}, u32[]{:S(2)}) collective-permute-start(bf16[776,128]{1,0:T(8,128)(2,1)S(1)} %collective-permute-done.15.refs_17_), channel_id=1, source_target_pairs={{0,56},{4,60},{32,8},{36,12},{8,32},{12,36},{40,16},{44,20},{16,40... | collective-permute-start | bytes 595976 | tf_op jit(solution)/shard_map/ppermute | solution.py:236
  36.1 10.2 %collective-permute-start.11 = (bf16[776,128]{1,0:T(8,128)(2,1)S(1)}, bf16[776,128]{1,0:T(8,128)(2,1)S(1)}, u32[]{:S(2)}, u32[]{:S(2)}) collective-permute-start(bf16[776,128]{1,0:T(8,128)(2,1)S(1)} %collective-permute-done.9.refs_11_), channel_id=1, source_target_pairs={{0,32},{4,36},{32,0},{36,4},{8,40},{12,44},{40,8},{44,12},{16,48},... | collective-permute-start | bytes 595976 | tf_op jit(solution)/shard_map/ppermute | solution.py:236
  36.7 16.9 %collective-permute-start.4 = (bf16[1544,128]{1,0:T(8,128)(2,1)S(1)}, bf16[1544,128]{1,0:T(8,128)(2,1)S(1)}, u32[]{:S(2)}, u32[]{:S(2)}) collective-permute-start(bf16[1544,128]{1,0:T(8,128)(2,1)S(1)} %collective-permute-done.refs_1_), channel_id=1, source_target_pairs={{0,4},{4,0},{1,5},{5,1},{2,6},{6,2},{3,7},{7,3},{8,12},{12,8},{9,1... | collective-permute-start | bytes 1185800 | tf_op jit(solution)/shard_map/ppermute | solution.py:258
  37.8 16.9 %collective-permute-start.5 = (bf16[1544,128]{1,0:T(8,128)(2,1)S(1)}, bf16[1544,128]{1,0:T(8,128)(2,1)S(1)}, u32[]{:S(2)}, u32[]{:S(2)}) collective-permute-start(bf16[1544,128]{1,0:T(8,128)(2,1)S(1)} %collective-permute-done.1.refs_2_), channel_id=1, source_target_pairs={{0,4},{4,0},{1,5},{5,1},{2,6},{6,2},{3,7},{7,3},{8,12},{12,8},{9,1... | collective-permute-start | bytes 1185800 | tf_op jit(solution)/shard_map/ppermute | solution.py:258
  42.1 12.7 %collective-permute-start.6 = (bf16[1544,128]{1,0:T(8,128)(2,1)S(1)}, bf16[1544,128]{1,0:T(8,128)(2,1)S(1)}, u32[]{:S(2)}, u32[]{:S(2)}) collective-permute-start(bf16[1544,128]{1,0:T(8,128)(2,1)S(1)} %collective-permute-done.2.refs_3_), channel_id=1, source_target_pairs={{0,4},{4,0},{1,5},{5,1},{2,6},{6,2},{3,7},{7,3},{8,12},{12,8},{9,1... | collective-permute-start | bytes 1185800 | tf_op jit(solution)/shard_map/ppermute | solution.py:258
  43.4 7.3 %collective-permute-start.20 = (bf16[776,128]{1,0:T(8,128)(2,1)S(1)}, bf16[776,128]{1,0:T(8,128)(2,1)S(1)}, u32[]{:S(2)}, u32[]{:S(2)}) collective-permute-start(bf16[776,128]{1,0:T(8,128)(2,1)S(1)} %collective-permute-done.18.refs_20_), channel_id=1, source_target_pairs={{0,56},{4,60},{32,8},{36,12},{8,32},{12,36},{40,16},{44,20},{16,40... | collective-permute-start | bytes 595976 | tf_op jit(solution)/shard_map/ppermute | solution.py:236
  46.4 5.7 %collective-permute-start.19 = (bf16[776,128]{1,0:T(8,128)(2,1)S(1)}, bf16[776,128]{1,0:T(8,128)(2,1)S(1)}, u32[]{:S(2)}, u32[]{:S(2)}) collective-permute-start(bf16[776,128]{1,0:T(8,128)(2,1)S(1)} %collective-permute-done.17.refs_19_), channel_id=1, source_target_pairs={{0,32},{4,36},{32,0},{36,4},{8,40},{12,44},{40,8},{44,12},{16,48},... | collective-permute-start | bytes 595976 | tf_op jit(solution)/shard_map/ppermute | solution.py:236
  50.7 6.3 %collective-permute-start.14 = (bf16[776,128]{1,0:T(8,128)(2,1)S(1)}, bf16[776,128]{1,0:T(8,128)(2,1)S(1)}, u32[]{:S(2)}, u32[]{:S(2)}) collective-permute-start(bf16[776,128]{1,0:T(8,128)(2,1)S(1)} %get-tuple-element.18), channel_id=1, source_target_pairs={{0,4},{4,0},{1,5},{5,1},{2,6},{6,2},{3,7},{7,3},{8,12},{12,8},{9,1... | collective-permute-start | bytes 595976 | tf_op jit(solution)/shard_map/ppermute | solution.py:255
  52.0 5.8 %collective-permute-start.12 = (bf16[776,128]{1,0:T(8,128)(2,1)S(1)}, bf16[776,128]{1,0:T(8,128)(2,1)S(1)}, u32[]{:S(2)}, u32[]{:S(2)}) collective-permute-start(bf16[776,128]{1,0:T(8,128)(2,1)S(1)} %collective-permute-done.10.refs_12_), channel_id=1, source_target_pairs={{0,56},{4,60},{32,8},{36,12},{8,32},{12,36},{40,16},{44,20},{16,40... | collective-permute-start | bytes 595976 | tf_op jit(solution)/shard_map/ppermute | solution.py:236
  53.6 10.8 %collective-permute-start.13 = (bf16[776,128]{1,0:T(8,128)(2,1)S(1)}, bf16[776,128]{1,0:T(8,128)(2,1)S(1)}, u32[]{:S(2)}, u32[]{:S(2)}) collective-permute-start(bf16[776,128]{1,0:T(8,128)(2,1)S(1)} %collective-permute-done.11.refs_13_), channel_id=1, source_target_pairs={{0,56},{4,60},{32,8},{36,12},{8,32},{12,36},{40,16},{44,20},{16,40... | collective-permute-start | bytes 595976 | tf_op jit(solution)/shard_map/ppermute | solution.py:236
  54.7 9.7 %collective-permute-start.22 = (bf16[392,128]{1,0:T(8,128)(2,1)S(1)}, bf16[392,128]{1,0:T(8,128)(2,1)S(1)}, u32[]{:S(2)}, u32[]{:S(2)}) collective-permute-start(bf16[392,128]{1,0:T(8,128)(2,1)S(1)} %slice.9), channel_id=1, source_target_pairs={{0,32},{4,36},{32,0},{36,4},{8,40},{12,44},{40,8},{44,12},{16,48},... | collective-permute-start | bytes 301064 | tf_op jit(solution)/shard_map/ppermute | solution.py:267
  54.9 9.6 %collective-permute-start.21 = (bf16[384,128]{1,0:T(8,128)(2,1)S(1)}, bf16[384,128]{1,0:T(8,128)(2,1)S(1)}, u32[]{:S(2)}, u32[]{:S(2)}) collective-permute-start(bf16[384,128]{1,0:T(8,128)(2,1)S(1)} %slice.8), channel_id=1, source_target_pairs={{0,56},{4,60},{32,8},{36,12},{8,32},{12,36},{40,16},{44,20},{16,40... | collective-permute-start | bytes 294920 | tf_op jit(solution)/shard_map/ppermute | solution.py:267

commit v6 on v4

--- a/solution.py
+++ b/solution.py
@@ -11,7 +11,7 @@
 
 ROWS_COLS = ("y", "z_lo", "z_hi", "core")
 ZC = ("z_lo", "z_hi", "core")
-TAIL = 16
+TAIL = 8
 NO_TARGET = -3
 
 
@@ -46,8 +46,8 @@
     def __init__(self, sizes, columns):
         self.rows, self.slots, self.n_y, self.n_lo, self.n_hi, self.tb = sizes
         self.columns = columns
-        place = 2 * self.n_y * self.rows
-        self.x, self.y, self.z, self.core = (columns[place + n, 0] for n in range(4))
+        self.x, self.y, self.core = (lax.axis_index(axis) for axis in ("x", "y", "core"))
+        self.z = lax.axis_index("z_hi") * self.n_lo + lax.axis_index("z_lo")
 
     def all(self):
         return [(n, row) for n in range(2 * self.n_y) for row in range(self.rows)]
@@ -104,10 +104,12 @@
         return total
 
 
-def first_payloads(place, columns, tiles, own, other, left_tail, held, arrived, listed):
+def first_payloads(columns, tiles, own, other, left_tail, held, arrived, listed):
     rows, groups, slots, tb, _ = tiles.shape
+    x, core = lax.axis_index("x"), lax.axis_index("core")
+    chosen_groups = (2 * x + core, 2 * x + 1 - core)
     copies = [
-        pltpu.make_async_copy(tiles.at[row, place[4 + g], slot], out.at[pl.ds((row * slots + slot) * tb, tb)], arrived)
+        pltpu.make_async_copy(tiles.at[row, chosen_groups[g], slot], out.at[pl.ds((row * slots + slot) * tb, tb)], arrived)
         for g, out in enumerate((own, other))
         for row in range(rows)
         for slot in range(slots)
@@ -122,7 +124,7 @@
     numbers = [held[row].astype(jnp.float32) for row in range(rows)]
     for g, out in enumerate((own, other)):
         tail = jnp.zeros((TAIL, tb), jnp.float32)
-        chosen = lax.broadcasted_iota(jnp.int32, (slots, groups), 1) == place[4 + g]
+        chosen = lax.broadcasted_iota(jnp.int32, (slots, groups), 1) == chosen_groups[g]
         for row in range(rows):
             of_group = jnp.sum(jnp.where(chosen, numbers[row], 0.0), axis=1, keepdims=True)
             for slot in range(slots):
@@ -140,11 +142,11 @@
         copy.wait()
 
 
-def left_payloads(n_y, place, tiles, left_tail, *outs):
+def left_payloads(n_y, tiles, left_tail, *outs):
     rows, groups, slots, tb, _ = tiles.shape
     per_y = groups // n_y
     for step, out in enumerate(outs):
-        to_y = lax.rem(place[1] + step, n_y)
+        to_y = lax.rem(lax.axis_index("y") + step, n_y)
         for row in range(rows):
             for g in range(per_y):
                 for slot in range(slots):
@@ -153,10 +155,8 @@
         out[pl.ds(rows * per_y * slots * tb, TAIL), :] = left_tail[...]
 
 
-def listed_columns(rows, place, *refs):
+def listed_columns(rows, *refs):
     left, out = refs[:-1], refs[-1]
-    for n in range(4):
-        out[pl.ds(len(left) * rows + n, 1), :] = jnp.full((1, out.shape[1]), place[n], jnp.int32)
     for n, ref in enumerate(left):
         tail = ref[pl.ds(ref.shape[0] - TAIL, TAIL), :].astype(jnp.float32).astype(jnp.int32)
         out[pl.ds(n * rows, rows), :] = tail[:rows]
@@ -200,26 +200,24 @@
     rows, groups, slots, tb, _ = density_tiles.shape
     n_x, n_y, n_lo, n_hi = (lax.axis_size(a) for a in ("x", "y", "z_lo", "z_hi"))
     n_z = n_lo * n_hi
-    x, y, core = lax.axis_index("x"), lax.axis_index("y"), lax.axis_index("core")
-    z = lax.axis_index("z_hi") * n_lo + lax.axis_index("z_lo")
     cores = [(0, 1), (1, 0)]
 
-    smem, vmem = pl.BlockSpec(memory_space=pltpu.SMEM), pl.BlockSpec(memory_space=pltpu.VMEM)
+    vmem = pl.BlockSpec(memory_space=pltpu.VMEM)
     hbm = pl.BlockSpec(memory_space=pltpu.HBM)
     limit = pltpu.CompilerParams(vmem_limit_bytes=4 * 2**20)
     payload = (rows * slots * tb + TAIL, tb)
-    place = jnp.zeros((6,), jnp.int32)
-    for n, number in enumerate((x, y, z, core, 2 * x + core, 2 * x + 1 - core)):
-        place = jnp.where(lax.iota(jnp.int32, 6) == n, number, place)
     own, other, left_tail = pl.pallas_call(
         first_payloads,
         out_shape=[pltpu.VMEM(shape, jnp.bfloat16) for shape in (payload, payload, (TAIL, tb))],
-        in_specs=[smem, hbm, hbm],
+        in_specs=[hbm, hbm],
         out_specs=[vmem] * 3,
-        scratch_shapes=[pltpu.VMEM((rows, slots, groups), jnp.int32), pltpu.SemaphoreType.DMA, pltpu.SemaphoreType.DMA],
+        scratch_shapes=[
+            pltpu.VMEM((rows, slots, groups), jnp.int32),
+            pltpu.SemaphoreType.DMA,
+            pltpu.SemaphoreType.DMA,
+        ],
         compiler_params=limit,
     )(
-        place,
         pltpu.with_memory_space_constraint(tile_columns.transpose(0, 2, 1), pltpu.HBM),
         pltpu.with_memory_space_constraint(density_tiles, pltpu.HBM),
     )
@@ -240,10 +238,10 @@
     sent = pl.pallas_call(
         functools.partial(left_payloads, n_y),
         out_shape=[pltpu.VMEM(left_payload, jnp.bfloat16)] * n_y,
-        in_specs=[smem, vmem, vmem],
+        in_specs=[vmem, vmem],
         out_specs=[vmem] * n_y,
         compiler_params=limit,
-    )(place, *[pltpu.with_memory_space_constraint(a, pltpu.VMEM) for a in (density_tiles, left_tail)])
+    )(*[pltpu.with_memory_space_constraint(a, pltpu.VMEM) for a in (density_tiles, left_tail)])
     left = {(0, 0): sent[0]}
     for step in (2, 1, 3):
         perm = [(s, (s + step) % n_y) for s in range(n_y)]
@@ -272,11 +270,11 @@
     rights = [pltpu.with_memory_space_constraint(r, pltpu.VMEM) for r in rights]
     columns = pl.pallas_call(
         functools.partial(listed_columns, rows),
-        out_shape=pltpu.VMEM((2 * n_y * rows + 8, tb), jnp.int32),
-        in_specs=[smem] + [vmem] * len(lefts),
+        out_shape=pltpu.VMEM((2 * n_y * rows, tb), jnp.int32),
+        in_specs=[vmem] * len(lefts),
         out_specs=vmem,
         compiler_params=limit,
-    )(place, *lefts)
+    )(*lefts)
     partial = pl.pallas_call(
         functools.partial(products, len(lefts), sizes),
         out_shape=pltpu.VMEM((2 * n_y, n_x, rows, slots, quarter, tb), jnp.bfloat16),
@@ -285,7 +283,7 @@
         scratch_shapes=[
             pltpu.VMEM((len(rights), payload[0] - TAIL, tb), jnp.bfloat16),
             pltpu.VMEM((len(rights) * TAIL, tb), jnp.float32),
-            pltpu.SMEM((2 * n_y * rows + 8, tb), jnp.int32),
+            pltpu.SMEM((2 * n_y * rows, tb), jnp.int32),
             pltpu.SemaphoreType.DMA,
         ],
         compiler_params=pltpu.CompilerParams(vmem_limit_bytes=12 * 2**20),

time: 97 us -> 95.7 us (0.987)
  Pallas kernels: 7.18 us -> 5.61 us
  transfers between devices with their start and end apart: 22 -> 22, of which waited for: 10 -> 10; matrix products, arithmetic and copies ran while one was open for 0% -> 0% of each run, Pallas kernels for 1% -> 0%
where the time goes in v6:
time: 95.7 us; the launch traced here: 95.6 us
  waiting for transfers between devices  32.9 us (34%)
  blocking collectives  32.1 us (34%)
  starting transfers between devices  24.9 us (26%)
  Pallas kernels  5.61 us (6%)
    all_to_all x1, blocking collectives, on_device(): lax.all_to_all(partial.reshape(2 * n_y * n_x, rows, slots, quarter, tb),...  32.1 us
    ppermute x14, waiting for transfers between devices, ring(): held[flip, chain] = lax.ppermute(held[flip, chain], ZC, perm)  22.3 us
    ppermute x14, starting transfers between devices, ring(): held[flip, chain] = lax.ppermute(held[flip, chain], ZC, perm)  18.1 us
    ppermute x3, waiting for transfers between devices, on_device(): left[0, -step % n_y] = lax.ppermute(sent[step], 'y', perm)  10.6 us
    ppermute x3, starting transfers between devices, on_device(): left[0, -step % n_y] = lax.ppermute(sent[step], 'y', perm)  3.85 us
    pallas_call x1, Pallas kernels, on_device(): pl.pallas_call(functools.partial(products, len(lefts), sizes), out_shape=...  3.4 us
    ppermute x3, starting transfers between devices, on_device(): left[1, step] = lax.ppermute(left[0, step], 'core', cores)  2.09 us
  transfers between devices with their start and end apart: 22, of which 10 were waited for; matrix products, arithmetic and copies ran while one was open for 0% of the time, Pallas kernels for 0%

profile of v6, /device:TPU:1, one launch (start us, length us, event | category | flops | bytes accessed | tf_op | source)
XLA Modules:
  0.0 95.6 jit_solution(15319926052618855458)
XLA Ops:
  0.0 1.2 %shard_map.28 = (bf16[776,128]{1,0:T(8,128)(2,1)S(1)}, bf16[776,128]{1,0:T(8,128)(2,1)S(1)}, bf16[8,128]{1,0:T(8,128)(2,1)S(1)}) custom-call(s32[3,2,8]{2,1,0:T(2,128)} %bitcast.5, bf16[3,8,2,128,128]{4,3,2,1,0:T(8,128)(2,1)} %tiles.3), custom_call_target="tpu_custom_call" | custom-call | tf_op jit(solution)/shard_map/pallas_call | solution.py:209
  1.2 6.5 %collective-permute-start.8 = (bf16[776,128]{1,0:T(8,128)(2,1)S(1)}, bf16[776,128]{1,0:T(8,128)(2,1)S(1)}, u32[]{:S(2)}, u32[]{:S(2)}) collective-permute-start(bf16[776,128]{1,0:T(8,128)(2,1)S(1)} %get-tuple-element.17.refs_8_), channel_id=1, source_target_pairs={{0,56},{4,60},{32,8},{36,12},{8,32},{12,36},{40,16},{44,20},{16,40... | collective-permute-start | bytes 595976 | tf_op jit(solution)/shard_map/ppermute | solution.py:230
  7.7 2.6 %collective-permute-start.16 = (bf16[776,128]{1,0:T(8,128)(2,1)S(1)}, bf16[776,128]{1,0:T(8,128)(2,1)S(1)}, u32[]{:S(2)}, u32[]{:S(2)}) collective-permute-start(bf16[776,128]{1,0:T(8,128)(2,1)S(1)} %get-tuple-element.18), channel_id=1, source_target_pairs={{0,60},{4,56},{32,12},{36,8},{8,36},{12,32},{40,20},{44,16},{16,44... | collective-permute-start | bytes 595976 | tf_op jit(solution)/shard_map/ppermute | solution.py:230
  10.3 2.8 %collective-permute-start = (bf16[1544,128]{1,0:T(8,128)(2,1)S(1)}, bf16[1544,128]{1,0:T(8,128)(2,1)S(1)}, u32[]{:S(2)}, u32[]{:S(2)}) collective-permute-start(bf16[1544,128]{1,0:T(8,128)(2,1)S(1)} %get-tuple-element.14), channel_id=1, source_target_pairs={{0,192},{64,0},{128,64},{192,128},{1,193},{65,1},{129,65},{193,129... | collective-permute-start | bytes 1185800 | tf_op jit(solution)/shard_map/ppermute | solution.py:248
  15.1 2.4 %collective-permute-done.16.refs_18_ = bf16[776,128]{1,0:T(8,128)(2,1)S(1)} collective-permute-done((bf16[776,128]{1,0:T(8,128)(2,1)S(1)}, bf16[776,128]{1,0:T(8,128)(2,1)S(1)}, u32[]{:S(2)}, u32[]{:S(2)}) %collective-permute-start.16) | collective-permute-done | bytes 198688 | tf_op jit(solution)/shard_map/ppermute | solution.py:230
  17.4 3.3 %collective-permute-done.15.refs_17_ = bf16[776,128]{1,0:T(8,128)(2,1)S(1)} collective-permute-done((bf16[776,128]{1,0:T(8,128)(2,1)S(1)}, bf16[776,128]{1,0:T(8,128)(2,1)S(1)}, u32[]{:S(2)}, u32[]{:S(2)}) %collective-permute-start.15) | collective-permute-done | bytes 198688 | tf_op jit(solution)/shard_map/ppermute | solution.py:230
  20.8 1.3 %collective-permute-start.10 = (bf16[776,128]{1,0:T(8,128)(2,1)S(1)}, bf16[776,128]{1,0:T(8,128)(2,1)S(1)}, u32[]{:S(2)}, u32[]{:S(2)}) collective-permute-start(bf16[776,128]{1,0:T(8,128)(2,1)S(1)} %collective-permute-done.8.refs_10_), channel_id=1, source_target_pairs={{0,32},{4,36},{32,0},{36,4},{8,40},{12,44},{40,8},{44,12},{16,48},... | collective-permute-start | bytes 595976 | tf_op jit(solution)/shard_map/ppermute | solution.py:230
  22.0 8.3 %collective-permute-done.refs_1_ = bf16[1544,128]{1,0:T(8,128)(2,1)S(1)} collective-permute-done((bf16[1544,128]{1,0:T(8,128)(2,1)S(1)}, bf16[1544,128]{1,0:T(8,128)(2,1)S(1)}, u32[]{:S(2)}, u32[]{:S(2)}) %collective-permute-start) | collective-permute-done | bytes 395296 | tf_op jit(solution)/shard_map/ppermute | solution.py:248
  30.3 1.2 %collective-permute-start.9 = (bf16[776,128]{1,0:T(8,128)(2,1)S(1)}, bf16[776,128]{1,0:T(8,128)(2,1)S(1)}, u32[]{:S(2)}, u32[]{:S(2)}) collective-permute-start(bf16[776,128]{1,0:T(8,128)(2,1)S(1)} %collective-permute-done.7.refs_9_), channel_id=1, source_target_pairs={{0,56},{4,60},{32,8},{36,12},{8,32},{12,36},{40,16},{44,20},{16,40... | collective-permute-start | bytes 595976 | tf_op jit(solution)/shard_map/ppermute | solution.py:230
  31.9 2.3 %collective-permute-done.2.refs_3_ = bf16[1544,128]{1,0:T(8,128)(2,1)S(1)} collective-permute-done((bf16[1544,128]{1,0:T(8,128)(2,1)S(1)}, bf16[1544,128]{1,0:T(8,128)(2,1)S(1)}, u32[]{:S(2)}, u32[]{:S(2)}) %collective-permute-start.2) | collective-permute-done | bytes 395296 | tf_op jit(solution)/shard_map/ppermute | solution.py:248
  34.2 0.9 collective-permute-start.17
  36.0 2.0 %collective-permute-done.9.refs_11_ = bf16[776,128]{1,0:T(8,128)(2,1)S(1)} collective-permute-done((bf16[776,128]{1,0:T(8,128)(2,1)S(1)}, bf16[776,128]{1,0:T(8,128)(2,1)S(1)}, u32[]{:S(2)}, u32[]{:S(2)}) %collective-permute-start.9) | collective-permute-done | bytes 198688 | tf_op jit(solution)/shard_map/ppermute | solution.py:230
  38.1 1.2 %collective-permute-start.6 = (bf16[1544,128]{1,0:T(8,128)(2,1)S(1)}, bf16[1544,128]{1,0:T(8,128)(2,1)S(1)}, u32[]{:S(2)}, u32[]{:S(2)}) collective-permute-start(bf16[1544,128]{1,0:T(8,128)(2,1)S(1)} %collective-permute-done.2.refs_3_), channel_id=1, source_target_pairs={{0,4},{4,0},{1,5},{5,1},{2,6},{6,2},{3,7},{7,3},{8,12},{12,8},{9,1... | collective-permute-start | bytes 1185800 | tf_op jit(solution)/shard_map/ppermute | solution.py:252
  39.3 2.9 %collective-permute-done.17.refs_19_ = bf16[776,128]{1,0:T(8,128)(2,1)S(1)} collective-permute-done((bf16[776,128]{1,0:T(8,128)(2,1)S(1)}, bf16[776,128]{1,0:T(8,128)(2,1)S(1)}, u32[]{:S(2)}, u32[]{:S(2)}) %collective-permute-start.17) | collective-permute-done | bytes 198688 | tf_op jit(solution)/shard_map/ppermute | solution.py:230
  42.2 1.1 %collective-permute-start.20 = (bf16[776,128]{1,0:T(8,128)(2,1)S(1)}, bf16[776,128]{1,0:T(8,128)(2,1)S(1)}, u32[]{:S(2)}, u32[]{:S(2)}) collective-permute-start(bf16[776,128]{1,0:T(8,128)(2,1)S(1)} %collective-permute-done.18.refs_20_), channel_id=1, source_target_pairs={{0,56},{4,60},{32,8},{36,12},{8,32},{12,36},{40,16},{44,20},{16,40... | collective-permute-start | bytes 595976 | tf_op jit(solution)/shard_map/ppermute | solution.py:230
  43.3 2.5 %collective-permute-done.11.refs_13_ = bf16[776,128]{1,0:T(8,128)(2,1)S(1)} collective-permute-done((bf16[776,128]{1,0:T(8,128)(2,1)S(1)}, bf16[776,128]{1,0:T(8,128)(2,1)S(1)}, u32[]{:S(2)}, u32[]{:S(2)}) %collective-permute-start.11) | collective-permute-done | bytes 198688 | tf_op jit(solution)/shard_map/ppermute | solution.py:230
  46.7 2.3 %collective-permute-done.20.refs_22_ = bf16[776,128]{1,0:T(8,128)(2,1)S(1)} collective-permute-done((bf16[776,128]{1,0:T(8,128)(2,1)S(1)}, bf16[776,128]{1,0:T(8,128)(2,1)S(1)}, u32[]{:S(2)}, u32[]{:S(2)}) %collective-permute-start.20) | collective-permute-done | bytes 198688 | tf_op jit(solution)/shard_map/ppermute | solution.py:230
  48.9 1.1 %collective-permute-start.12 = (bf16[776,128]{1,0:T(8,128)(2,1)S(1)}, bf16[776,128]{1,0:T(8,128)(2,1)S(1)}, u32[]{:S(2)}, u32[]{:S(2)}) collective-permute-start(bf16[776,128]{1,0:T(8,128)(2,1)S(1)} %collective-permute-done.10.refs_12_), channel_id=1, source_target_pairs={{0,56},{4,60},{32,8},{36,12},{8,32},{12,36},{40,16},{44,20},{16,40... | collective-permute-start | bytes 595976 | tf_op jit(solution)/shard_map/ppermute | solution.py:230
  50.0 1.9 %collective-permute-start.13 = (bf16[776,128]{1,0:T(8,128)(2,1)S(1)}, bf16[776,128]{1,0:T(8,128)(2,1)S(1)}, u32[]{:S(2)}, u32[]{:S(2)}) collective-permute-start(bf16[776,128]{1,0:T(8,128)(2,1)S(1)} %collective-permute-done.11.refs_13_), channel_id=1, source_target_pairs={{0,56},{4,60},{32,8},{36,12},{8,32},{12,36},{40,16},{44,20},{16,40... | collective-permute-start | bytes 595976 | tf_op jit(solution)/shard_map/ppermute | solution.py:230
  52.2 2.5 %collective-permute-done.12.refs_14_ = bf16[776,128]{1,0:T(8,128)(2,1)S(1)} collective-permute-done((bf16[776,128]{1,0:T(8,128)(2,1)S(1)}, bf16[776,128]{1,0:T(8,128)(2,1)S(1)}, u32[]{:S(2)}, u32[]{:S(2)}) %collective-permute-start.12) | collective-permute-done | bytes 198688 | tf_op jit(solution)/shard_map/ppermute | solution.py:230
  54.7 4.4 %collective-permute-done.13.refs_15_ = bf16[776,128]{1,0:T(8,128)(2,1)S(1)} collective-permute-done((bf16[776,128]{1,0:T(8,128)(2,1)S(1)}, bf16[776,128]{1,0:T(8,128)(2,1)S(1)}, u32[]{:S(2)}, u32[]{:S(2)}) %collective-permute-start.13) | collective-permute-done | bytes 198688 | tf_op jit(solution)/shard_map/ppermute | solution.py:230
  59.1 3.4 %shard_map.31 = bf16[8,4,3,2,32,128]{5,4,3,2,1,0:T(8,128)(2,1)S(1)} custom-call(s32[24,128]{1,0:T(8,128)S(1)} %shard_map.30.columns_in, bf16[1544,128]{1,0:T(8,128)(2,1)S(1)} %get-tuple-element.13.refs_0_, bf16[1544,128]{1,0:T(8,128)(2,1)S(1)} %collective-permute-done.refs_1_, bf16[1544,128]{1,0:T(8,128)(2,1)S(1)} %collective-permute-done.1.refs_2_, ...), custom_call_target="tpu_custom_call" | custom-call | tf_op jit(solution)/shard_map/pallas_call | solution.py:278
  62.5 32.1 %all_to_all.5 = bf16[32,3,2,32,128]{4,3,2,1,0:T(8,128)(2,1)S(1)} all-to-all(bf16[32,3,2,32,128]{4,3,2,1,0:T(8,128)(2,1)S(1)} %bitcast.3), channel_id=1, replica_groups=mesh['y'=4,'z_lo'=2,'z_hi'=4,'core'=2,'x'=4] {'y','core','x'}, dimensions={0} | all-to-all | bytes 3145728 | tf_op jit(solution)/shard_map/all_to_all | solution.py:292
  94.6 0.9 shard_map.32
  (28 shorter events, 4.5 us)
Async XLA Ops:
  0.0 10.2 %copy-start = (bf16[3,8,2,128,128]{4,3,2,1,0:T(8,128)(2,1)S(1)}, bf16[3,8,2,128,128]{4,3,2,1,0:T(8,128)(2,1)}, u32[]{:S(2)}) copy-start(bf16[3,8,2,128,128]{4,3,2,1,0:T(8,128)(2,1)} %tiles.3) | copy-start | bytes 4718596
  1.2 12.3 %collective-permute-start.8 = (bf16[776,128]{1,0:T(8,128)(2,1)S(1)}, bf16[776,128]{1,0:T(8,128)(2,1)S(1)}, u32[]{:S(2)}, u32[]{:S(2)}) collective-permute-start(bf16[776,128]{1,0:T(8,128)(2,1)S(1)} %get-tuple-element.17.refs_8_), channel_id=1, source_target_pairs={{0,56},{4,60},{32,8},{36,12},{8,32},{12,36},{40,16},{44,20},{16,40... | collective-permute-start | bytes 595976 | tf_op jit(solution)/shard_map/ppermute | solution.py:230
  7.7 6.5 %collective-permute-start.7 = (bf16[776,128]{1,0:T(8,128)(2,1)S(1)}, bf16[776,128]{1,0:T(8,128)(2,1)S(1)}, u32[]{:S(2)}, u32[]{:S(2)}) collective-permute-start(bf16[776,128]{1,0:T(8,128)(2,1)S(1)} %get-tuple-element.17.refs_8_), channel_id=1, source_target_pairs={{0,32},{4,36},{32,0},{36,4},{8,40},{12,44},{40,8},{44,12},{16,48},... | collective-permute-start | bytes 595976 | tf_op jit(solution)/shard_map/ppermute | solution.py:230
  7.7 9.8 %collective-permute-start.16 = (bf16[776,128]{1,0:T(8,128)(2,1)S(1)}, bf16[776,128]{1,0:T(8,128)(2,1)S(1)}, u32[]{:S(2)}, u32[]{:S(2)}) collective-permute-start(bf16[776,128]{1,0:T(8,128)(2,1)S(1)} %get-tuple-element.18), channel_id=1, source_target_pairs={{0,60},{4,56},{32,12},{36,8},{8,36},{12,32},{40,20},{44,16},{16,44... | collective-permute-start | bytes 595976 | tf_op jit(solution)/shard_map/ppermute | solution.py:230
  10.3 20.0 %collective-permute-start = (bf16[1544,128]{1,0:T(8,128)(2,1)S(1)}, bf16[1544,128]{1,0:T(8,128)(2,1)S(1)}, u32[]{:S(2)}, u32[]{:S(2)}) collective-permute-start(bf16[1544,128]{1,0:T(8,128)(2,1)S(1)} %get-tuple-element.14), channel_id=1, source_target_pairs={{0,192},{64,0},{128,64},{192,128},{1,193},{65,1},{129,65},{193,129... | collective-permute-start | bytes 1185800 | tf_op jit(solution)/shard_map/ppermute | solution.py:248
  13.1 18.4 %collective-permute-start.1 = (bf16[1544,128]{1,0:T(8,128)(2,1)S(1)}, bf16[1544,128]{1,0:T(8,128)(2,1)S(1)}, u32[]{:S(2)}, u32[]{:S(2)}) collective-permute-start(bf16[1544,128]{1,0:T(8,128)(2,1)S(1)} %get-tuple-element.15), channel_id=1, source_target_pairs={{0,128},{64,192},{128,0},{192,64},{1,129},{65,193},{129,1},{193,65... | collective-permute-start | bytes 1185800 | tf_op jit(solution)/shard_map/ppermute | solution.py:248
  13.5 20.7 %collective-permute-start.2 = (bf16[1544,128]{1,0:T(8,128)(2,1)S(1)}, bf16[1544,128]{1,0:T(8,128)(2,1)S(1)}, u32[]{:S(2)}, u32[]{:S(2)}) collective-permute-start(bf16[1544,128]{1,0:T(8,128)(2,1)S(1)} %get-tuple-element.16), channel_id=1, source_target_pairs={{0,64},{64,128},{128,192},{192,0},{1,65},{65,129},{129,193},{193,1... | collective-permute-start | bytes 1185800 | tf_op jit(solution)/shard_map/ppermute | solution.py:248
  14.2 6.6 %collective-permute-start.15 = (bf16[776,128]{1,0:T(8,128)(2,1)S(1)}, bf16[776,128]{1,0:T(8,128)(2,1)S(1)}, u32[]{:S(2)}, u32[]{:S(2)}) collective-permute-start(bf16[776,128]{1,0:T(8,128)(2,1)S(1)} %get-tuple-element.18), channel_id=1, source_target_pairs={{0,36},{4,32},{32,4},{36,0},{8,44},{12,40},{40,12},{44,8},{16,52},... | collective-permute-start | bytes 595976 | tf_op jit(solution)/shard_map/ppermute | solution.py:230
  17.4 17.7 %collective-permute-start.3 = (bf16[1544,128]{1,0:T(8,128)(2,1)S(1)}, bf16[1544,128]{1,0:T(8,128)(2,1)S(1)}, u32[]{:S(2)}, u32[]{:S(2)}) collective-permute-start(bf16[1544,128]{1,0:T(8,128)(2,1)S(1)} %get-tuple-element.13.refs_0_), channel_id=1, source_target_pairs={{0,4},{4,0},{1,5},{5,1},{2,6},{6,2},{3,7},{7,3},{8,12},{12,8},{9,1... | collective-permute-start | bytes 1185800 | tf_op jit(solution)/shard_map/ppermute | solution.py:250
  20.8 15.2 %collective-permute-start.10 = (bf16[776,128]{1,0:T(8,128)(2,1)S(1)}, bf16[776,128]{1,0:T(8,128)(2,1)S(1)}, u32[]{:S(2)}, u32[]{:S(2)}) collective-permute-start(bf16[776,128]{1,0:T(8,128)(2,1)S(1)} %collective-permute-done.8.refs_10_), channel_id=1, source_target_pairs={{0,32},{4,36},{32,0},{36,4},{8,40},{12,44},{40,8},{44,12},{16,48},... | collective-permute-start | bytes 595976 | tf_op jit(solution)/shard_map/ppermute | solution.py:230
  30.3 7.7 %collective-permute-start.9 = (bf16[776,128]{1,0:T(8,128)(2,1)S(1)}, bf16[776,128]{1,0:T(8,128)(2,1)S(1)}, u32[]{:S(2)}, u32[]{:S(2)}) collective-permute-start(bf16[776,128]{1,0:T(8,128)(2,1)S(1)} %collective-permute-done.7.refs_9_), channel_id=1, source_target_pairs={{0,56},{4,60},{32,8},{36,12},{8,32},{12,36},{40,16},{44,20},{16,40... | collective-permute-start | bytes 595976 | tf_op jit(solution)/shard_map/ppermute | solution.py:230
  31.5 7.8 %collective-permute-start.18 = (bf16[776,128]{1,0:T(8,128)(2,1)S(1)}, bf16[776,128]{1,0:T(8,128)(2,1)S(1)}, u32[]{:S(2)}, u32[]{:S(2)}) collective-permute-start(bf16[776,128]{1,0:T(8,128)(2,1)S(1)} %collective-permute-done.16.refs_18_), channel_id=1, source_target_pairs={{0,32},{4,36},{32,0},{36,4},{8,40},{12,44},{40,8},{44,12},{16,48},... | collective-permute-start | bytes 595976 | tf_op jit(solution)/shard_map/ppermute | solution.py:230
  34.2 8.0 %collective-permute-start.17 = (bf16[776,128]{1,0:T(8,128)(2,1)S(1)}, bf16[776,128]{1,0:T(8,128)(2,1)S(1)}, u32[]{:S(2)}, u32[]{:S(2)}) collective-permute-start(bf16[776,128]{1,0:T(8,128)(2,1)S(1)} %collective-permute-done.15.refs_17_), channel_id=1, source_target_pairs={{0,56},{4,60},{32,8},{36,12},{8,32},{12,36},{40,16},{44,20},{16,40... | collective-permute-start | bytes 595976 | tf_op jit(solution)/shard_map/ppermute | solution.py:230
  35.2 14.9 %collective-permute-start.4 = (bf16[1544,128]{1,0:T(8,128)(2,1)S(1)}, bf16[1544,128]{1,0:T(8,128)(2,1)S(1)}, u32[]{:S(2)}, u32[]{:S(2)}) collective-permute-start(bf16[1544,128]{1,0:T(8,128)(2,1)S(1)} %collective-permute-done.refs_1_), channel_id=1, source_target_pairs={{0,4},{4,0},{1,5},{5,1},{2,6},{6,2},{3,7},{7,3},{8,12},{12,8},{9,1... | collective-permute-start | bytes 1185800 | tf_op jit(solution)/shard_map/ppermute | solution.py:252
  35.9 14.1 %collective-permute-start.5 = (bf16[1544,128]{1,0:T(8,128)(2,1)S(1)}, bf16[1544,128]{1,0:T(8,128)(2,1)S(1)}, u32[]{:S(2)}, u32[]{:S(2)}) collective-permute-start(bf16[1544,128]{1,0:T(8,128)(2,1)S(1)} %collective-permute-done.1.refs_2_), channel_id=1, source_target_pairs={{0,4},{4,0},{1,5},{5,1},{2,6},{6,2},{3,7},{7,3},{8,12},{12,8},{9,1... | collective-permute-start | bytes 1185800 | tf_op jit(solution)/shard_map/ppermute | solution.py:252
  38.1 13.8 %collective-permute-start.6 = (bf16[1544,128]{1,0:T(8,128)(2,1)S(1)}, bf16[1544,128]{1,0:T(8,128)(2,1)S(1)}, u32[]{:S(2)}, u32[]{:S(2)}) collective-permute-start(bf16[1544,128]{1,0:T(8,128)(2,1)S(1)} %collective-permute-done.2.refs_3_), channel_id=1, source_target_pairs={{0,4},{4,0},{1,5},{5,1},{2,6},{6,2},{3,7},{7,3},{8,12},{12,8},{9,1... | collective-permute-start | bytes 1185800 | tf_op jit(solution)/shard_map/ppermute | solution.py:252
  39.3 6.5 %collective-permute-start.11 = (bf16[776,128]{1,0:T(8,128)(2,1)S(1)}, bf16[776,128]{1,0:T(8,128)(2,1)S(1)}, u32[]{:S(2)}, u32[]{:S(2)}) collective-permute-start(bf16[776,128]{1,0:T(8,128)(2,1)S(1)} %collective-permute-done.9.refs_11_), channel_id=1, source_target_pairs={{0,32},{4,36},{32,0},{36,4},{8,40},{12,44},{40,8},{44,12},{16,48},... | collective-permute-start | bytes 595976 | tf_op jit(solution)/shard_map/ppermute | solution.py:230
  42.2 6.8 %collective-permute-start.20 = (bf16[776,128]{1,0:T(8,128)(2,1)S(1)}, bf16[776,128]{1,0:T(8,128)(2,1)S(1)}, u32[]{:S(2)}, u32[]{:S(2)}) collective-permute-start(bf16[776,128]{1,0:T(8,128)(2,1)S(1)} %collective-permute-done.18.refs_20_), channel_id=1, source_target_pairs={{0,56},{4,60},{32,8},{36,12},{8,32},{12,36},{40,16},{44,20},{16,40... | collective-permute-start | bytes 595976 | tf_op jit(solution)/shard_map/ppermute | solution.py:230
  45.8 6.4 %collective-permute-start.14 = (bf16[776,128]{1,0:T(8,128)(2,1)S(1)}, bf16[776,128]{1,0:T(8,128)(2,1)S(1)}, u32[]{:S(2)}, u32[]{:S(2)}) collective-permute-start(bf16[776,128]{1,0:T(8,128)(2,1)S(1)} %get-tuple-element.18), channel_id=1, source_target_pairs={{0,4},{4,0},{1,5},{5,1},{2,6},{6,2},{3,7},{7,3},{8,12},{12,8},{9,1... | collective-permute-start | bytes 595976 | tf_op jit(solution)/shard_map/ppermute | solution.py:249
  48.9 5.8 %collective-permute-start.12 = (bf16[776,128]{1,0:T(8,128)(2,1)S(1)}, bf16[776,128]{1,0:T(8,128)(2,1)S(1)}, u32[]{:S(2)}, u32[]{:S(2)}) collective-permute-start(bf16[776,128]{1,0:T(8,128)(2,1)S(1)} %collective-permute-done.10.refs_12_), channel_id=1, source_target_pairs={{0,56},{4,60},{32,8},{36,12},{8,32},{12,36},{40,16},{44,20},{16,40... | collective-permute-start | bytes 595976 | tf_op jit(solution)/shard_map/ppermute | solution.py:230
  50.0 4.7 %collective-permute-start.19 = (bf16[776,128]{1,0:T(8,128)(2,1)S(1)}, bf16[776,128]{1,0:T(8,128)(2,1)S(1)}, u32[]{:S(2)}, u32[]{:S(2)}) collective-permute-start(bf16[776,128]{1,0:T(8,128)(2,1)S(1)} %collective-permute-done.17.refs_19_), channel_id=1, source_target_pairs={{0,32},{4,36},{32,0},{36,4},{8,40},{12,44},{40,8},{44,12},{16,48},... | collective-permute-start | bytes 595976 | tf_op jit(solution)/shard_map/ppermute | solution.py:230
  50.0 9.1 %collective-permute-start.13 = (bf16[776,128]{1,0:T(8,128)(2,1)S(1)}, bf16[776,128]{1,0:T(8,128)(2,1)S(1)}, u32[]{:S(2)}, u32[]{:S(2)}) collective-permute-start(bf16[776,128]{1,0:T(8,128)(2,1)S(1)} %collective-permute-done.11.refs_13_), channel_id=1, source_target_pairs={{0,56},{4,60},{32,8},{36,12},{8,32},{12,36},{40,16},{44,20},{16,40... | collective-permute-start | bytes 595976 | tf_op jit(solution)/shard_map/ppermute | solution.py:230
  51.9 7.2 %collective-permute-start.21 = (bf16[776,128]{1,0:T(8,128)(2,1)S(1)}, bf16[776,128]{1,0:T(8,128)(2,1)S(1)}, u32[]{:S(2)}, u32[]{:S(2)}) collective-permute-start(bf16[776,128]{1,0:T(8,128)(2,1)S(1)} %collective-permute-done.20.refs_22_), channel_id=1, source_target_pairs={{0,32},{4,36},{32,0},{36,4},{8,40},{12,44},{40,8},{44,12},{16,48},... | collective-permute-start | bytes 595976 | tf_op jit(solution)/shard_map/ppermute | solution.py:230

commit v7 on v6

--- a/solution.py
+++ b/solution.py
@@ -155,23 +155,27 @@
         out[pl.ds(rows * per_y * slots * tb, TAIL), :] = left_tail[...]
 
 
-def listed_columns(rows, *refs):
-    left, out = refs[:-1], refs[-1]
+def hold(right, right_columns, n, payload):
+    tiles_end = right.shape[1]
+    right[n] = payload[pl.ds(0, tiles_end), :]
+    right_columns[pl.ds(n * TAIL, TAIL), :] = payload[pl.ds(tiles_end, TAIL), :].astype(jnp.float32)
+
+
+def hold_early(rows, n_left, *refs):
+    left, right_in, (columns, right, right_columns) = refs[:n_left], refs[n_left:-3], refs[-3:]
     for n, ref in enumerate(left):
         tail = ref[pl.ds(ref.shape[0] - TAIL, TAIL), :].astype(jnp.float32).astype(jnp.int32)
-        out[pl.ds(n * rows, rows), :] = tail[:rows]
-
-
-def products(n_left, sizes, columns_in, *refs):
-    left, right_in = refs[:n_left], refs[n_left:-5]
-    out, right, right_columns, columns, listed = refs[-5:]
-    fetch = pltpu.make_async_copy(columns_in, columns, listed)
-    fetch.start()
-    tiles_end = right.shape[1]
+        columns[pl.ds(n * rows, rows), :] = tail[:rows]
+    per_core = len(right_in) // 2
     for n, ref in enumerate(right_in):
-        right[n] = ref[pl.ds(0, tiles_end), :]
-        right_columns[pl.ds(n * TAIL, TAIL), :] = ref[pl.ds(tiles_end, TAIL), :].astype(jnp.float32)
-    fetch.wait()
+        hold(right, right_columns, n + n // per_core, ref)
+
+
+def products(n_left, sizes, columns, *refs):
+    left, last = refs[:n_left], refs[n_left : n_left + 2]
+    out, right, right_columns = refs[-3:]
+    for flip, ref in enumerate(last):
+        hold(right, right_columns, (flip + 1) * right.shape[0] // 2 - 1, ref)
     work = Rows(sizes, columns)
     tb = work.tb
     quarters, quarter = out.shape[1], out.shape[4]
@@ -211,11 +215,7 @@
         out_shape=[pltpu.VMEM(shape, jnp.bfloat16) for shape in (payload, payload, (TAIL, tb))],
         in_specs=[hbm, hbm],
         out_specs=[vmem] * 3,
-        scratch_shapes=[
-            pltpu.VMEM((rows, slots, groups), jnp.int32),
-            pltpu.SemaphoreType.DMA,
-            pltpu.SemaphoreType.DMA,
-        ],
+        scratch_shapes=[pltpu.VMEM((rows, slots, groups), jnp.int32), pltpu.SemaphoreType.DMA, pltpu.SemaphoreType.DMA],
         compiler_params=limit,
     )(
         pltpu.with_memory_space_constraint(tile_columns.transpose(0, 2, 1), pltpu.HBM),
@@ -268,26 +268,28 @@
     ]
     lefts = [pltpu.with_memory_space_constraint(left[k], pltpu.VMEM) for k in left_keys]
     rights = [pltpu.with_memory_space_constraint(r, pltpu.VMEM) for r in rights]
-    columns = pl.pallas_call(
-        functools.partial(listed_columns, rows),
-        out_shape=pltpu.VMEM((2 * n_y * rows, tb), jnp.int32),
-        in_specs=[vmem] * len(lefts),
-        out_specs=vmem,
-        compiler_params=limit,
-    )(*lefts)
-    partial = pl.pallas_call(
+    early, last = rights[: n_z - 1] + rights[n_z:-1], [rights[n_z - 1], rights[-1]]
+    held_shapes = [
+        pltpu.VMEM((2 * n_z, payload[0] - TAIL, tb), jnp.bfloat16),
+        pltpu.VMEM((2 * n_z * TAIL, tb), jnp.float32),
+    ]
+    columns, *kept = pl.pallas_call(
+        functools.partial(hold_early, rows, len(lefts)),
+        out_shape=[jax.ShapeDtypeStruct((2 * n_y * rows, tb), jnp.int32)] + held_shapes,
+        in_specs=[vmem] * (len(lefts) + len(early)),
+        out_specs=[vmem] * 3,
+        compiler_params=limit,
+    )(*lefts, *early)
+    kept = [pltpu.with_memory_space_constraint(k, pltpu.VMEM) for k in kept]
+    operands = [pltpu.with_memory_space_constraint(columns, pltpu.SMEM), *lefts, *last, *kept]
+    partial, _, _ = pl.pallas_call(
         functools.partial(products, len(lefts), sizes),
-        out_shape=pltpu.VMEM((2 * n_y, n_x, rows, slots, quarter, tb), jnp.bfloat16),
-        in_specs=[vmem] * (1 + len(lefts) + len(rights)),
-        out_specs=vmem,
-        scratch_shapes=[
-            pltpu.VMEM((len(rights), payload[0] - TAIL, tb), jnp.bfloat16),
-            pltpu.VMEM((len(rights) * TAIL, tb), jnp.float32),
-            pltpu.SMEM((2 * n_y * rows, tb), jnp.int32),
-            pltpu.SemaphoreType.DMA,
-        ],
-        compiler_params=pltpu.CompilerParams(vmem_limit_bytes=12 * 2**20),
-    )(pltpu.with_memory_space_constraint(columns, pltpu.VMEM), *lefts, *rights)
+        out_shape=[pltpu.VMEM((2 * n_y, n_x, rows, slots, quarter, tb), jnp.bfloat16)] + held_shapes,
+        in_specs=[pl.BlockSpec(memory_space=pltpu.SMEM)] + [vmem] * (len(operands) - 1),
+        out_specs=[vmem] * 3,
+        input_output_aliases={len(operands) - 2: 1, len(operands) - 1: 2},
+        compiler_params=limit,
+    )(*operands)
 
     arrived = lax.all_to_all(
         partial.reshape(2 * n_y * n_x, rows, slots, quarter, tb),

time: 95.7 us -> 95.7 us (level)
  waiting for transfers between devices: 32.9 us -> 26.2 us
  starting transfers between devices: 24.9 us -> 31.3 us
    ppermute x14, waiting for transfers between devices: 22.3 us -> 13 us  [ring(): held[flip, chain] = lax.ppermute(held[flip, chain], ZC, perm)]
    ppermute x3, starting transfers between devices: 3.85 us -> 6.93 us  [on_device(): left[0, -step % n_y] = lax.ppermute(sent[step], 'y', perm)]
    ppermute x3, waiting for transfers between devices: 10.6 us -> 13.2 us  [on_device(): left[0, -step % n_y] = lax.ppermute(sent[step], 'y', perm)]
    ppermute x14, starting transfers between devices: 18.1 us -> 20.2 us  [ring(): held[flip, chain] = lax.ppermute(held[flip, chain], ZC, perm)]
    ppermute x3, starting transfers between devices: 2.09 us -> 3.37 us  [on_device(): left[1, step] = lax.ppermute(left[0, step], 'core', cores)]
  transfers between devices with their start and end apart: 22 -> 22, of which waited for: 10 -> 8; matrix products, arithmetic and copies ran while one was open for 0% -> 0% of each run, Pallas kernels for 0% -> 0%
where the time goes in v7:
time: 95.7 us; the launch traced here: 95.6 us
  blocking collectives  32.1 us (34%)
  starting transfers between devices  31.3 us (33%)
  waiting for transfers between devices  26.2 us (27%)
  Pallas kernels  5.81 us (6%)
    all_to_all x1, blocking collectives, on_device(): lax.all_to_all(partial.reshape(2 * n_y * n_x, rows, slots, quarter, tb),...  32.1 us
    ppermute x14, starting transfers between devices, ring(): held[flip, chain] = lax.ppermute(held[flip, chain], ZC, perm)  20.2 us
    ppermute x3, waiting for transfers between devices, on_device(): left[0, -step % n_y] = lax.ppermute(sent[step], 'y', perm)  13.2 us
    ppermute x14, waiting for transfers between devices, ring(): held[flip, chain] = lax.ppermute(held[flip, chain], ZC, perm)  13 us
    ppermute x3, starting transfers between devices, on_device(): left[0, -step % n_y] = lax.ppermute(sent[step], 'y', perm)  6.93 us
    pallas_call x1, Pallas kernels, on_device(): pl.pallas_call(functools.partial(products, len(lefts), sizes), out_shape=...  3.41 us
    ppermute x3, starting transfers between devices, on_device(): left[1, step] = lax.ppermute(left[0, step], 'core', cores)  3.37 us
  transfers between devices with their start and end apart: 22, of which 8 were waited for; matrix products, arithmetic and copies ran while one was open for 0% of the time, Pallas kernels for 0%

profile of v7, /device:TPU:1, one launch (start us, length us, event | category | flops | bytes accessed | tf_op | source)
XLA Modules:
  0.0 95.6 jit_solution(3665545785632889076)
XLA Ops:
  0.0 1.2 %shard_map.28 = (bf16[776,128]{1,0:T(8,128)(2,1)S(1)}, bf16[776,128]{1,0:T(8,128)(2,1)S(1)}, bf16[8,128]{1,0:T(8,128)(2,1)S(1)}) custom-call(s32[3,2,8]{2,1,0:T(2,128)} %bitcast.5, bf16[3,8,2,128,128]{4,3,2,1,0:T(8,128)(2,1)} %tiles.3), custom_call_target="tpu_custom_call" | custom-call | tf_op jit(solution)/shard_map/pallas_call | solution.py:213
  1.2 6.5 %collective-permute-start.8 = (bf16[776,128]{1,0:T(8,128)(2,1)S(1)}, bf16[776,128]{1,0:T(8,128)(2,1)S(1)}, u32[]{:S(2)}, u32[]{:S(2)}) collective-permute-start(bf16[776,128]{1,0:T(8,128)(2,1)S(1)} %get-tuple-element.21.refs_8_), channel_id=1, source_target_pairs={{0,56},{4,60},{32,8},{36,12},{8,32},{12,36},{40,16},{44,20},{16,40... | collective-permute-start | bytes 595976 | tf_op jit(solution)/shard_map/ppermute | solution.py:230
  7.7 2.6 %collective-permute-start.15 = (bf16[776,128]{1,0:T(8,128)(2,1)S(1)}, bf16[776,128]{1,0:T(8,128)(2,1)S(1)}, u32[]{:S(2)}, u32[]{:S(2)}) collective-permute-start(bf16[776,128]{1,0:T(8,128)(2,1)S(1)} %get-tuple-element.22), channel_id=1, source_target_pairs={{0,60},{4,56},{32,12},{36,8},{8,36},{12,32},{40,20},{44,16},{16,44... | collective-permute-start | bytes 595976 | tf_op jit(solution)/shard_map/ppermute | solution.py:230
  10.3 2.8 %collective-permute-start = (bf16[1544,128]{1,0:T(8,128)(2,1)S(1)}, bf16[1544,128]{1,0:T(8,128)(2,1)S(1)}, u32[]{:S(2)}, u32[]{:S(2)}) collective-permute-start(bf16[1544,128]{1,0:T(8,128)(2,1)S(1)} %get-tuple-element.18), channel_id=1, source_target_pairs={{0,192},{64,0},{128,64},{192,128},{1,193},{65,1},{129,65},{193,129... | collective-permute-start | bytes 1185800 | tf_op jit(solution)/shard_map/ppermute | solution.py:248
  13.4 0.8 collective-permute-start.13
  14.3 2.9 %collective-permute-start.1 = (bf16[1544,128]{1,0:T(8,128)(2,1)S(1)}, bf16[1544,128]{1,0:T(8,128)(2,1)S(1)}, u32[]{:S(2)}, u32[]{:S(2)}) collective-permute-start(bf16[1544,128]{1,0:T(8,128)(2,1)S(1)} %get-tuple-element.19), channel_id=1, source_target_pairs={{0,128},{64,192},{128,0},{192,64},{1,129},{65,193},{129,1},{193,65... | collective-permute-start | bytes 1185800 | tf_op jit(solution)/shard_map/ppermute | solution.py:248
  17.2 1.2 %collective-permute-start.2 = (bf16[1544,128]{1,0:T(8,128)(2,1)S(1)}, bf16[1544,128]{1,0:T(8,128)(2,1)S(1)}, u32[]{:S(2)}, u32[]{:S(2)}) collective-permute-start(bf16[1544,128]{1,0:T(8,128)(2,1)S(1)} %get-tuple-element.20), channel_id=1, source_target_pairs={{0,64},{64,128},{128,192},{192,0},{1,65},{65,129},{129,193},{193,1... | collective-permute-start | bytes 1185800 | tf_op jit(solution)/shard_map/ppermute | solution.py:248
  18.4 1.1 %collective-permute-done.14.refs_16_ = bf16[776,128]{1,0:T(8,128)(2,1)S(1)} collective-permute-done((bf16[776,128]{1,0:T(8,128)(2,1)S(1)}, bf16[776,128]{1,0:T(8,128)(2,1)S(1)}, u32[]{:S(2)}, u32[]{:S(2)}) %collective-permute-start.14) | collective-permute-done | bytes 198688 | tf_op jit(solution)/shard_map/ppermute | solution.py:230
  19.6 0.9 collective-permute-start.10
  21.2 9.1 %collective-permute-done.refs_1_ = bf16[1544,128]{1,0:T(8,128)(2,1)S(1)} collective-permute-done((bf16[1544,128]{1,0:T(8,128)(2,1)S(1)}, bf16[1544,128]{1,0:T(8,128)(2,1)S(1)}, u32[]{:S(2)}, u32[]{:S(2)}) %collective-permute-start) | collective-permute-done | bytes 395296 | tf_op jit(solution)/shard_map/ppermute | solution.py:248
  30.3 1.0 %collective-permute-start.17 = (bf16[776,128]{1,0:T(8,128)(2,1)S(1)}, bf16[776,128]{1,0:T(8,128)(2,1)S(1)}, u32[]{:S(2)}, u32[]{:S(2)}) collective-permute-start(bf16[776,128]{1,0:T(8,128)(2,1)S(1)} %collective-permute-done.15.refs_17_), channel_id=1, source_target_pairs={{0,32},{4,36},{32,0},{36,4},{8,40},{12,44},{40,8},{44,12},{16,48},... | collective-permute-start | bytes 595976 | tf_op jit(solution)/shard_map/ppermute | solution.py:230
  31.3 4.1 %collective-permute-done.2.refs_3_ = bf16[1544,128]{1,0:T(8,128)(2,1)S(1)} collective-permute-done((bf16[1544,128]{1,0:T(8,128)(2,1)S(1)}, bf16[1544,128]{1,0:T(8,128)(2,1)S(1)}, u32[]{:S(2)}, u32[]{:S(2)}) %collective-permute-start.2) | collective-permute-done | bytes 395296 | tf_op jit(solution)/shard_map/ppermute | solution.py:248
  35.4 3.1 %collective-permute-start.16 = (bf16[776,128]{1,0:T(8,128)(2,1)S(1)}, bf16[776,128]{1,0:T(8,128)(2,1)S(1)}, u32[]{:S(2)}, u32[]{:S(2)}) collective-permute-start(bf16[776,128]{1,0:T(8,128)(2,1)S(1)} %collective-permute-done.14.refs_16_), channel_id=1, source_target_pairs={{0,56},{4,60},{32,8},{36,12},{8,32},{12,36},{40,16},{44,20},{16,40... | collective-permute-start | bytes 595976 | tf_op jit(solution)/shard_map/ppermute | solution.py:230
  38.6 2.7 %collective-permute-start.19 = (bf16[776,128]{1,0:T(8,128)(2,1)S(1)}, bf16[776,128]{1,0:T(8,128)(2,1)S(1)}, u32[]{:S(2)}, u32[]{:S(2)}) collective-permute-start(bf16[776,128]{1,0:T(8,128)(2,1)S(1)} %collective-permute-done.17.refs_19_), channel_id=1, source_target_pairs={{0,56},{4,60},{32,8},{36,12},{8,32},{12,36},{40,16},{44,20},{16,40... | collective-permute-start | bytes 595976 | tf_op jit(solution)/shard_map/ppermute | solution.py:230
  41.2 2.1 %collective-permute-done.16.refs_18_ = bf16[776,128]{1,0:T(8,128)(2,1)S(1)} collective-permute-done((bf16[776,128]{1,0:T(8,128)(2,1)S(1)}, bf16[776,128]{1,0:T(8,128)(2,1)S(1)}, u32[]{:S(2)}, u32[]{:S(2)}) %collective-permute-start.16) | collective-permute-done | bytes 198688 | tf_op jit(solution)/shard_map/ppermute | solution.py:230
  43.3 1.7 %collective-permute-start.4 = (bf16[1544,128]{1,0:T(8,128)(2,1)S(1)}, bf16[1544,128]{1,0:T(8,128)(2,1)S(1)}, u32[]{:S(2)}, u32[]{:S(2)}) collective-permute-start(bf16[1544,128]{1,0:T(8,128)(2,1)S(1)} %collective-permute-done.refs_1_), channel_id=1, source_target_pairs={{0,4},{4,0},{1,5},{5,1},{2,6},{6,2},{3,7},{7,3},{8,12},{12,8},{9,1... | collective-permute-start | bytes 1185800 | tf_op jit(solution)/shard_map/ppermute | solution.py:252
  45.0 2.6 %collective-permute-done.12.refs_14_ = bf16[776,128]{1,0:T(8,128)(2,1)S(1)} collective-permute-done((bf16[776,128]{1,0:T(8,128)(2,1)S(1)}, bf16[776,128]{1,0:T(8,128)(2,1)S(1)}, u32[]{:S(2)}, u32[]{:S(2)}) %collective-permute-start.12) | collective-permute-done | bytes 198688 | tf_op jit(solution)/shard_map/ppermute | solution.py:230
  47.6 1.7 %collective-permute-start.5 = (bf16[1544,128]{1,0:T(8,128)(2,1)S(1)}, bf16[1544,128]{1,0:T(8,128)(2,1)S(1)}, u32[]{:S(2)}, u32[]{:S(2)}) collective-permute-start(bf16[1544,128]{1,0:T(8,128)(2,1)S(1)} %collective-permute-done.1.refs_2_), channel_id=1, source_target_pairs={{0,4},{4,0},{1,5},{5,1},{2,6},{6,2},{3,7},{7,3},{8,12},{12,8},{9,1... | collective-permute-start | bytes 1185800 | tf_op jit(solution)/shard_map/ppermute | solution.py:252
  49.2 2.6 %collective-permute-done.19.refs_21_ = bf16[776,128]{1,0:T(8,128)(2,1)S(1)} collective-permute-done((bf16[776,128]{1,0:T(8,128)(2,1)S(1)}, bf16[776,128]{1,0:T(8,128)(2,1)S(1)}, u32[]{:S(2)}, u32[]{:S(2)}) %collective-permute-start.19) | collective-permute-done | bytes 198688 | tf_op jit(solution)/shard_map/ppermute | solution.py:230
  51.8 2.4 %collective-permute-start.20 = (bf16[776,128]{1,0:T(8,128)(2,1)S(1)}, bf16[776,128]{1,0:T(8,128)(2,1)S(1)}, u32[]{:S(2)}, u32[]{:S(2)}) collective-permute-start(bf16[776,128]{1,0:T(8,128)(2,1)S(1)} %collective-permute-done.11.refs_13_), channel_id=1, source_target_pairs={{0,56},{4,60},{32,8},{36,12},{8,32},{12,36},{40,16},{44,20},{16,40... | collective-permute-start | bytes 595976 | tf_op jit(solution)/shard_map/ppermute | solution.py:230
  54.4 4.0 %collective-permute-done.20.refs_8_ = bf16[776,128]{1,0:T(8,128)(2,1)S(1)} collective-permute-done((bf16[776,128]{1,0:T(8,128)(2,1)S(1)}, bf16[776,128]{1,0:T(8,128)(2,1)S(1)}, u32[]{:S(2)}, u32[]{:S(2)}) %collective-permute-start.20) | collective-permute-done | bytes 198688 | tf_op jit(solution)/shard_map/ppermute | solution.py:230
  59.1 3.4 %shard_map.31 = (bf16[8,4,3,2,32,128]{5,4,3,2,1,0:T(8,128)(2,1)S(1)}, bf16[16,768,128]{2,1,0:T(8,128)(2,1)S(1)}, f32[128,128]{1,0:T(8,128)S(1)}) custom-call(s32[24,128]{1,0:T(8,128)S(1)} %get-tuple-element.23.columns, bf16[1544,128]{1,0:T(8,128)(2,1)S(1)} %get-tuple-element.17.refs_0_, ...), custom_call_target="tpu_custom_call", output_to_operand_aliasing={{1}: (11, {}), {2}: (12, {})} | custom-call | tf_op jit(solution)/shard_map/pallas_call | solution.py:285
  62.5 32.1 %all_to_all.5 = bf16[32,3,2,32,128]{4,3,2,1,0:T(8,128)(2,1)S(1)} all-to-all(bf16[32,3,2,32,128]{4,3,2,1,0:T(8,128)(2,1)S(1)} %bitcast.4), channel_id=1, replica_groups=mesh['y'=4,'z_lo'=2,'z_hi'=4,'core'=2,'x'=4] {'y','core','x'}, dimensions={0} | all-to-all | bytes 3145728 | tf_op jit(solution)/shard_map/all_to_all | solution.py:294
  94.7 0.9 shard_map.32
  (28 shorter events, 2.2 us)
Async XLA Ops:
  0.0 10.2 %copy-start = (bf16[3,8,2,128,128]{4,3,2,1,0:T(8,128)(2,1)S(1)}, bf16[3,8,2,128,128]{4,3,2,1,0:T(8,128)(2,1)}, u32[]{:S(2)}) copy-start(bf16[3,8,2,128,128]{4,3,2,1,0:T(8,128)(2,1)} %tiles.3) | copy-start | bytes 4718596
  1.2 12.3 %collective-permute-start.8 = (bf16[776,128]{1,0:T(8,128)(2,1)S(1)}, bf16[776,128]{1,0:T(8,128)(2,1)S(1)}, u32[]{:S(2)}, u32[]{:S(2)}) collective-permute-start(bf16[776,128]{1,0:T(8,128)(2,1)S(1)} %get-tuple-element.21.refs_8_), channel_id=1, source_target_pairs={{0,56},{4,60},{32,8},{36,12},{8,32},{12,36},{40,16},{44,20},{16,40... | collective-permute-start | bytes 595976 | tf_op jit(solution)/shard_map/ppermute | solution.py:230
  7.7 6.6 %collective-permute-start.7 = (bf16[776,128]{1,0:T(8,128)(2,1)S(1)}, bf16[776,128]{1,0:T(8,128)(2,1)S(1)}, u32[]{:S(2)}, u32[]{:S(2)}) collective-permute-start(bf16[776,128]{1,0:T(8,128)(2,1)S(1)} %get-tuple-element.21.refs_8_), channel_id=1, source_target_pairs={{0,32},{4,36},{32,0},{36,4},{8,40},{12,44},{40,8},{44,12},{16,48},... | collective-permute-start | bytes 595976 | tf_op jit(solution)/shard_map/ppermute | solution.py:230
  7.7 9.6 %collective-permute-start.15 = (bf16[776,128]{1,0:T(8,128)(2,1)S(1)}, bf16[776,128]{1,0:T(8,128)(2,1)S(1)}, u32[]{:S(2)}, u32[]{:S(2)}) collective-permute-start(bf16[776,128]{1,0:T(8,128)(2,1)S(1)} %get-tuple-element.22), channel_id=1, source_target_pairs={{0,60},{4,56},{32,12},{36,8},{8,36},{12,32},{40,20},{44,16},{16,44... | collective-permute-start | bytes 595976 | tf_op jit(solution)/shard_map/ppermute | solution.py:230
  10.3 20.0 %collective-permute-start = (bf16[1544,128]{1,0:T(8,128)(2,1)S(1)}, bf16[1544,128]{1,0:T(8,128)(2,1)S(1)}, u32[]{:S(2)}, u32[]{:S(2)}) collective-permute-start(bf16[1544,128]{1,0:T(8,128)(2,1)S(1)} %get-tuple-element.18), channel_id=1, source_target_pairs={{0,192},{64,0},{128,64},{192,128},{1,193},{65,1},{129,65},{193,129... | collective-permute-start | bytes 1185800 | tf_op jit(solution)/shard_map/ppermute | solution.py:248
  13.1 6.4 %collective-permute-start.14 = (bf16[776,128]{1,0:T(8,128)(2,1)S(1)}, bf16[776,128]{1,0:T(8,128)(2,1)S(1)}, u32[]{:S(2)}, u32[]{:S(2)}) collective-permute-start(bf16[776,128]{1,0:T(8,128)(2,1)S(1)} %get-tuple-element.22), channel_id=1, source_target_pairs={{0,36},{4,32},{32,4},{36,0},{8,44},{12,40},{40,12},{44,8},{16,52},... | collective-permute-start | bytes 595976 | tf_op jit(solution)/shard_map/ppermute | solution.py:230
  13.4 7.0 %collective-permute-start.13 = (bf16[776,128]{1,0:T(8,128)(2,1)S(1)}, bf16[776,128]{1,0:T(8,128)(2,1)S(1)}, u32[]{:S(2)}, u32[]{:S(2)}) collective-permute-start(bf16[776,128]{1,0:T(8,128)(2,1)S(1)} %get-tuple-element.22), channel_id=1, source_target_pairs={{0,4},{4,0},{1,5},{5,1},{2,6},{6,2},{3,7},{7,3},{8,12},{12,8},{9,1... | collective-permute-start | bytes 595976 | tf_op jit(solution)/shard_map/ppermute | solution.py:249
  14.3 16.0 %collective-permute-start.1 = (bf16[1544,128]{1,0:T(8,128)(2,1)S(1)}, bf16[1544,128]{1,0:T(8,128)(2,1)S(1)}, u32[]{:S(2)}, u32[]{:S(2)}) collective-permute-start(bf16[1544,128]{1,0:T(8,128)(2,1)S(1)} %get-tuple-element.19), channel_id=1, source_target_pairs={{0,128},{64,192},{128,0},{192,64},{1,129},{65,193},{129,1},{193,65... | collective-permute-start | bytes 1185800 | tf_op jit(solution)/shard_map/ppermute | solution.py:248
  17.2 18.1 %collective-permute-start.2 = (bf16[1544,128]{1,0:T(8,128)(2,1)S(1)}, bf16[1544,128]{1,0:T(8,128)(2,1)S(1)}, u32[]{:S(2)}, u32[]{:S(2)}) collective-permute-start(bf16[1544,128]{1,0:T(8,128)(2,1)S(1)} %get-tuple-element.20), channel_id=1, source_target_pairs={{0,64},{64,128},{128,192},{192,0},{1,65},{65,129},{129,193},{193,1... | collective-permute-start | bytes 1185800 | tf_op jit(solution)/shard_map/ppermute | solution.py:248
  19.6 18.9 %collective-permute-start.10 = (bf16[776,128]{1,0:T(8,128)(2,1)S(1)}, bf16[776,128]{1,0:T(8,128)(2,1)S(1)}, u32[]{:S(2)}, u32[]{:S(2)}) collective-permute-start(bf16[776,128]{1,0:T(8,128)(2,1)S(1)} %collective-permute-done.8.refs_10_), channel_id=1, source_target_pairs={{0,32},{4,36},{32,0},{36,4},{8,40},{12,44},{40,8},{44,12},{16,48},... | collective-permute-start | bytes 595976 | tf_op jit(solution)/shard_map/ppermute | solution.py:230
  20.4 18.1 %collective-permute-start.9 = (bf16[776,128]{1,0:T(8,128)(2,1)S(1)}, bf16[776,128]{1,0:T(8,128)(2,1)S(1)}, u32[]{:S(2)}, u32[]{:S(2)}) collective-permute-start(bf16[776,128]{1,0:T(8,128)(2,1)S(1)} %collective-permute-done.7.refs_9_), channel_id=1, source_target_pairs={{0,56},{4,60},{32,8},{36,12},{8,32},{12,36},{40,16},{44,20},{16,40... | collective-permute-start | bytes 595976 | tf_op jit(solution)/shard_map/ppermute | solution.py:230
  30.3 13.0 %collective-permute-start.3 = (bf16[1544,128]{1,0:T(8,128)(2,1)S(1)}, bf16[1544,128]{1,0:T(8,128)(2,1)S(1)}, u32[]{:S(2)}, u32[]{:S(2)}) collective-permute-start(bf16[1544,128]{1,0:T(8,128)(2,1)S(1)} %get-tuple-element.17.refs_0_), channel_id=1, source_target_pairs={{0,4},{4,0},{1,5},{5,1},{2,6},{6,2},{3,7},{7,3},{8,12},{12,8},{9,1... | collective-permute-start | bytes 1185800 | tf_op jit(solution)/shard_map/ppermute | solution.py:250
  30.3 8.2 %collective-permute-start.17 = (bf16[776,128]{1,0:T(8,128)(2,1)S(1)}, bf16[776,128]{1,0:T(8,128)(2,1)S(1)}, u32[]{:S(2)}, u32[]{:S(2)}) collective-permute-start(bf16[776,128]{1,0:T(8,128)(2,1)S(1)} %collective-permute-done.15.refs_17_), channel_id=1, source_target_pairs={{0,32},{4,36},{32,0},{36,4},{8,40},{12,44},{40,8},{44,12},{16,48},... | collective-permute-start | bytes 595976 | tf_op jit(solution)/shard_map/ppermute | solution.py:230
  35.4 7.9 %collective-permute-start.16 = (bf16[776,128]{1,0:T(8,128)(2,1)S(1)}, bf16[776,128]{1,0:T(8,128)(2,1)S(1)}, u32[]{:S(2)}, u32[]{:S(2)}) collective-permute-start(bf16[776,128]{1,0:T(8,128)(2,1)S(1)} %collective-permute-done.14.refs_16_), channel_id=1, source_target_pairs={{0,56},{4,60},{32,8},{36,12},{8,32},{12,36},{40,16},{44,20},{16,40... | collective-permute-start | bytes 595976 | tf_op jit(solution)/shard_map/ppermute | solution.py:230
  38.4 9.1 %collective-permute-start.12 = (bf16[776,128]{1,0:T(8,128)(2,1)S(1)}, bf16[776,128]{1,0:T(8,128)(2,1)S(1)}, u32[]{:S(2)}, u32[]{:S(2)}) collective-permute-start(bf16[776,128]{1,0:T(8,128)(2,1)S(1)} %collective-permute-done.10.refs_12_), channel_id=1, source_target_pairs={{0,56},{4,60},{32,8},{36,12},{8,32},{12,36},{40,16},{44,20},{16,40... | collective-permute-start | bytes 595976 | tf_op jit(solution)/shard_map/ppermute | solution.py:230
  38.5 10.8 %collective-permute-start.11 = (bf16[776,128]{1,0:T(8,128)(2,1)S(1)}, bf16[776,128]{1,0:T(8,128)(2,1)S(1)}, u32[]{:S(2)}, u32[]{:S(2)}) collective-permute-start(bf16[776,128]{1,0:T(8,128)(2,1)S(1)} %collective-permute-done.9.refs_11_), channel_id=1, source_target_pairs={{0,32},{4,36},{32,0},{36,4},{8,40},{12,44},{40,8},{44,12},{16,48},... | collective-permute-start | bytes 595976 | tf_op jit(solution)/shard_map/ppermute | solution.py:230
  38.6 13.2 %collective-permute-start.19 = (bf16[776,128]{1,0:T(8,128)(2,1)S(1)}, bf16[776,128]{1,0:T(8,128)(2,1)S(1)}, u32[]{:S(2)}, u32[]{:S(2)}) collective-permute-start(bf16[776,128]{1,0:T(8,128)(2,1)S(1)} %collective-permute-done.17.refs_19_), channel_id=1, source_target_pairs={{0,56},{4,60},{32,8},{36,12},{8,32},{12,36},{40,16},{44,20},{16,40... | collective-permute-start | bytes 595976 | tf_op jit(solution)/shard_map/ppermute | solution.py:230
  43.3 10.9 %collective-permute-start.18 = (bf16[776,128]{1,0:T(8,128)(2,1)S(1)}, bf16[776,128]{1,0:T(8,128)(2,1)S(1)}, u32[]{:S(2)}, u32[]{:S(2)}) collective-permute-start(bf16[776,128]{1,0:T(8,128)(2,1)S(1)} %collective-permute-done.16.refs_18_), channel_id=1, source_target_pairs={{0,32},{4,36},{32,0},{36,4},{8,40},{12,44},{40,8},{44,12},{16,48},... | collective-permute-start | bytes 595976 | tf_op jit(solution)/shard_map/ppermute | solution.py:230
  43.3 10.9 %collective-permute-start.4 = (bf16[1544,128]{1,0:T(8,128)(2,1)S(1)}, bf16[1544,128]{1,0:T(8,128)(2,1)S(1)}, u32[]{:S(2)}, u32[]{:S(2)}) collective-permute-start(bf16[1544,128]{1,0:T(8,128)(2,1)S(1)} %collective-permute-done.refs_1_), channel_id=1, source_target_pairs={{0,4},{4,0},{1,5},{5,1},{2,6},{6,2},{3,7},{7,3},{8,12},{12,8},{9,1... | collective-permute-start | bytes 1185800 | tf_op jit(solution)/shard_map/ppermute | solution.py:252
  47.6 6.7 %collective-permute-start.5 = (bf16[1544,128]{1,0:T(8,128)(2,1)S(1)}, bf16[1544,128]{1,0:T(8,128)(2,1)S(1)}, u32[]{:S(2)}, u32[]{:S(2)}) collective-permute-start(bf16[1544,128]{1,0:T(8,128)(2,1)S(1)} %collective-permute-done.1.refs_2_), channel_id=1, source_target_pairs={{0,4},{4,0},{1,5},{5,1},{2,6},{6,2},{3,7},{7,3},{8,12},{12,8},{9,1... | collective-permute-start | bytes 1185800 | tf_op jit(solution)/shard_map/ppermute | solution.py:252
  49.2 5.0 %collective-permute-start.6 = (bf16[1544,128]{1,0:T(8,128)(2,1)S(1)}, bf16[1544,128]{1,0:T(8,128)(2,1)S(1)}, u32[]{:S(2)}, u32[]{:S(2)}) collective-permute-start(bf16[1544,128]{1,0:T(8,128)(2,1)S(1)} %collective-permute-done.2.refs_3_), channel_id=1, source_target_pairs={{0,4},{4,0},{1,5},{5,1},{2,6},{6,2},{3,7},{7,3},{8,12},{12,8},{9,1... | collective-permute-start | bytes 1185800 | tf_op jit(solution)/shard_map/ppermute | solution.py:252
  51.8 6.7 %collective-permute-start.20 = (bf16[776,128]{1,0:T(8,128)(2,1)S(1)}, bf16[776,128]{1,0:T(8,128)(2,1)S(1)}, u32[]{:S(2)}, u32[]{:S(2)}) collective-permute-start(bf16[776,128]{1,0:T(8,128)(2,1)S(1)} %collective-permute-done.11.refs_13_), channel_id=1, source_target_pairs={{0,56},{4,60},{32,8},{36,12},{8,32},{12,36},{40,16},{44,20},{16,40... | collective-permute-start | bytes 595976 | tf_op jit(solution)/shard_map/ppermute | solution.py:230
  54.2 4.9 %collective-permute-start.21 = (bf16[776,128]{1,0:T(8,128)(2,1)S(1)}, bf16[776,128]{1,0:T(8,128)(2,1)S(1)}, u32[]{:S(2)}, u32[]{:S(2)}) collective-permute-start(bf16[776,128]{1,0:T(8,128)(2,1)S(1)} %collective-permute-done.19.refs_21_), channel_id=1, source_target_pairs={{0,32},{4,36},{32,0},{36,4},{8,40},{12,44},{40,8},{44,12},{16,48},... | collective-permute-start | bytes 595976 | tf_op jit(solution)/shard_map/ppermute | solution.py:230

commit v8 on v7

--- a/solution.py
+++ b/solution.py
@@ -162,13 +162,17 @@
 
 
 def hold_early(rows, n_left, *refs):
-    left, right_in, (columns, right, right_columns) = refs[:n_left], refs[n_left:-3], refs[-3:]
+    left, right_in = refs[:n_left], refs[n_left:-5]
+    columns, right, right_columns, listed, arrived = refs[-5:]
     for n, ref in enumerate(left):
         tail = ref[pl.ds(ref.shape[0] - TAIL, TAIL), :].astype(jnp.float32).astype(jnp.int32)
-        columns[pl.ds(n * rows, rows), :] = tail[:rows]
+        listed[pl.ds(n * rows, rows), :] = tail[:rows]
+    fetch = pltpu.make_async_copy(listed, columns, arrived)
+    fetch.start()
     per_core = len(right_in) // 2
     for n, ref in enumerate(right_in):
         hold(right, right_columns, n + n // per_core, ref)
+    fetch.wait()
 
 
 def products(n_left, sizes, columns, *refs):
@@ -275,9 +279,10 @@
     ]
     columns, *kept = pl.pallas_call(
         functools.partial(hold_early, rows, len(lefts)),
-        out_shape=[jax.ShapeDtypeStruct((2 * n_y * rows, tb), jnp.int32)] + held_shapes,
+        out_shape=[pltpu.SMEM((2 * n_y * rows, tb), jnp.int32)] + held_shapes,
         in_specs=[vmem] * (len(lefts) + len(early)),
-        out_specs=[vmem] * 3,
+        out_specs=[pl.BlockSpec(memory_space=pltpu.SMEM)] + [vmem] * 2,
+        scratch_shapes=[pltpu.VMEM((2 * n_y * rows, tb), jnp.int32), pltpu.SemaphoreType.DMA],
         compiler_params=limit,
     )(*lefts, *early)
     kept = [pltpu.with_memory_space_constraint(k, pltpu.VMEM) for k in kept]

time: 95.7 us -> 95 us (level)
  transfers between devices with their start and end apart: 22 -> 22, of which waited for: 8 -> 8; matrix products, arithmetic and copies ran while one was open for 0% -> 0% of each run, Pallas kernels for 0% -> 1%
where the time goes in v8:
time: 95 us; the launch traced here: 94.9 us
  blocking collectives  32.1 us (34%)
  starting transfers between devices  31.3 us (33%)
  waiting for transfers between devices  25.7 us (27%)
  Pallas kernels  5.62 us (6%)
    all_to_all x1, blocking collectives, on_device(): lax.all_to_all(partial.reshape(2 * n_y * n_x, rows, slots, quarter, tb),...  32.1 us
    ppermute x14, starting transfers between devices, ring(): held[flip, chain] = lax.ppermute(held[flip, chain], ZC, perm)  20.2 us
    ppermute x3, waiting for transfers between devices, on_device(): left[0, -step % n_y] = lax.ppermute(sent[step], 'y', perm)  13.2 us
    ppermute x14, waiting for transfers between devices, ring(): held[flip, chain] = lax.ppermute(held[flip, chain], ZC, perm)  12.5 us
    ppermute x3, starting transfers between devices, on_device(): left[0, -step % n_y] = lax.ppermute(sent[step], 'y', perm)  6.93 us
    ppermute x3, starting transfers between devices, on_device(): left[1, step] = lax.ppermute(left[0, step], 'core', cores)  3.37 us
    pallas_call x1, Pallas kernels, on_device(): pl.pallas_call(functools.partial(products, len(lefts), sizes), out_shape=...  2.66 us
  transfers between devices with their start and end apart: 22, of which 8 were waited for; matrix products, arithmetic and copies ran while one was open for 0% of the time, Pallas kernels for 1%

profile of v8, /device:TPU:1, one launch (start us, length us, event | category | flops | bytes accessed | tf_op | source)
XLA Modules:
  0.0 94.9 jit_solution(14725220392500329645)
XLA Ops:
  0.0 1.2 %shard_map.28 = (bf16[776,128]{1,0:T(8,128)(2,1)S(1)}, bf16[776,128]{1,0:T(8,128)(2,1)S(1)}, bf16[8,128]{1,0:T(8,128)(2,1)S(1)}) custom-call(s32[3,2,8]{2,1,0:T(2,128)} %bitcast.5, bf16[3,8,2,128,128]{4,3,2,1,0:T(8,128)(2,1)} %tiles.3), custom_call_target="tpu_custom_call" | custom-call | tf_op jit(solution)/shard_map/pallas_call | solution.py:217
  1.2 6.5 %collective-permute-start.8 = (bf16[776,128]{1,0:T(8,128)(2,1)S(1)}, bf16[776,128]{1,0:T(8,128)(2,1)S(1)}, u32[]{:S(2)}, u32[]{:S(2)}) collective-permute-start(bf16[776,128]{1,0:T(8,128)(2,1)S(1)} %get-tuple-element.21.refs_8_), channel_id=1, source_target_pairs={{0,56},{4,60},{32,8},{36,12},{8,32},{12,36},{40,16},{44,20},{16,40... | collective-permute-start | bytes 595976 | tf_op jit(solution)/shard_map/ppermute | solution.py:234
  7.7 2.6 %collective-permute-start.15 = (bf16[776,128]{1,0:T(8,128)(2,1)S(1)}, bf16[776,128]{1,0:T(8,128)(2,1)S(1)}, u32[]{:S(2)}, u32[]{:S(2)}) collective-permute-start(bf16[776,128]{1,0:T(8,128)(2,1)S(1)} %get-tuple-element.22), channel_id=1, source_target_pairs={{0,60},{4,56},{32,12},{36,8},{8,36},{12,32},{40,20},{44,16},{16,44... | collective-permute-start | bytes 595976 | tf_op jit(solution)/shard_map/ppermute | solution.py:234
  10.3 2.8 %collective-permute-start = (bf16[1544,128]{1,0:T(8,128)(2,1)S(1)}, bf16[1544,128]{1,0:T(8,128)(2,1)S(1)}, u32[]{:S(2)}, u32[]{:S(2)}) collective-permute-start(bf16[1544,128]{1,0:T(8,128)(2,1)S(1)} %get-tuple-element.18), channel_id=1, source_target_pairs={{0,192},{64,0},{128,64},{192,128},{1,193},{65,1},{129,65},{193,129... | collective-permute-start | bytes 1185800 | tf_op jit(solution)/shard_map/ppermute | solution.py:252
  13.4 0.8 collective-permute-start.13
  14.3 2.9 %collective-permute-start.1 = (bf16[1544,128]{1,0:T(8,128)(2,1)S(1)}, bf16[1544,128]{1,0:T(8,128)(2,1)S(1)}, u32[]{:S(2)}, u32[]{:S(2)}) collective-permute-start(bf16[1544,128]{1,0:T(8,128)(2,1)S(1)} %get-tuple-element.19), channel_id=1, source_target_pairs={{0,128},{64,192},{128,0},{192,64},{1,129},{65,193},{129,1},{193,65... | collective-permute-start | bytes 1185800 | tf_op jit(solution)/shard_map/ppermute | solution.py:252
  17.2 1.2 %collective-permute-start.2 = (bf16[1544,128]{1,0:T(8,128)(2,1)S(1)}, bf16[1544,128]{1,0:T(8,128)(2,1)S(1)}, u32[]{:S(2)}, u32[]{:S(2)}) collective-permute-start(bf16[1544,128]{1,0:T(8,128)(2,1)S(1)} %get-tuple-element.20), channel_id=1, source_target_pairs={{0,64},{64,128},{128,192},{192,0},{1,65},{65,129},{129,193},{193,1... | collective-permute-start | bytes 1185800 | tf_op jit(solution)/shard_map/ppermute | solution.py:252
  18.4 1.1 %collective-permute-done.14.refs_16_ = bf16[776,128]{1,0:T(8,128)(2,1)S(1)} collective-permute-done((bf16[776,128]{1,0:T(8,128)(2,1)S(1)}, bf16[776,128]{1,0:T(8,128)(2,1)S(1)}, u32[]{:S(2)}, u32[]{:S(2)}) %collective-permute-start.14) | collective-permute-done | bytes 198688 | tf_op jit(solution)/shard_map/ppermute | solution.py:234
  19.6 0.9 collective-permute-start.10
  21.2 9.1 %collective-permute-done.refs_1_ = bf16[1544,128]{1,0:T(8,128)(2,1)S(1)} collective-permute-done((bf16[1544,128]{1,0:T(8,128)(2,1)S(1)}, bf16[1544,128]{1,0:T(8,128)(2,1)S(1)}, u32[]{:S(2)}, u32[]{:S(2)}) %collective-permute-start) | collective-permute-done | bytes 395296 | tf_op jit(solution)/shard_map/ppermute | solution.py:252
  30.3 1.0 %collective-permute-start.17 = (bf16[776,128]{1,0:T(8,128)(2,1)S(1)}, bf16[776,128]{1,0:T(8,128)(2,1)S(1)}, u32[]{:S(2)}, u32[]{:S(2)}) collective-permute-start(bf16[776,128]{1,0:T(8,128)(2,1)S(1)} %collective-permute-done.15.refs_17_), channel_id=1, source_target_pairs={{0,32},{4,36},{32,0},{36,4},{8,40},{12,44},{40,8},{44,12},{16,48},... | collective-permute-start | bytes 595976 | tf_op jit(solution)/shard_map/ppermute | solution.py:234
  31.3 4.1 %collective-permute-done.2.refs_3_ = bf16[1544,128]{1,0:T(8,128)(2,1)S(1)} collective-permute-done((bf16[1544,128]{1,0:T(8,128)(2,1)S(1)}, bf16[1544,128]{1,0:T(8,128)(2,1)S(1)}, u32[]{:S(2)}, u32[]{:S(2)}) %collective-permute-start.2) | collective-permute-done | bytes 395296 | tf_op jit(solution)/shard_map/ppermute | solution.py:252
  35.4 3.1 %collective-permute-start.16 = (bf16[776,128]{1,0:T(8,128)(2,1)S(1)}, bf16[776,128]{1,0:T(8,128)(2,1)S(1)}, u32[]{:S(2)}, u32[]{:S(2)}) collective-permute-start(bf16[776,128]{1,0:T(8,128)(2,1)S(1)} %collective-permute-done.14.refs_16_), channel_id=1, source_target_pairs={{0,56},{4,60},{32,8},{36,12},{8,32},{12,36},{40,16},{44,20},{16,40... | collective-permute-start | bytes 595976 | tf_op jit(solution)/shard_map/ppermute | solution.py:234
  38.6 2.7 %collective-permute-start.19 = (bf16[776,128]{1,0:T(8,128)(2,1)S(1)}, bf16[776,128]{1,0:T(8,128)(2,1)S(1)}, u32[]{:S(2)}, u32[]{:S(2)}) collective-permute-start(bf16[776,128]{1,0:T(8,128)(2,1)S(1)} %collective-permute-done.17.refs_19_), channel_id=1, source_target_pairs={{0,56},{4,60},{32,8},{36,12},{8,32},{12,36},{40,16},{44,20},{16,40... | collective-permute-start | bytes 595976 | tf_op jit(solution)/shard_map/ppermute | solution.py:234
  41.2 2.1 %collective-permute-done.16.refs_18_ = bf16[776,128]{1,0:T(8,128)(2,1)S(1)} collective-permute-done((bf16[776,128]{1,0:T(8,128)(2,1)S(1)}, bf16[776,128]{1,0:T(8,128)(2,1)S(1)}, u32[]{:S(2)}, u32[]{:S(2)}) %collective-permute-start.16) | collective-permute-done | bytes 198688 | tf_op jit(solution)/shard_map/ppermute | solution.py:234
  43.3 1.7 %collective-permute-start.4 = (bf16[1544,128]{1,0:T(8,128)(2,1)S(1)}, bf16[1544,128]{1,0:T(8,128)(2,1)S(1)}, u32[]{:S(2)}, u32[]{:S(2)}) collective-permute-start(bf16[1544,128]{1,0:T(8,128)(2,1)S(1)} %collective-permute-done.refs_1_), channel_id=1, source_target_pairs={{0,4},{4,0},{1,5},{5,1},{2,6},{6,2},{3,7},{7,3},{8,12},{12,8},{9,1... | collective-permute-start | bytes 1185800 | tf_op jit(solution)/shard_map/ppermute | solution.py:256
  45.0 2.6 %collective-permute-done.12.refs_14_ = bf16[776,128]{1,0:T(8,128)(2,1)S(1)} collective-permute-done((bf16[776,128]{1,0:T(8,128)(2,1)S(1)}, bf16[776,128]{1,0:T(8,128)(2,1)S(1)}, u32[]{:S(2)}, u32[]{:S(2)}) %collective-permute-start.12) | collective-permute-done | bytes 198688 | tf_op jit(solution)/shard_map/ppermute | solution.py:234
  47.6 1.7 %collective-permute-start.5 = (bf16[1544,128]{1,0:T(8,128)(2,1)S(1)}, bf16[1544,128]{1,0:T(8,128)(2,1)S(1)}, u32[]{:S(2)}, u32[]{:S(2)}) collective-permute-start(bf16[1544,128]{1,0:T(8,128)(2,1)S(1)} %collective-permute-done.1.refs_2_), channel_id=1, source_target_pairs={{0,4},{4,0},{1,5},{5,1},{2,6},{6,2},{3,7},{7,3},{8,12},{12,8},{9,1... | collective-permute-start | bytes 1185800 | tf_op jit(solution)/shard_map/ppermute | solution.py:256
  49.2 2.6 %collective-permute-done.19.refs_21_ = bf16[776,128]{1,0:T(8,128)(2,1)S(1)} collective-permute-done((bf16[776,128]{1,0:T(8,128)(2,1)S(1)}, bf16[776,128]{1,0:T(8,128)(2,1)S(1)}, u32[]{:S(2)}, u32[]{:S(2)}) %collective-permute-start.19) | collective-permute-done | bytes 198688 | tf_op jit(solution)/shard_map/ppermute | solution.py:234
  51.8 2.4 %collective-permute-start.20 = (bf16[776,128]{1,0:T(8,128)(2,1)S(1)}, bf16[776,128]{1,0:T(8,128)(2,1)S(1)}, u32[]{:S(2)}, u32[]{:S(2)}) collective-permute-start(bf16[776,128]{1,0:T(8,128)(2,1)S(1)} %collective-permute-done.11.refs_13_), channel_id=1, source_target_pairs={{0,56},{4,60},{32,8},{36,12},{8,32},{12,36},{40,16},{44,20},{16,40... | collective-permute-start | bytes 595976 | tf_op jit(solution)/shard_map/ppermute | solution.py:234
  55.0 3.5 %collective-permute-done.20.refs_8_ = bf16[776,128]{1,0:T(8,128)(2,1)S(1)} collective-permute-done((bf16[776,128]{1,0:T(8,128)(2,1)S(1)}, bf16[776,128]{1,0:T(8,128)(2,1)S(1)}, u32[]{:S(2)}, u32[]{:S(2)}) %collective-permute-start.20) | collective-permute-done | bytes 198688 | tf_op jit(solution)/shard_map/ppermute | solution.py:234
  59.1 2.7 %shard_map.31 = (bf16[8,4,3,2,32,128]{5,4,3,2,1,0:T(8,128)(2,1)S(1)}, bf16[16,768,128]{2,1,0:T(8,128)(2,1)S(1)}, f32[128,128]{1,0:T(8,128)S(1)}) custom-call(s32[24,128]{1,0:T(8,128)S(4)} %get-tuple-element.23.columns, bf16[1544,128]{1,0:T(8,128)(2,1)S(1)} %get-tuple-element.17.refs_0_, ...), custom_call_target="tpu_custom_call", output_to_operand_aliasing={{1}: (11, {}), {2}: (12, {})} | custom-call | tf_op jit(solution)/shard_map/pallas_call | solution.py:290
  61.8 32.1 %all_to_all.5 = bf16[32,3,2,32,128]{4,3,2,1,0:T(8,128)(2,1)S(1)} all-to-all(bf16[32,3,2,32,128]{4,3,2,1,0:T(8,128)(2,1)S(1)} %bitcast.4), channel_id=1, replica_groups=mesh['y'=4,'z_lo'=2,'z_hi'=4,'core'=2,'x'=4] {'y','core','x'}, dimensions={0} | all-to-all | bytes 3145728 | tf_op jit(solution)/shard_map/all_to_all | solution.py:299
  93.9 0.9 shard_map.32
  (28 shorter events, 2.7 us)
Async XLA Ops:
  0.0 10.2 %copy-start = (bf16[3,8,2,128,128]{4,3,2,1,0:T(8,128)(2,1)S(1)}, bf16[3,8,2,128,128]{4,3,2,1,0:T(8,128)(2,1)}, u32[]{:S(2)}) copy-start(bf16[3,8,2,128,128]{4,3,2,1,0:T(8,128)(2,1)} %tiles.3) | copy-start | bytes 4718596
  1.2 12.3 %collective-permute-start.8 = (bf16[776,128]{1,0:T(8,128)(2,1)S(1)}, bf16[776,128]{1,0:T(8,128)(2,1)S(1)}, u32[]{:S(2)}, u32[]{:S(2)}) collective-permute-start(bf16[776,128]{1,0:T(8,128)(2,1)S(1)} %get-tuple-element.21.refs_8_), channel_id=1, source_target_pairs={{0,56},{4,60},{32,8},{36,12},{8,32},{12,36},{40,16},{44,20},{16,40... | collective-permute-start | bytes 595976 | tf_op jit(solution)/shard_map/ppermute | solution.py:234
  7.7 6.6 %collective-permute-start.7 = (bf16[776,128]{1,0:T(8,128)(2,1)S(1)}, bf16[776,128]{1,0:T(8,128)(2,1)S(1)}, u32[]{:S(2)}, u32[]{:S(2)}) collective-permute-start(bf16[776,128]{1,0:T(8,128)(2,1)S(1)} %get-tuple-element.21.refs_8_), channel_id=1, source_target_pairs={{0,32},{4,36},{32,0},{36,4},{8,40},{12,44},{40,8},{44,12},{16,48},... | collective-permute-start | bytes 595976 | tf_op jit(solution)/shard_map/ppermute | solution.py:234
  7.7 9.6 %collective-permute-start.15 = (bf16[776,128]{1,0:T(8,128)(2,1)S(1)}, bf16[776,128]{1,0:T(8,128)(2,1)S(1)}, u32[]{:S(2)}, u32[]{:S(2)}) collective-permute-start(bf16[776,128]{1,0:T(8,128)(2,1)S(1)} %get-tuple-element.22), channel_id=1, source_target_pairs={{0,60},{4,56},{32,12},{36,8},{8,36},{12,32},{40,20},{44,16},{16,44... | collective-permute-start | bytes 595976 | tf_op jit(solution)/shard_map/ppermute | solution.py:234
  10.3 20.0 %collective-permute-start = (bf16[1544,128]{1,0:T(8,128)(2,1)S(1)}, bf16[1544,128]{1,0:T(8,128)(2,1)S(1)}, u32[]{:S(2)}, u32[]{:S(2)}) collective-permute-start(bf16[1544,128]{1,0:T(8,128)(2,1)S(1)} %get-tuple-element.18), channel_id=1, source_target_pairs={{0,192},{64,0},{128,64},{192,128},{1,193},{65,1},{129,65},{193,129... | collective-permute-start | bytes 1185800 | tf_op jit(solution)/shard_map/ppermute | solution.py:252
  13.1 6.4 %collective-permute-start.14 = (bf16[776,128]{1,0:T(8,128)(2,1)S(1)}, bf16[776,128]{1,0:T(8,128)(2,1)S(1)}, u32[]{:S(2)}, u32[]{:S(2)}) collective-permute-start(bf16[776,128]{1,0:T(8,128)(2,1)S(1)} %get-tuple-element.22), channel_id=1, source_target_pairs={{0,36},{4,32},{32,4},{36,0},{8,44},{12,40},{40,12},{44,8},{16,52},... | collective-permute-start | bytes 595976 | tf_op jit(solution)/shard_map/ppermute | solution.py:234
  13.4 7.0 %collective-permute-start.13 = (bf16[776,128]{1,0:T(8,128)(2,1)S(1)}, bf16[776,128]{1,0:T(8,128)(2,1)S(1)}, u32[]{:S(2)}, u32[]{:S(2)}) collective-permute-start(bf16[776,128]{1,0:T(8,128)(2,1)S(1)} %get-tuple-element.22), channel_id=1, source_target_pairs={{0,4},{4,0},{1,5},{5,1},{2,6},{6,2},{3,7},{7,3},{8,12},{12,8},{9,1... | collective-permute-start | bytes 595976 | tf_op jit(solution)/shard_map/ppermute | solution.py:253
  14.3 16.0 %collective-permute-start.1 = (bf16[1544,128]{1,0:T(8,128)(2,1)S(1)}, bf16[1544,128]{1,0:T(8,128)(2,1)S(1)}, u32[]{:S(2)}, u32[]{:S(2)}) collective-permute-start(bf16[1544,128]{1,0:T(8,128)(2,1)S(1)} %get-tuple-element.19), channel_id=1, source_target_pairs={{0,128},{64,192},{128,0},{192,64},{1,129},{65,193},{129,1},{193,65... | collective-permute-start | bytes 1185800 | tf_op jit(solution)/shard_map/ppermute | solution.py:252
  17.2 18.1 %collective-permute-start.2 = (bf16[1544,128]{1,0:T(8,128)(2,1)S(1)}, bf16[1544,128]{1,0:T(8,128)(2,1)S(1)}, u32[]{:S(2)}, u32[]{:S(2)}) collective-permute-start(bf16[1544,128]{1,0:T(8,128)(2,1)S(1)} %get-tuple-element.20), channel_id=1, source_target_pairs={{0,64},{64,128},{128,192},{192,0},{1,65},{65,129},{129,193},{193,1... | collective-permute-start | bytes 1185800 | tf_op jit(solution)/shard_map/ppermute | solution.py:252
  19.6 18.9 %collective-permute-start.10 = (bf16[776,128]{1,0:T(8,128)(2,1)S(1)}, bf16[776,128]{1,0:T(8,128)(2,1)S(1)}, u32[]{:S(2)}, u32[]{:S(2)}) collective-permute-start(bf16[776,128]{1,0:T(8,128)(2,1)S(1)} %collective-permute-done.8.refs_10_), channel_id=1, source_target_pairs={{0,32},{4,36},{32,0},{36,4},{8,40},{12,44},{40,8},{44,12},{16,48},... | collective-permute-start | bytes 595976 | tf_op jit(solution)/shard_map/ppermute | solution.py:234
  20.4 18.1 %collective-permute-start.9 = (bf16[776,128]{1,0:T(8,128)(2,1)S(1)}, bf16[776,128]{1,0:T(8,128)(2,1)S(1)}, u32[]{:S(2)}, u32[]{:S(2)}) collective-permute-start(bf16[776,128]{1,0:T(8,128)(2,1)S(1)} %collective-permute-done.7.refs_9_), channel_id=1, source_target_pairs={{0,56},{4,60},{32,8},{36,12},{8,32},{12,36},{40,16},{44,20},{16,40... | collective-permute-start | bytes 595976 | tf_op jit(solution)/shard_map/ppermute | solution.py:234
  30.3 13.0 %collective-permute-start.3 = (bf16[1544,128]{1,0:T(8,128)(2,1)S(1)}, bf16[1544,128]{1,0:T(8,128)(2,1)S(1)}, u32[]{:S(2)}, u32[]{:S(2)}) collective-permute-start(bf16[1544,128]{1,0:T(8,128)(2,1)S(1)} %get-tuple-element.17.refs_0_), channel_id=1, source_target_pairs={{0,4},{4,0},{1,5},{5,1},{2,6},{6,2},{3,7},{7,3},{8,12},{12,8},{9,1... | collective-permute-start | bytes 1185800 | tf_op jit(solution)/shard_map/ppermute | solution.py:254
  30.3 8.2 %collective-permute-start.17 = (bf16[776,128]{1,0:T(8,128)(2,1)S(1)}, bf16[776,128]{1,0:T(8,128)(2,1)S(1)}, u32[]{:S(2)}, u32[]{:S(2)}) collective-permute-start(bf16[776,128]{1,0:T(8,128)(2,1)S(1)} %collective-permute-done.15.refs_17_), channel_id=1, source_target_pairs={{0,32},{4,36},{32,0},{36,4},{8,40},{12,44},{40,8},{44,12},{16,48},... | collective-permute-start | bytes 595976 | tf_op jit(solution)/shard_map/ppermute | solution.py:234
  35.4 7.9 %collective-permute-start.16 = (bf16[776,128]{1,0:T(8,128)(2,1)S(1)}, bf16[776,128]{1,0:T(8,128)(2,1)S(1)}, u32[]{:S(2)}, u32[]{:S(2)}) collective-permute-start(bf16[776,128]{1,0:T(8,128)(2,1)S(1)} %collective-permute-done.14.refs_16_), channel_id=1, source_target_pairs={{0,56},{4,60},{32,8},{36,12},{8,32},{12,36},{40,16},{44,20},{16,40... | collective-permute-start | bytes 595976 | tf_op jit(solution)/shard_map/ppermute | solution.py:234
  38.4 9.1 %collective-permute-start.12 = (bf16[776,128]{1,0:T(8,128)(2,1)S(1)}, bf16[776,128]{1,0:T(8,128)(2,1)S(1)}, u32[]{:S(2)}, u32[]{:S(2)}) collective-permute-start(bf16[776,128]{1,0:T(8,128)(2,1)S(1)} %collective-permute-done.10.refs_12_), channel_id=1, source_target_pairs={{0,56},{4,60},{32,8},{36,12},{8,32},{12,36},{40,16},{44,20},{16,40... | collective-permute-start | bytes 595976 | tf_op jit(solution)/shard_map/ppermute | solution.py:234
  38.5 10.8 %collective-permute-start.11 = (bf16[776,128]{1,0:T(8,128)(2,1)S(1)}, bf16[776,128]{1,0:T(8,128)(2,1)S(1)}, u32[]{:S(2)}, u32[]{:S(2)}) collective-permute-start(bf16[776,128]{1,0:T(8,128)(2,1)S(1)} %collective-permute-done.9.refs_11_), channel_id=1, source_target_pairs={{0,32},{4,36},{32,0},{36,4},{8,40},{12,44},{40,8},{44,12},{16,48},... | collective-permute-start | bytes 595976 | tf_op jit(solution)/shard_map/ppermute | solution.py:234
  38.6 13.2 %collective-permute-start.19 = (bf16[776,128]{1,0:T(8,128)(2,1)S(1)}, bf16[776,128]{1,0:T(8,128)(2,1)S(1)}, u32[]{:S(2)}, u32[]{:S(2)}) collective-permute-start(bf16[776,128]{1,0:T(8,128)(2,1)S(1)} %collective-permute-done.17.refs_19_), channel_id=1, source_target_pairs={{0,56},{4,60},{32,8},{36,12},{8,32},{12,36},{40,16},{44,20},{16,40... | collective-permute-start | bytes 595976 | tf_op jit(solution)/shard_map/ppermute | solution.py:234
  43.3 10.9 %collective-permute-start.18 = (bf16[776,128]{1,0:T(8,128)(2,1)S(1)}, bf16[776,128]{1,0:T(8,128)(2,1)S(1)}, u32[]{:S(2)}, u32[]{:S(2)}) collective-permute-start(bf16[776,128]{1,0:T(8,128)(2,1)S(1)} %collective-permute-done.16.refs_18_), channel_id=1, source_target_pairs={{0,32},{4,36},{32,0},{36,4},{8,40},{12,44},{40,8},{44,12},{16,48},... | collective-permute-start | bytes 595976 | tf_op jit(solution)/shard_map/ppermute | solution.py:234
  43.3 10.9 %collective-permute-start.4 = (bf16[1544,128]{1,0:T(8,128)(2,1)S(1)}, bf16[1544,128]{1,0:T(8,128)(2,1)S(1)}, u32[]{:S(2)}, u32[]{:S(2)}) collective-permute-start(bf16[1544,128]{1,0:T(8,128)(2,1)S(1)} %collective-permute-done.refs_1_), channel_id=1, source_target_pairs={{0,4},{4,0},{1,5},{5,1},{2,6},{6,2},{3,7},{7,3},{8,12},{12,8},{9,1... | collective-permute-start | bytes 1185800 | tf_op jit(solution)/shard_map/ppermute | solution.py:256
  47.6 6.7 %collective-permute-start.5 = (bf16[1544,128]{1,0:T(8,128)(2,1)S(1)}, bf16[1544,128]{1,0:T(8,128)(2,1)S(1)}, u32[]{:S(2)}, u32[]{:S(2)}) collective-permute-start(bf16[1544,128]{1,0:T(8,128)(2,1)S(1)} %collective-permute-done.1.refs_2_), channel_id=1, source_target_pairs={{0,4},{4,0},{1,5},{5,1},{2,6},{6,2},{3,7},{7,3},{8,12},{12,8},{9,1... | collective-permute-start | bytes 1185800 | tf_op jit(solution)/shard_map/ppermute | solution.py:256
  49.2 5.0 %collective-permute-start.6 = (bf16[1544,128]{1,0:T(8,128)(2,1)S(1)}, bf16[1544,128]{1,0:T(8,128)(2,1)S(1)}, u32[]{:S(2)}, u32[]{:S(2)}) collective-permute-start(bf16[1544,128]{1,0:T(8,128)(2,1)S(1)} %collective-permute-done.2.refs_3_), channel_id=1, source_target_pairs={{0,4},{4,0},{1,5},{5,1},{2,6},{6,2},{3,7},{7,3},{8,12},{12,8},{9,1... | collective-permute-start | bytes 1185800 | tf_op jit(solution)/shard_map/ppermute | solution.py:256
  51.8 6.7 %collective-permute-start.20 = (bf16[776,128]{1,0:T(8,128)(2,1)S(1)}, bf16[776,128]{1,0:T(8,128)(2,1)S(1)}, u32[]{:S(2)}, u32[]{:S(2)}) collective-permute-start(bf16[776,128]{1,0:T(8,128)(2,1)S(1)} %collective-permute-done.11.refs_13_), channel_id=1, source_target_pairs={{0,56},{4,60},{32,8},{36,12},{8,32},{12,36},{40,16},{44,20},{16,40... | collective-permute-start | bytes 595976 | tf_op jit(solution)/shard_map/ppermute | solution.py:234
  54.2 4.9 %collective-permute-start.21 = (bf16[776,128]{1,0:T(8,128)(2,1)S(1)}, bf16[776,128]{1,0:T(8,128)(2,1)S(1)}, u32[]{:S(2)}, u32[]{:S(2)}) collective-permute-start(bf16[776,128]{1,0:T(8,128)(2,1)S(1)} %collective-permute-done.19.refs_21_), channel_id=1, source_target_pairs={{0,32},{4,36},{32,0},{36,4},{8,40},{12,44},{40,8},{44,12},{16,48},... | collective-permute-start | bytes 595976 | tf_op jit(solution)/shard_map/ppermute | solution.py:234
